TPU v7x, 32 devices: a whole 2x2x4 slice. The times are simulated.
32 devices in a mesh: seq: 8 (over y, x, core), chan: 4 (over z).
Axes of the slice: x: 2, y: 2, z: 4, core: 2. Of those that a mesh axis runs over, the one named last changes fastest.
Arguments:
- stream: float32 [6144, 4096], P('seq', 'chan'), may hold values from -6 to 6
- short_gate_pre: float32 [6144, 4096], P('seq', 'chan'), may hold values from -6 to 6
- short_gate_post: float32 [6144, 4096], P('seq', 'chan'), may hold values from -6 to 6
- short_filter: float32 [128, 4096], P(None, 'chan'), may hold values from -0.5 to 0.5
- long_gate_pre: float32 [6144, 4096], P('seq', 'chan'), may hold values from -6 to 6
- long_gate_post: float32 [6144, 4096], P('seq', 'chan'), may hold values from -6 to 6
- long_filter: float32 [4096, 6144], P('chan', 'seq'), may hold values from -0.078125 to 0.078125
- queries: float32 [6144, 4096], P('seq', 'chan'), may hold values from -8 to 8
- key_vectors: float32 [6144, 4096], P('seq', 'chan'), may hold values from -8 to 8
- head_reach: int32 [32], P('chan'), may hold values from 1 to 3
- out_weight: float32 [4096, 4096], P('seq', 'chan'), may hold values from -0.09375 to 0.09375
Outputs:
- hyena_out: float32 [6144, 4096], P('seq', 'chan')
- mixed: float32 [6144, 4096], P('seq', 'chan')
Inputs may be any that keep to these rules, and one draw needn't show every extreme that they name: Head h reads its own block and the head_reach[h] blocks of 768 tokens before it.
All inputs are finite; a program needn't handle non-finite values.
Results may differ from a plain program's by a relative error of at most 0.0003.
Values sent between devices are 32-bit elements; how exact they have to be, the bound alone decides.
No kernel may reach another device: no remote copies, remote signals or barrier semaphores. Data moves between devices by JAX's collectives and lax.ppermute only.
A program may use at most 256 MiB of HBM per device.

v0:
```python
import math

import jax
import jax.numpy as jnp
from jax import lax
from jax.sharding import PartitionSpec as P

HEAD_DIM = 128
TAPS = 128
REACH = 3


highest_mode = lax.Precision.HIGHEST
masked_low = -1e30


def from_behind(shard, axis, by):
    size = lax.axis_size(axis)
    pairs = [(i, i + by) for i in range(size) if 0 <= i + by < size]
    return lax.ppermute(shard, axis, pairs)


def short_convolve(extended, taps):
    kernel = taps[::-1][:, None, :]
    result = lax.conv_general_dilated(
        extended[None],
        kernel,
        (1,),
        "VALID",
        dimension_numbers=("NWC", "WIO", "NWC"),
        feature_group_count=taps.shape[1],
        precision=highest_mode,
    )
    return result[0]


def angle_table(row_count, col_count, modulus):
    product = (
        lax.iota(jnp.int32, row_count)[:, None] * lax.iota(jnp.int32, col_count)[None, :] % modulus
    )
    phase = product.astype(jnp.float32) * (2.0 * math.pi / modulus)
    return (jnp.cos(phase), jnp.sin(phase))


def long_convolve(signal, kernel):
    channels, length = signal.shape
    inner_len = 128
    outer_len = 2 * length // inner_len
    half_len = outer_len // 2
    cos_outer, sin_outer = angle_table(outer_len, half_len, outer_len)
    cos_twist, sin_twist = angle_table(outer_len, inner_len, 2 * length)
    cos_inner, sin_inner = angle_table(inner_len, inner_len, inner_len)
    stacked = jnp.concatenate([signal, kernel], axis=0).reshape(2 * channels, half_len, inner_len)
    real_part = jnp.einsum("kn,cnq->ckq", cos_outer, stacked, precision=highest_mode)
    imag_part = -jnp.einsum("kn,cnq->ckq", sin_outer, stacked, precision=highest_mode)
    twist_real = real_part * cos_twist + imag_part * sin_twist
    twist_imag = imag_part * cos_twist - real_part * sin_twist
    spec_real = jnp.dot(twist_real, cos_inner, precision=highest_mode) + jnp.dot(
        twist_imag, sin_inner, precision=highest_mode
    )
    spec_imag = jnp.dot(twist_imag, cos_inner, precision=highest_mode) - jnp.dot(
        twist_real, sin_inner, precision=highest_mode
    )
    sig_real, ker_real = (spec_real[:channels], spec_real[channels:])
    sig_imag, ker_imag = (spec_imag[:channels], spec_imag[channels:])
    prod_real = sig_real * ker_real - sig_imag * ker_imag
    prod_imag = sig_real * ker_imag + sig_imag * ker_real
    back_real = jnp.dot(prod_real, cos_inner, precision=highest_mode) - jnp.dot(
        prod_imag, sin_inner, precision=highest_mode
    )
    back_imag = jnp.dot(prod_imag, cos_inner, precision=highest_mode) + jnp.dot(
        prod_real, sin_inner, precision=highest_mode
    )
    turn_real = back_real * cos_twist - back_imag * sin_twist
    turn_imag = back_real * sin_twist + back_imag * cos_twist
    result = jnp.einsum("kn,ckq->cnq", cos_outer, turn_real, precision=highest_mode) - jnp.einsum(
        "kn,ckq->cnq", sin_outer, turn_imag, precision=highest_mode
    )
    return result.reshape(channels, length) / (2.0 * length)


def shards(
    stream,
    short_gate_pre,
    short_gate_post,
    short_filter,
    long_gate_pre,
    long_gate_post,
    long_filter,
    queries,
    key_vectors,
    head_reach,
    out_weight,
):
    length, width = stream.shape
    short_in = short_gate_pre * stream
    rim_rows = from_behind(short_in[length - (TAPS - 1) :], "seq", 1)
    short_conv = short_convolve(jnp.concatenate([rim_rows, short_in], axis=0), short_filter)
    short_out = stream + short_gate_post * short_conv
    seq_parts = lax.axis_size("seq")
    long_in = (long_gate_pre * short_out).T.reshape(seq_parts, width // seq_parts, length)
    filter_cols = long_filter.reshape(seq_parts, width // seq_parts, length)
    signal_part = lax.all_to_all(long_in, "seq", split_axis=0, concat_axis=2, tiled=True)
    kernel_part = lax.all_to_all(filter_cols, "seq", split_axis=0, concat_axis=2, tiled=True)
    convolved = long_convolve(signal_part[0], kernel_part[0])
    long_cols = lax.all_to_all(convolved[None], "seq", split_axis=2, concat_axis=0, tiled=True)
    long_conv = long_cols.reshape(width, length).T
    hyena_out = short_out + long_gate_post * long_conv
    heads_here = width // HEAD_DIM
    scale = 1.0 / math.sqrt(HEAD_DIM)
    query_heads = queries.reshape(length, heads_here, HEAD_DIM)
    position = lax.axis_index("seq")
    row_pos = lax.iota(jnp.int32, length)[:, None]
    col_pos = lax.iota(jnp.int32, length)[None, :]

    def absorb_block(state, keys_here, values_here, distance):
        running_max, running_sum, weighted = state
        key_heads = keys_here.reshape(length, heads_here, HEAD_DIM)
        value_heads = values_here.reshape(length, heads_here, HEAD_DIM)
        scores = jnp.einsum("qhd,khd->hqk", query_heads, key_heads, precision=highest_mode) * scale
        allowed = (head_reach >= distance)[:, None, None] & (position >= distance)
        if distance == 0:
            allowed = allowed & (row_pos >= col_pos)[None]
        masked = jnp.where(allowed, scores, masked_low)
        new_max = jnp.maximum(running_max, jnp.max(masked, axis=2))
        weight = jnp.where(allowed, jnp.exp(masked - new_max[..., None]), 0.0)
        shrink = jnp.exp(running_max - new_max)
        running_sum = running_sum * shrink + jnp.sum(weight, axis=2)
        weighted = weighted * shrink[..., None] + jnp.einsum(
            "hqk,khd->hqd", weight, value_heads, precision=highest_mode
        )
        return (new_max, running_sum, weighted)

    state = (
        jnp.full((heads_here, length), masked_low, jnp.float32),
        jnp.zeros((heads_here, length), jnp.float32),
        jnp.zeros((heads_here, length, HEAD_DIM), jnp.float32),
    )
    state = absorb_block(state, key_vectors, hyena_out, 0)
    carried = (key_vectors, hyena_out)
    for distance in range(1, REACH + 1):
        carried = from_behind((carried[0], carried[1]), "seq", 1)
        state = absorb_block(state, carried[0], carried[1], distance)
    attended = (state[2] / state[1][..., None]).transpose(1, 0, 2).reshape(length, width)
    all_heads = lax.all_gather(attended, "chan", axis=1, tiled=True)
    mixed = jnp.dot(
        all_heads,
        lax.all_gather(out_weight, "seq", axis=0, tiled=True),
        precision=highest_mode,
        preferred_element_type=jnp.float32,
    )
    return (hyena_out, mixed)


def solution(mesh):
    return jax.shard_map(
        shards,
        mesh=mesh,
        in_specs=(
            P("seq", "chan"),
            P("seq", "chan"),
            P("seq", "chan"),
            P(None, "chan"),
            P("seq", "chan"),
            P("seq", "chan"),
            P("chan", "seq"),
            P("seq", "chan"),
            P("seq", "chan"),
            P("chan"),
            P("seq", "chan"),
        ),
        out_specs=(P("seq", "chan"), P("seq", "chan")),
        check_vma=False,
    )
```

profile of v0, /device:TPU:0, one launch (start us, length us, event | category | flops | bytes accessed | tf_op | source)
XLA Modules:
  0.0 911.1 jit_solution(13444177433485212782)
XLA Ops:
  7.2 3.9 mul.363
  11.1 1.7 copy-done.6
  12.8 0.8 slice.20
  13.6 3.2 collective-permute-start
  16.8 4.5 all-to-all-start.1
  21.3 4.7 rev.3
  26.0 2.5 pad_maximum_fusion.3
  28.6 2.7 broadcast_in_dim.87
  31.3 31.4 %fusion.78 = f32[1,768,1024]{2,0,1:T(1,128)S(1)} fusion(f32[1,895,1024]{2,0,1:T(1,128)S(1)} %broadcast_in_dim.87, f32[128,1,1024]{2,0,1:T(8,128)S(1)} %bitcast.253), kind=kOutput, calls=%fused_computation.100 | convolution fusion | flops 1207959552 | bytes 7335936 | tf_op jit(solution)/shard_map/conv_general_dilated | solution.py:25
  62.7 1.7 copy-done.9
  64.4 2.6 copy_bitcast_fusion
  67.0 5.4 all-to-all-start
  72.4 0.0 all-gather.5.cloned.1.call-start
  72.4 3.7 copy.79
  76.1 4.7 collective-permute-start.1
  80.9 0.2 fusion.102
  81.1 5.4 copy.66
  86.5 4.7 concatenate.13
  91.2 36.5 %all-to-all-done = f32[8,128,768]{1,2,0:T(8,128)} async-done(((f32[8,128,768]{1,2,0:T(8,128)}), f32[8,128,768]{1,2,0:T(8,128)}, u32[]{:S(2)}, u32[]{:S(2)}) %all-to-all-start) | async-done | bytes 3145760 | tf_op jit(solution)/shard_map/all_to_all | solution.py:103
  127.7 3.5 copy.99
  131.2 15.3 %fusion.47 = f32[256,128,96]{1,2,0:T(8,128)} fusion(f32[128,48,128]{2,1,0:T(8,128)} %concatenate.13, f32[128,48,128]{2,1,0:T(8,128)} %copy.99), kind=kOutput, calls=%fused_computation.64 | convolution fusion | flops 1813553664 | bytes 18874368 | tf_op jit(solution)/shard_map/kn,cnq->ckq/dot_general | solution.py:55
  146.5 21.8 %fusion.10 = (f32[256,96,128]{2,1,0:T(8,128)}, f32[256,96,128]{2,1,0:T(8,128)}) fusion(f32[256,128,96]{1,2,0:T(8,128)} %fusion.47, f32[96,128]{1,0:T(8,128)S(1)} %get-tuple-element.29, f32[96,128]{1,0:T(8,128)S(1)} %get-tuple-element.30, f32[128,48,128]{2,1,0:T(8,128)} %concatenate.13, f32[128,48,128]{2,1,0:T(8,128)} %copy.99), kind=kOutput, calls=%fused_computation.20 | convolution fusion | flops 1835573760 | bytes 44138496 | tf_op jit(solution)/shard_map/kn,cnq->ckq/dot_general | solution.py:54
  168.3 24.1 %fusion.12 = f32[256,96,128]{2,0,1:T(8,128)} fusion(f32[256,96,128]{2,1,0:T(8,128)} %get-tuple-element.11), kind=kOutput, calls=%fused_computation.24 | convolution fusion | flops 4832067584 | bytes 25165824 | tf_op jit(solution)/shard_map/dot_general | solution.py:61
  192.4 22.9 %fusion.14 = f32[256,96,128]{2,0,1:T(8,128)} fusion(f32[256,96,128]{2,1,0:T(8,128)S(1)} %copy-done.1), kind=kOutput, calls=%fused_computation.26 | convolution fusion | flops 4832067584 | bytes 25165824 | tf_op jit(solution)/shard_map/dot_general | solution.py:58
  215.3 23.2 %fusion.52 = f32[256,96,128]{2,0,1:T(8,128)} fusion(f32[256,96,128]{2,0,1:T(8,128)} %fusion.12, f32[256,96,128]{2,1,0:T(8,128)S(1)} %bitcast.244), kind=kOutput, calls=%fused_computation.67 | convolution fusion | flops 4835213312 | bytes 37748736 | tf_op jit(solution)/shard_map/dot_general | solution.py:61
  238.5 23.2 %fusion.49 = f32[256,96,128]{2,0,1:T(8,128)} fusion(f32[256,96,128]{2,0,1:T(8,128)S(1)} %copy-done.2, f32[256,96,128]{2,1,0:T(8,128)S(1)} %bitcast.244), kind=kOutput, calls=%fused_computation.66 | convolution fusion | flops 4835213312 | bytes 37748736 | tf_op jit(solution)/shard_map/dot_general | solution.py:58
  261.7 9.7 %multiply_subtract_fusion.1 = (f32[128,96,128]{2,0,1:T(8,128)S(1)}, f32[128,96,128]{2,0,1:T(8,128)S(1)}) fusion(f32[256,96,128]{2,0,1:T(8,128)} %fusion.52, f32[256,96,128]{2,0,1:T(8,128)} %fusion.49), kind=kLoop, calls=%fused_computation.63 | loop fusion | flops 9437184 | bytes 37748736 | tf_op jit(solution)/shard_map/sub | solution.py:66
  271.4 7.3 fusion.83
  278.8 7.5 fusion.91
  286.3 7.3 fusion.85
  293.6 15.5 %multiply_subtract_fusion = (f32[128,96,128]{2,0,1:T(8,128)}, f32[128,96,128]{2,0,1:T(8,128)}) fusion(f32[96,128]{1,0:T(8,128)S(1)} %get-tuple-element.29, f32[96,128]{1,0:T(8,128)S(1)} %get-tuple-element.30, f32[128,96,128]{2,0,1:T(8,128)} %fusion.83, f32[128,96,128]{2,0,1:T(8,128)} %fusion.91, f32[128,96,128]{2,0,1:T(8,128)} %fusion.85, ...), kind=kOutput, calls=%fused_computation.61 | convolution fusion | flops 2428731392 | bytes 37847040 | tf_op jit(solution)/shard_map/dot_general | solution.py:71
  309.1 10.2 %fusion.43 = f32[128,128,48]{1,2,0:T(8,128)S(1)} fusion(f32[128,96,128]{2,0,1:T(8,128)} %get-tuple-element.9), kind=kOutput, calls=%fused_computation.56 | convolution fusion | flops 906011136 | bytes 9437184 | tf_op jit(solution)/shard_map/kn,ckq->cnq/dot_general | solution.py:76
  319.3 9.2 %multiply_bitcast_fusion = f32[128,48,128]{2,1,0:T(8,128)} fusion(f32[128,128,48]{1,2,0:T(8,128)S(1)} %fusion.43, f32[128,96,128]{2,0,1:T(8,128)S(1)} %copy-done.5), kind=kOutput, calls=%fused_computation.93 | convolution fusion | flops 907584000 | bytes 12582912 | tf_op jit(solution)/shard_map/kn,ckq->cnq/dot_general | solution.py:76
  328.5 3.8 copy.100
  332.3 4.5 all-to-all-start.2
  336.8 0.0 all-gather.3.cloned.1.call-start
  336.9 4.0 collective-permute-start.3
  340.9 33.8 %all-to-all-done.2 = f32[1,128,6144]{1,0,2:T(1,128)} async-done(((f32[1,128,6144]{1,0,2:T(1,128)}), f32[1,128,6144]{1,0,2:T(1,128)}, u32[]{:S(2)}, u32[]{:S(2)}) %all-to-all-start.2) | async-done | bytes 3145760 | tf_op jit(solution)/shard_map/all_to_all | solution.py:106
  374.7 3.9 copy.74
  378.6 7.2 fusion.56
  385.8 2.9 collective-permute-start.2
  388.7 20.3 %collective-permute-start.5 = (f32[768,1024]{0,1:T(8,128)}, f32[768,1024]{0,1:T(8,128)}, u32[]{:S(2)}, u32[]{:S(2)}) collective-permute-start(f32[768,1024]{0,1:T(8,128)} %collective-permute-done.3), channel_id=1, source_target_pairs={{0,4},{4,8},{8,12},{12,16},{16,20},{20,24},{24,28},{1,5},{5,9},{9,... | collective-permute-start | bytes 9437192 | tf_op jit(solution)/shard_map/ppermute | solution.py:20
  409.0 0.2 iota_compare_fusion
  409.3 22.6 %fusion.3 = (f32[8,768]{1,0:T(8,128)S(1)}, f32[8,768,768]{1,2,0:T(8,128)}) fusion(pred[768,768]{0,1:T(8,128)(4,1)S(1)} %iota_compare_fusion, pred[8]{0:T(512)(128)(4,1)S(1)} %get-tuple-element.17, f32[768,1024]{1,0:T(8,128)} %param.19, f32[768,1024]{1,0:T(8,128)S(1)} %copy-done), kind=kOutput, calls=%fused_computation.11 | convolution fusion | flops 7266625536 | bytes 25780232 | tf_op jit(solution)/shard_map/qhd,khd->hqk/dot_general | solution.py:120
  431.9 21.2 %fusion = (f32[8,768]{1,0:T(8,128)S(1)}, f32[8,768,768]{1,2,0:T(8,128)}) fusion(pred[8]{0:T(512)(128)(4,1)S(1)} %get-tuple-element.18, f32[768,8,128]{0,2,1:T(8,128)} %bitcast.22, f32[768,1024]{1,0:T(8,128)S(1)} %copy-done), kind=kOutput, calls=%fused_computation.8 | convolution fusion | flops 7261906944 | bytes 25190408 | tf_op jit(solution)/shard_map/qhd,khd->hqk/dot_general | solution.py:120
  453.1 3.5 copy.101
  456.6 21.2 %fusion.1 = (f32[8,768]{1,0:T(8,128)S(1)}, f32[8,768,768]{1,2,0:T(8,128)}) fusion(pred[8]{0:T(512)(128)(4,1)S(1)} %get-tuple-element.20, f32[768,8,128]{0,2,1:T(8,128)} %bitcast.26, f32[768,1024]{1,0:T(8,128)S(1)} %copy-done), kind=kOutput, calls=%fused_computation.9 | convolution fusion | flops 7261906944 | bytes 25190408 | tf_op jit(solution)/shard_map/qhd,khd->hqk/dot_general | solution.py:120
  477.7 4.4 collective-permute-start.4
  482.1 3.8 copy.102
  485.9 21.4 %fusion.2 = (f32[8,768]{1,0:T(8,128)S(1)}, f32[8,768,768]{1,2,0:T(8,128)}) fusion(pred[8]{0:T(512)(128)(4,1)S(1)} %get-tuple-element.19, f32[768,8,128]{0,2,1:T(8,128)} %bitcast.30, f32[768,1024]{1,0:T(8,128)S(1)} %copy-done), kind=kOutput, calls=%fused_computation.10 | convolution fusion | flops 7261906944 | bytes 25190408 | tf_op jit(solution)/shard_map/qhd,khd->hqk/dot_general | solution.py:120
  507.4 12.1 %fusion.20 = f32[8,768]{1,0:T(8,128)S(1)} fusion(f32[8,768,768]{1,2,0:T(8,128)} %get-tuple-element.28, f32[8,768]{1,0:T(8,128)S(1)} %get-tuple-element.16, pred[768,768]{0,1:T(8,128)(4,1)} %copy-done.10, pred[8]{0:T(512)(128)(4,1)S(1)} %get-tuple-element.17), kind=kLoop, calls=%fused_computation.32 | loop fusion | flops 28305408 | bytes 19513352 | tf_op jit(solution)/shard_map/reduce_sum | solution.py:128
  519.5 15.9 %fusion.4 = (f32[8,768]{1,0:T(8,128)S(1)}, f32[8,768]{1,0:T(8,128)S(1)}) fusion(f32[8,768,768]{1,2,0:T(8,128)} %get-tuple-element.26, f32[8,768]{1,0:T(8,128)S(1)} %get-tuple-element.7, pred[8]{0:T(512)(128)(4,1)S(1)} %get-tuple-element.18, f32[8,768]{1,0:T(8,128)S(1)} %get-tuple-element.6, f32[8,768,768]{1,2,0:T(8,128)} %get-tuple-element.24, ...), kind=kLoop, calls=%fused_computation.12 | loop fusion | flops 47173632 | bytes 37847056 | tf_op jit(solution)/shard_map/reduce_sum | solution.py:128
  535.4 10.7 %fusion.8 = f32[8,768]{1,0:T(8,128)S(1)} fusion(f32[8,768,768]{1,2,0:T(8,128)} %get-tuple-element.22, f32[8,768]{1,0:T(8,128)S(1)} %get-tuple-element.5, pred[8]{0:T(512)(128)(4,1)S(1)} %get-tuple-element.19), kind=kLoop, calls=%fused_computation.16 | loop fusion | flops 23586816 | bytes 18923528 | tf_op jit(solution)/shard_map/reduce_sum | solution.py:128
  546.1 0.6 bitcast_add_fusion.4
  546.8 21.8 %fusion.21 = f32[8,768,128]{1,2,0:T(8,128)} fusion(f32[768,8,128]{0,2,1:T(8,128)} %bitcast.249, f32[8,768,768]{1,2,0:T(8,128)} %get-tuple-element.28, f32[8,768]{1,0:T(8,128)S(1)} %get-tuple-element.16, pred[768,768]{0,1:T(8,128)(4,1)} %copy-done.10, pred[8]{0:T(512)(128)(4,1)S(1)} %get-tuple-element.17), kind=kOutput, calls=%fused_computation.33 | convolution fusion | flops 7271350272 | bytes 25780232 | tf_op jit(solution)/shard_map/hqk,khd->hqd/dot_general | solution.py:129
  568.6 2.9 collective-permute-start.6
  571.5 20.3 %fusion.5 = f32[8,768,128]{1,2,0:T(8,128)} fusion(f32[768,8,128]{0,2,1:T(8,128)S(1)} %bitcast.248, f32[8,768,768]{1,2,0:T(8,128)} %get-tuple-element.26, f32[8,768]{1,0:T(8,128)S(1)} %get-tuple-element.7, pred[8]{0:T(512)(128)(4,1)S(1)} %get-tuple-element.18), kind=kOutput, calls=%fused_computation.13 | convolution fusion | flops 7266631680 | bytes 25190408 | tf_op jit(solution)/shard_map/hqk,khd->hqd/dot_general | solution.py:129
  591.8 3.5 copy.103
  595.4 20.4 %fusion.7 = f32[8,768,128]{1,2,0:T(8,128)} fusion(f32[768,8,128]{0,2,1:T(8,128)} %bitcast.252, f32[8,768,768]{1,2,0:T(8,128)} %get-tuple-element.24, f32[8,768]{1,0:T(8,128)S(1)} %get-tuple-element.6, pred[8]{0:T(512)(128)(4,1)S(1)} %get-tuple-element.20), kind=kOutput, calls=%fused_computation.15 | convolution fusion | flops 7266631680 | bytes 25190408 | tf_op jit(solution)/shard_map/hqk,khd->hqd/dot_general | solution.py:129
  615.8 3.5 copy.104
  619.3 22.0 %fusion.68 = f32[768,8,128]{0,2,1:T(8,128)} fusion(f32[8,768,128]{1,2,0:T(8,128)} %fusion.7, f32[8,768,128]{1,2,0:T(8,128)} %fusion.5, f32[8,768,128]{1,2,0:T(8,128)} %fusion.21, f32[768,8,128]{0,2,1:T(8,128)} %bitcast.251, f32[8,768,768]{1,2,0:T(8,128)} %get-tuple-element.22, f32[8,768]{1,0:T(8,128)S(1)} %get-tuple-element.5, ...), kind=kOutput, calls=%fused_computation.86 | convolution fusion | flops 7272923136 | bytes 34750472 | tf_op jit(solution)/shard_map/hqk,khd->hqd/dot_general | solution.py:129
  641.4 0.0 all-gather.5.cloned.1.call-done
  641.4 217.4 %all-gather.3.cloned.1.call-done = f32[768,4096]{0,1:T(8,128)} async-done(((f32[768,1024]{0,1:T(8,128)}), f32[768,4096]{0,1:T(8,128)}) %all-gather.3.cloned.1.call-update) | async-done | bytes 12582928 | tf_op jit(solution)/shard_map/all_gather | solution.py:145
  858.8 45.2 %fusion.211 = f32[768,1024]{1,0:T(8,128)} fusion(f32[768,4096]{0,1:T(8,128)} %all-gather.3.cloned.1.call-done, f32[4096,1024]{1,0:T(8,128)} %all-gather.5.cloned.1.call-done), kind=kOutput, calls=%fused_computation.237 | convolution fusion | flops 38654705664 | bytes 32505856 | tf_op jit(solution)/shard_map/dot_general | solution.py:146
  (49 shorter events, 0.2 us)
Async XLA Ops:
  7.2 402.1 %copy-start = (f32[768,1024]{1,0:T(8,128)S(1)}, f32[768,1024]{1,0:T(8,128)}, u32[]{:S(2)}) copy-start(f32[768,1024]{1,0:T(8,128)} %param.18) | copy-start | bytes 9437188
  11.1 1.7 copy-start.6
  13.6 12.4 %collective-permute-start = (f32[127,1024]{1,0:T(8,128)}, f32[127,1024]{1,0:T(8,128)}, u32[]{:S(2)}, u32[]{:S(2)}) collective-permute-start(f32[127,1024]{1,0:T(8,128)} %slice.20), channel_id=1, source_target_pairs={{0,4},{4,8},{8,12},{12,16},{16,20},{20,24},{24,28},{1,5},{5,9},{9,... | collective-permute-start | bytes 1560584 | tf_op jit(solution)/shard_map/ppermute | solution.py:20
  16.8 50.2 %all-to-all-start.1 = ((f32[8,128,768]{2,1,0:T(8,128)}), f32[8,128,768]{2,1,0:T(8,128)}, u32[]{:S(2)}, u32[]{:S(2)}) async-start(f32[8,128,768]{2,1,0:T(8,128)} %bitcast.247), calls=%async_computation.1 | async-start | bytes 6291456 | tf_op jit(solution)/shard_map/all_to_all | solution.py:104
  26.0 5.3 copy-start.13
  31.3 33.1 %copy-start.3 = (f32[768,1024]{1,0:T(8,128)S(1)}, f32[768,1024]{1,0:T(8,128)}, u32[]{:S(2)}) copy-start(f32[768,1024]{1,0:T(8,128)} %param.11) | copy-start | bytes 9437188
  31.3 33.1 %copy-start.7 = (f32[768,1024]{1,0:T(8,128)S(1)}, f32[768,1024]{1,0:T(8,128)}, u32[]{:S(2)}) copy-start(f32[768,1024]{1,0:T(8,128)} %param.13) | copy-start | bytes 9437188
  31.3 33.1 %copy-start.12 = (f32[768,1024]{1,0:T(8,128)S(1)}, f32[768,1024]{1,0:T(8,128)}, u32[]{:S(2)}) copy-start(f32[768,1024]{1,0:T(8,128)} %param.15) | copy-start | bytes 9437188
  62.7 1.7 copy-start.9
  67.0 60.7 %all-to-all-start = ((f32[8,128,768]{1,2,0:T(8,128)}), f32[8,128,768]{1,2,0:T(8,128)}, u32[]{:S(2)}, u32[]{:S(2)}) async-start(f32[8,128,768]{1,2,0:T(8,128)} %copy_bitcast_fusion), calls=%async_computation | async-start | bytes 6291456 | tf_op jit(solution)/shard_map/all_to_all | solution.py:103
  72.4 569.0 %all-gather.5.cloned.1.call-start = ((), (), s32[]{:S(2)}) async-start(), calls=%async_computation.4 | async-start | bytes 18874368 | tf_op jit(solution)/shard_map/all_gather | solution.py:148
  76.1 260.8 %collective-permute-start.1 = (f32[768,1024]{0,1:T(8,128)}, f32[768,1024]{0,1:T(8,128)}, u32[]{:S(2)}, u32[]{:S(2)}) collective-permute-start(f32[768,1024]{0,1:T(8,128)} %copy.79), channel_id=1, source_target_pairs={{0,4},{4,8},{8,12},{12,16},{16,20},{20,24},{24,28},{1,5},{5,9},{9,... | collective-permute-start | bytes 9437192 | tf_op jit(solution)/shard_map/ppermute | solution.py:20
  168.3 24.1 %copy-start.1 = (f32[256,96,128]{2,1,0:T(8,128)S(1)}, f32[256,96,128]{2,1,0:T(8,128)}, u32[]{:S(2)}) copy-start(f32[256,96,128]{2,1,0:T(8,128)} %get-tuple-element.11) | copy-start | bytes 37748740
  168.3 47.0 %slice-start = ((s8[12582912]{0:T(1024)(128)(4,1)}), s8[4194304]{0:T(1024)(128)(4,1)S(1)}, s32[]{:S(2)}) async-start(s8[12582912]{0:T(1024)(128)(4,1)} %bitcast.243), calls=%async_computation.5 | async-start | bytes 8388608
  168.3 47.0 %slice-start.1 = ((s8[12582912]{0:T(1024)(128)(4,1)}), s8[4194304]{0:T(1024)(128)(4,1)S(1)}, s32[]{:S(2)}) async-start(s8[12582912]{0:T(1024)(128)(4,1)} %bitcast.243), calls=%async_computation.6 | async-start | bytes 8388608
  192.4 22.9 %slice-start.2 = ((s8[12582912]{0:T(1024)(128)(4,1)}), s8[4194304]{0:T(1024)(128)(4,1)S(1)}, s32[]{:S(2)}) async-start(s8[12582912]{0:T(1024)(128)(4,1)} %bitcast.243), calls=%async_computation.7 | async-start | bytes 8388608
  215.3 23.2 %copy-start.2 = (f32[256,96,128]{2,0,1:T(8,128)S(1)}, f32[256,96,128]{2,0,1:T(8,128)}, u32[]{:S(2)}) copy-start(f32[256,96,128]{2,0,1:T(8,128)} %fusion.14) | copy-start | bytes 37748740
  309.1 10.2 %copy-start.5 = (f32[128,96,128]{2,0,1:T(8,128)S(1)}, f32[128,96,128]{2,0,1:T(8,128)}, u32[]{:S(2)}) copy-start(f32[128,96,128]{2,0,1:T(8,128)} %get-tuple-element.8) | copy-start | bytes 18874372
  332.3 42.4 %all-to-all-start.2 = ((f32[1,128,6144]{1,0,2:T(1,128)}), f32[1,128,6144]{1,0,2:T(1,128)}, u32[]{:S(2)}, u32[]{:S(2)}) async-start(f32[1,128,6144]{1,0,2:T(1,128)} %bitcast.246), calls=%async_computation.2 | async-start | bytes 6291456 | tf_op jit(solution)/shard_map/all_to_all | solution.py:106
  336.8 522.0 %all-gather.3.cloned.1.call-start = ((), (), s32[]{:S(2)}) async-start(), calls=%async_computation.3 | async-start | bytes 15728640 | tf_op jit(solution)/shard_map/all_gather | solution.py:145
  336.9 51.9 %collective-permute-start.3 = (f32[768,1024]{0,1:T(8,128)}, f32[768,1024]{0,1:T(8,128)}, u32[]{:S(2)}, u32[]{:S(2)}) collective-permute-start(f32[768,1024]{0,1:T(8,128)} %collective-permute-done.1), channel_id=1, source_target_pairs={{0,4},{4,8},{8,12},{12,16},{16,20},{20,24},{24,28},{1,5},{5,9},{9,... | collective-permute-start | bytes 9437192 | tf_op jit(solution)/shard_map/ppermute | solution.py:20
  374.7 3.9 copy-start.4
  374.7 3.9 copy-start.8
  378.6 30.7 %copy-start.15 = (s32[8]{0:T(128)S(1)}, s32[8]{0:T(128)}, u32[]{:S(2)}) copy-start(s32[8]{0:T(128)} %param.20) | copy-start | bytes 100
  385.8 91.9 %collective-permute-start.2 = (f32[768,1024]{1,0:T(8,128)}, f32[768,1024]{1,0:T(8,128)}, u32[]{:S(2)}, u32[]{:S(2)}) collective-permute-start(f32[768,1024]{1,0:T(8,128)} %fusion.56), channel_id=1, source_target_pairs={{0,4},{4,8},{8,12},{12,16},{16,20},{20,24},{24,28},{1,5},{5,9},{9,... | collective-permute-start | bytes 9437192 | tf_op jit(solution)/shard_map/ppermute | solution.py:20
  388.7 97.2 %collective-permute-start.5 = (f32[768,1024]{0,1:T(8,128)}, f32[768,1024]{0,1:T(8,128)}, u32[]{:S(2)}, u32[]{:S(2)}) collective-permute-start(f32[768,1024]{0,1:T(8,128)} %collective-permute-done.3), channel_id=1, source_target_pairs={{0,4},{4,8},{8,12},{12,16},{16,20},{20,24},{24,28},{1,5},{5,9},{9,... | collective-permute-start | bytes 9437192 | tf_op jit(solution)/shard_map/ppermute | solution.py:20
  409.2 22.6 %copy-start.10 = (pred[768,768]{0,1:T(8,128)(4,1)}, pred[768,768]{0,1:T(8,128)(4,1)S(1)}, u32[]{:S(2)}) copy-start(pred[768,768]{0,1:T(8,128)(4,1)S(1)} %iota_compare_fusion) | copy-start | bytes 1769476
  477.7 90.9 %collective-permute-start.4 = (f32[768,1024]{1,0:T(8,128)}, f32[768,1024]{1,0:T(8,128)}, u32[]{:S(2)}, u32[]{:S(2)}) collective-permute-start(f32[768,1024]{1,0:T(8,128)} %collective-permute-done.2), channel_id=1, source_target_pairs={{0,4},{4,8},{8,12},{12,16},{16,20},{20,24},{24,28},{1,5},{5,9},{9,... | collective-permute-start | bytes 9437192 | tf_op jit(solution)/shard_map/ppermute | solution.py:20
  546.8 24.8 %copy-start.11 = (f32[768,1024]{0,1:T(8,128)S(1)}, f32[768,1024]{0,1:T(8,128)}, u32[]{:S(2)}) copy-start(f32[768,1024]{0,1:T(8,128)} %copy.102) | copy-start | bytes 9437188
  568.6 47.2 %collective-permute-start.6 = (f32[768,1024]{1,0:T(8,128)}, f32[768,1024]{1,0:T(8,128)}, u32[]{:S(2)}, u32[]{:S(2)}) collective-permute-start(f32[768,1024]{1,0:T(8,128)} %collective-permute-done.4), channel_id=1, source_target_pairs={{0,4},{4,8},{8,12},{12,16},{16,20},{20,24},{24,28},{1,5},{5,9},{9,... | collective-permute-start | bytes 9437192 | tf_op jit(solution)/shard_map/ppermute | solution.py:20
  615.7 3.6 copy-start.14
Sparse Core Ops, SparseCore 0:
  81.0 131.1 all-gather.4
  641.5 217.2 all-gather.2
where the time goes:
time: 917 us; the launch traced here: 911 us
  matrix products  435 us (47%)
  waiting for transfers between devices  288 us (31%)
  other arithmetic  65.8 us (7%)
  starting transfers between devices  56.9 us (6%)
  local copies, waits for them, and re-layouts  51 us (6%)
  between operations  14.5 us (2%)
    all_gather x1, waiting for transfers between devices, shards(): all_heads = lax.all_gather(attended, 'chan', axis=1, tiled=True)  217 us
    dot_general x4, matrix products, absorb_block(): jnp.einsum('qhd,khd->hqk', query_heads, key_heads, precision=highest_mode)  86.4 us
    dot_general x4, matrix products, absorb_block(): jnp.einsum('hqk,khd->hqd', weight, value_heads, precision=highest_mode)  84.5 us
    dot_general x1, matrix products, shards(): jnp.dot(all_heads, lax.all_gather(out_weight, 'seq', axis=0, tiled=True),...  45.2 us
    ppermute x7, starting transfers between devices, from_behind(): return lax.ppermute(shard, axis, pairs)  42.5 us
    reduce_sum x3, other arithmetic, absorb_block(): running_sum = running_sum * shrink + jnp.sum(weight, axis=2)  38.8 us
    all_to_all x1, waiting for transfers between devices, shards(): lax.all_to_all(long_in, 'seq', split_axis=0, concat_axis=2, tiled=True)  36.5 us
    all_to_all x1, waiting for transfers between devices, shards(): lax.all_to_all(convolved[None], 'seq', split_axis=2, concat_axis=0, tiled...  33.8 us
  transfers between devices with their start and end apart: 12, of which 3 were waited for; matrix products, arithmetic and copies ran while one was open for 55% of the time, Pallas kernels for 0%

commit v1 on v0

v1 whole, which is shorter than its diff:
```python
import functools
import math

import jax
import jax.numpy as jnp
import numpy as np
from jax import lax
from jax.experimental import pallas as pl
from jax.experimental.pallas import tpu as pltpu
from jax.sharding import PartitionSpec as P

HEAD_DIM = 128
REACH = 3
INNER = 128
SUB = 8
CHUNKS = 2

F32 = jnp.float32
BF16 = jnp.bfloat16
masked_low = -1e30
VMEM_CAP = 58 * 1024 * 1024


def halves(x):
    hi = x.astype(BF16)
    lo = (x - hi.astype(F32)).astype(BF16)
    return hi, lo


def const_halves(x):
    x = np.asarray(x, np.float32)
    hi = x.astype(BF16)
    lo = (x - hi.astype(np.float32)).astype(BF16)
    return hi, lo


def mm(a, b):
    return jnp.dot(a, b, preferred_element_type=F32)


def mm3(a_hi, a_lo, b):
    b_hi, b_lo = halves(b)
    return mm(a_hi, b_hi) + (mm(a_lo, b_hi) + mm(a_hi, b_lo))


@functools.lru_cache(None)
def short_tables(taps):
    size = 2 * taps
    freq = 2.0 * np.pi * (np.arange(taps) + 0.5) / size
    angle = freq[:, None] * np.arange(size)[None, :]
    forward = np.concatenate([np.cos(angle), -np.sin(angle)], axis=0)
    back = angle[:, taps:].T
    inverse = np.concatenate([np.cos(back), -np.sin(back)], axis=1) * (2.0 / size)
    return const_halves(forward) + const_halves(inverse)


def short_kernel(
    f_hi, f_lo, g_hi, g_lo, halo, stream, pre, post, taps_ref, long_pre, out_ref, in_ref
):
    taps = taps_ref.shape[0]
    group = in_ref.shape[2]
    spec = mm3(f_hi[:, :taps], f_lo[:, :taps], taps_ref[...])
    h_re, h_im = spec[:taps], spec[taps:]
    before = halo[...]
    for block in range(stream.shape[0] // taps):
        rows = pl.ds(block * taps, taps)
        signal = stream[rows, :]
        here = pre[rows, :] * signal
        window = jnp.concatenate([before, here], axis=0)
        before = here
        x = mm3(f_hi[...], f_lo[...], window)
        x_re, x_im = x[:taps], x[taps:]
        z = jnp.concatenate([x_re * h_re - x_im * h_im, x_re * h_im + x_im * h_re], axis=0)
        conv = mm3(g_hi[...], g_lo[...], z)
        short_out = signal + post[rows, :] * conv
        out_ref[rows, :] = short_out
        long_in = long_pre[rows, :] * short_out
        for g in range(in_ref.shape[0]):
            in_ref[g, rows, :] = long_in[:, g * group : (g + 1) * group]


def short_stage(halo, stream, pre, post, taps, long_pre, parts):
    length, width = stream.shape
    taps_n = taps.shape[0]
    tile = min(width, 256)
    group = width // parts
    tables = short_tables(taps_n)
    wide = pl.BlockSpec((length, tile), lambda i: (0, i))
    narrow = pl.BlockSpec((taps_n, tile), lambda i: (0, i))
    fixed = [pl.BlockSpec(t.shape, lambda i: (0, 0)) for t in tables]
    return pl.pallas_call(
        short_kernel,
        grid=(width // tile,),
        in_specs=fixed + [narrow, wide, wide, wide, narrow, wide],
        out_specs=[wide, pl.BlockSpec((tile // group, length, group), lambda i: (i, 0, 0))],
        out_shape=[
            jax.ShapeDtypeStruct((length, width), F32),
            jax.ShapeDtypeStruct((parts, length, group), F32),
        ],
        compiler_params=pltpu.CompilerParams(vmem_limit_bytes=VMEM_CAP),
        name="short_stage",
    )(*tables, halo, stream, pre, post, taps, long_pre)


@functools.lru_cache(None)
def long_tables(length):
    outer = length // INNER
    k1 = np.arange(outer) + 0.25
    sub = np.arange(SUB)
    phase = (
        k1[:, None, None] * np.arange(outer)[None, :, None] / outer
        + k1[:, None, None] * sub[None, None, :] / length
    )
    angle = 2.0 * np.pi * phase
    eye = np.eye(SUB)

    def spread(values):
        full = np.einsum("knr,rs->krns", values, eye)
        return full.reshape(outer * SUB, outer * SUB)

    first = np.concatenate([spread(np.cos(angle)), spread(-np.sin(angle))], axis=0)
    last = np.concatenate([spread(np.cos(angle)).T, spread(-np.sin(angle)).T], axis=1) / length
    inner = 2.0 * np.pi * np.outer(np.arange(INNER), np.arange(INNER)) / INNER
    c, s = np.cos(inner), np.sin(inner)
    middle = np.block([[c, s], [-s, c]])
    unmiddle = np.block([[c, -s], [s, c]])
    turn = 2.0 * np.pi * k1[None, :] * (SUB * np.arange(INNER // SUB))[:, None] / length
    scal_re = np.cos(turn).astype(np.float32)
    scal_im = np.sin(turn).astype(np.float32)
    return (
        const_halves(first),
        const_halves(last),
        const_halves(middle),
        const_halves(unmiddle),
        scal_re,
        scal_im,
    )


def forward_outer(x_ref, w_hi, w_lo, t_re, t_im, work):
    outer = x_ref.shape[0]
    lanes = x_ref.shape[2]

    def pair(i, carry):
        tiles = [
            x_ref[:, pl.ds(pl.multiple_of((2 * i + u) * SUB, SUB), SUB), :].reshape(
                outer * SUB, lanes
            )
            for u in range(2)
        ]
        out = mm3(w_hi[...], w_lo[...], jnp.concatenate(tiles, axis=1))
        for u in range(2):
            j = 2 * i + u
            row = pl.multiple_of(j * SUB, SUB)
            for k in range(outer):
                re = out[k * SUB : (k + 1) * SUB, u * lanes : (u + 1) * lanes]
                im = out[(outer + k) * SUB : (outer + k + 1) * SUB, u * lanes : (u + 1) * lanes]
                c, s = t_re[j, k], t_im[j, k]
                work[k, pl.ds(row, SUB), :] = re * c + im * s
                work[k, pl.ds(pl.multiple_of(INNER + row, SUB), SUB), :] = im * c - re * s
        return carry

    lax.fori_loop(0, INNER // SUB // 2, pair, 0)


def filter_kernel(w_hi, w_lo, b_hi, b_lo, t_re, t_im, filt, spec, x_ref, work):
    per = filt.shape[2] // INNER

    def turn(s, carry):
        for a in range(per):
            x_ref[per * s + a] = filt[s, :, a * INNER : (a + 1) * INNER].T
        return carry

    lax.fori_loop(0, filt.shape[0], turn, 0)
    forward_outer(x_ref, w_hi, w_lo, t_re, t_im, work)
    lanes = x_ref.shape[2]

    def inner(i, carry):
        both = jnp.concatenate([work[2 * i], work[2 * i + 1]], axis=1)
        out = mm3(b_hi[...], b_lo[...], both)
        spec[2 * i] = out[:, :lanes]
        spec[2 * i + 1] = out[:, lanes:]
        return carry

    lax.fori_loop(0, work.shape[0] // 2, inner, 0)


def signal_kernel(
    w_hi, w_lo, v_hi, v_lo, b_hi, b_lo, u_hi, u_lo, t_re, t_im, x_ref, spec, out_ref, work
):
    outer = x_ref.shape[0]
    lanes = x_ref.shape[2]
    forward_outer(x_ref, w_hi, w_lo, t_re, t_im, work)

    def inner(i, carry):
        both = jnp.concatenate([work[2 * i], work[2 * i + 1]], axis=1)
        x = mm3(b_hi[...], b_lo[...], both)
        h = jnp.concatenate([spec[2 * i], spec[2 * i + 1]], axis=1)
        x_re, x_im, h_re, h_im = x[:INNER], x[INNER:], h[:INNER], h[INNER:]
        z = jnp.concatenate([x_re * h_re - x_im * h_im, x_re * h_im + x_im * h_re], axis=0)
        y = mm3(u_hi[...], u_lo[...], z)
        work[2 * i] = y[:, :lanes]
        work[2 * i + 1] = y[:, lanes:]
        return carry

    lax.fori_loop(0, outer // 2, inner, 0)

    def back(i, carry):
        tiles = []
        for u in range(2):
            j = 2 * i + u
            row = pl.multiple_of(j * SUB, SUB)
            res, ims = [], []
            for k in range(outer):
                re = work[k, pl.ds(row, SUB), :]
                im = work[k, pl.ds(pl.multiple_of(INNER + row, SUB), SUB), :]
                c, s = t_re[j, k], t_im[j, k]
                res.append(re * c - im * s)
                ims.append(re * s + im * c)
            tiles.append(jnp.concatenate(res + ims, axis=0))
        out = mm3(v_hi[...], v_lo[...], jnp.concatenate(tiles, axis=1))
        for u in range(2):
            row = pl.multiple_of((2 * i + u) * SUB, SUB)
            part = out[:, u * lanes : (u + 1) * lanes].reshape(outer, SUB, lanes)
            out_ref[:, pl.ds(row, SUB), :] = part
        return carry

    lax.fori_loop(0, INNER // SUB // 2, back, 0)


def vmem_spec():
    return pl.BlockSpec(memory_space=pltpu.VMEM)


def smem_spec():
    return pl.BlockSpec(memory_space=pltpu.SMEM)


def filter_stage(filt, length):
    first, _, middle, _, t_re, t_im = long_tables(length)
    outer = length // INNER
    lanes = filt.shape[1]
    return pl.pallas_call(
        filter_kernel,
        in_specs=[vmem_spec()] * 4 + [smem_spec()] * 2 + [vmem_spec()],
        out_specs=vmem_spec(),
        out_shape=jax.ShapeDtypeStruct((outer, 2 * INNER, lanes), F32),
        scratch_shapes=[
            pltpu.VMEM((outer, INNER, lanes), F32),
            pltpu.VMEM((outer, 2 * INNER, lanes), F32),
        ],
        compiler_params=pltpu.CompilerParams(vmem_limit_bytes=VMEM_CAP),
        name="filter_stage",
    )(*first, *middle, t_re, t_im, filt)


def signal_stage(signal, spec):
    outer, _, lanes = signal.shape
    first, last, middle, unmiddle, t_re, t_im = long_tables(outer * INNER)
    return pl.pallas_call(
        signal_kernel,
        in_specs=[vmem_spec()] * 8 + [smem_spec()] * 2 + [vmem_spec()] * 2,
        out_specs=vmem_spec(),
        out_shape=jax.ShapeDtypeStruct(signal.shape, F32),
        scratch_shapes=[pltpu.VMEM((outer, 2 * INNER, lanes), F32)],
        compiler_params=pltpu.CompilerParams(vmem_limit_bytes=VMEM_CAP),
        name="signal_stage",
    )(*first, *last, *middle, *unmiddle, t_re, t_im, signal, spec)


def angle_table(row_count, col_count, modulus):
    product = (
        lax.iota(jnp.int32, row_count)[:, None] * lax.iota(jnp.int32, col_count)[None, :] % modulus
    )
    phase = product.astype(F32) * (2.0 * math.pi / modulus)
    return (jnp.cos(phase), jnp.sin(phase))


def plain_long_convolve(signal, kernel):
    high = lax.Precision.HIGHEST
    channels, length = signal.shape
    outer_len = 2 * length // INNER
    half_len = outer_len // 2
    cos_o, sin_o = angle_table(outer_len, half_len, outer_len)
    cos_t, sin_t = angle_table(outer_len, INNER, 2 * length)
    cos_i, sin_i = angle_table(INNER, INNER, INNER)
    stacked = jnp.concatenate([signal, kernel], axis=0).reshape(2 * channels, half_len, INNER)
    real = jnp.einsum("kn,cnq->ckq", cos_o, stacked, precision=high)
    imag = -jnp.einsum("kn,cnq->ckq", sin_o, stacked, precision=high)
    t_re = real * cos_t + imag * sin_t
    t_im = imag * cos_t - real * sin_t
    s_re = jnp.dot(t_re, cos_i, precision=high) + jnp.dot(t_im, sin_i, precision=high)
    s_im = jnp.dot(t_im, cos_i, precision=high) - jnp.dot(t_re, sin_i, precision=high)
    x_re, h_re, x_im, h_im = s_re[:channels], s_re[channels:], s_im[:channels], s_im[channels:]
    p_re = x_re * h_re - x_im * h_im
    p_im = x_re * h_im + x_im * h_re
    b_re = jnp.dot(p_re, cos_i, precision=high) - jnp.dot(p_im, sin_i, precision=high)
    b_im = jnp.dot(p_im, cos_i, precision=high) + jnp.dot(p_re, sin_i, precision=high)
    u_re = b_re * cos_t - b_im * sin_t
    u_im = b_re * sin_t + b_im * cos_t
    result = jnp.einsum("kn,ckq->cnq", cos_o, u_re, precision=high) - jnp.einsum(
        "kn,ckq->cnq", sin_o, u_im, precision=high
    )
    return result.reshape(channels, length) / (2.0 * length)


def hyena_kernel(short_out, post, conv, out_ref):
    parts = [conv[g] for g in range(conv.shape[0])]
    here = parts[0] if len(parts) == 1 else jnp.concatenate(parts, axis=1)
    out_ref[...] = short_out[...] + post[...] * here


def hyena_stage(short_out, post, conv):
    length, width = short_out.shape
    parts, _, group = conv.shape
    tile = max(group, 128)
    wide = pl.BlockSpec((length, tile), lambda i: (0, i))
    return pl.pallas_call(
        hyena_kernel,
        grid=(width // tile,),
        in_specs=[
            wide,
            wide,
            pl.BlockSpec((tile // group, length, group), lambda i: (i, 0, 0)),
        ],
        out_specs=wide,
        out_shape=jax.ShapeDtypeStruct((length, width), F32),
        name="hyena_stage",
    )(short_out, post, conv)


def attend_kernel(reach_ref, chip_ref, *refs):
    steps = REACH + 2
    q_ref = refs[0]
    k_refs = refs[1 : 1 + steps]
    v_refs = refs[1 + steps : 1 + 2 * steps]
    out_ref, k_cat, v_cat, top, total, acc = refs[1 + 2 * steps :]
    head, odd, tile = pl.program_id(0), pl.program_id(1), pl.program_id(2)
    dim = q_ref.shape[2]
    rows = q_ref.shape[1]
    length = k_refs[0].shape[0]

    @pl.when((odd == 0) & (tile == 0))
    def _():
        for n in range(steps):
            hi, lo = halves(k_refs[n][...])
            k_cat[n] = jnp.concatenate([hi, hi, lo], axis=1)
            hi, lo = halves(v_refs[n][...])
            v_cat[n] = jnp.concatenate([hi, lo], axis=1)

    scale = math.log2(math.e) / math.sqrt(dim)
    q_hi, q_lo = halves(q_ref[0] * scale)
    q_cat = jnp.concatenate([q_hi, q_lo, q_hi], axis=1)
    reach = reach_ref[head]
    block = 2 * chip_ref[0] + odd

    def scores_of(slot):
        return lax.dot_general(
            q_cat, k_cat[slot], (((1,), (1,)), ((), ())), preferred_element_type=F32
        )

    def weigh(slot, weight):
        w_hi, w_lo = halves(weight)
        both = mm(w_hi, v_cat[slot])
        return both[:, :dim] + both[:, dim:] + mm(w_lo, v_cat[slot][:, :dim])

    own = odd + REACH
    scores = scores_of(own)
    row = tile * rows + lax.broadcasted_iota(jnp.int32, (rows, length), 0)
    col = lax.broadcasted_iota(jnp.int32, (rows, length), 1)
    scores = jnp.where(row >= col, scores, masked_low)
    best = jnp.max(scores, axis=1, keepdims=True)
    weight = jnp.exp2(scores - best)
    top[...] = best
    total[...] = jnp.sum(weight, axis=1, keepdims=True)
    acc[...] = weigh(own, weight)

    for distance in range(1, REACH + 1):

        @pl.when((distance <= reach) & (block >= distance))
        def _():
            slot = own - distance
            scores = scores_of(slot)
            old = top[...]
            best = jnp.maximum(old, jnp.max(scores, axis=1, keepdims=True))
            shrink = jnp.exp2(old - best)
            weight = jnp.exp2(scores - best)
            top[...] = best
            total[...] = total[...] * shrink + jnp.sum(weight, axis=1, keepdims=True)
            acc[...] = acc[...] * shrink + weigh(slot, weight)

    out_ref[0] = acc[...] / total[...]


def attend_stage(reach, chip, queries, keys, values, first_head, heads):
    blocks, length, _ = queries.shape
    rows = min(length, 256)
    steps = REACH + 2
    key_spec = pl.BlockSpec((length, HEAD_DIM), lambda h, b, t, *_: (0, first_head + h))
    value_spec = pl.BlockSpec((length, HEAD_DIM), lambda h, b, t, *_: (0, h))
    return pl.pallas_call(
        attend_kernel,
        grid_spec=pltpu.PrefetchScalarGridSpec(
            num_scalar_prefetch=2,
            grid=(heads, blocks, length // rows),
            in_specs=[pl.BlockSpec((1, rows, HEAD_DIM), lambda h, b, t, *_: (b, t, first_head + h))]
            + [key_spec] * steps
            + [value_spec] * steps,
            out_specs=pl.BlockSpec((1, rows, HEAD_DIM), lambda h, b, t, *_: (b, t, h)),
            scratch_shapes=[
                pltpu.VMEM((steps, length, 3 * HEAD_DIM), BF16),
                pltpu.VMEM((steps, length, 2 * HEAD_DIM), BF16),
                pltpu.VMEM((rows, 1), F32),
                pltpu.VMEM((rows, 1), F32),
                pltpu.VMEM((rows, HEAD_DIM), F32),
            ],
        ),
        out_shape=jax.ShapeDtypeStruct((blocks, length, heads * HEAD_DIM), F32),
        compiler_params=pltpu.CompilerParams(vmem_limit_bytes=VMEM_CAP),
        name="attend_stage",
    )(reach, chip, queries, *keys, *values)


def shards(
    stream,
    short_gate_pre,
    short_gate_post,
    short_filter,
    long_gate_pre,
    long_gate_post,
    long_filter,
    queries,
    key_vectors,
    head_reach,
    out_weight,
):
    length, width = stream.shape
    taps = short_filter.shape[0]
    parts = lax.axis_size("seq")
    group = width // parts
    here = lax.axis_index("seq")
    chip, core = here // 2, here % 2
    half = width // 2
    heads_half = half // HEAD_DIM
    chunks = math.gcd(CHUNKS, heads_half)
    heads_chunk = heads_half // chunks
    part = heads_chunk * HEAD_DIM

    def shift(x, by):
        pairs = [(i, i + by) for i in range(parts) if i + by < parts]
        return lax.ppermute(x, "seq", pairs)

    def swap(x):
        return lax.ppermute(x, "seq", [(i, i ^ 1) for i in range(parts)])

    def both_blocks(x):
        cols = x.shape[1] // 2
        mine = lax.dynamic_slice_in_dim(x, core * cols, cols, 1)
        other = swap(lax.dynamic_slice_in_dim(x, (1 - core) * cols, cols, 1))
        even = jnp.where(core == 0, mine, other)
        odd = jnp.where(core == 0, other, mine)
        return jnp.stack([even, odd])

    def window(pair):
        behind = shift(pair, 2)
        far = shift(pair[1], 4)
        return [far, behind[0], behind[1], pair[0], pair[1]]

    filt = long_filter.reshape(parts, group, length)
    filt = lax.all_to_all(filt, "seq", split_axis=0, concat_axis=0, tiled=True)

    tail = short_gate_pre[length - taps :] * stream[length - taps :]
    halo = shift(tail, 1)
    short_out, long_in = short_stage(
        halo, stream, short_gate_pre, short_gate_post, short_filter, long_gate_pre, parts
    )
    signal = lax.all_to_all(long_in, "seq", split_axis=0, concat_axis=0, tiled=True)

    whole = parts * length
    if group == 128 and whole <= 6144:
        spec = filter_stage(filt, whole)
        conv = signal_stage(signal.reshape(whole // INNER, INNER, group), spec)
        conv = conv.reshape(parts, length, group)
    else:
        conv = plain_long_convolve(
            signal.reshape(whole, group).T, filt.transpose(1, 0, 2).reshape(group, whole)
        ).T.reshape(parts, length, group)
    back = lax.all_to_all(conv, "seq", split_axis=0, concat_axis=0, tiled=True)
    hyena_out = hyena_stage(short_out, long_gate_post, back)

    query_pair = both_blocks(queries)
    keys = window(both_blocks(key_vectors))
    groups = [list(range(c, parts, 2)) for c in range(2)]
    weight = lax.all_gather(out_weight, "seq", axis=0, axis_index_groups=groups)

    reach = lax.dynamic_slice_in_dim(head_reach, core * heads_half, heads_half)
    chip_at = chip[None].astype(jnp.int32)
    mixed = None
    for n in range(chunks):
        cols = jnp.concatenate(
            [hyena_out[:, n * part : (n + 1) * part], hyena_out[:, half + n * part : half + (n + 1) * part]],
            axis=1,
        )
        values = window(both_blocks(cols))
        attended = attend_stage(
            lax.dynamic_slice_in_dim(reach, n * heads_chunk, heads_chunk),
            chip_at,
            query_pair,
            keys,
            values,
            n * heads_chunk,
            heads_chunk,
        ).reshape(2 * length, part)
        spread = lax.all_gather(attended, "chan", axis=0)
        product = lax.dot_general(
            spread,
            weight[:, n * part : (n + 1) * part, :],
            (((0, 2), (0, 1)), ((), ())),
            precision=lax.Precision.HIGH,
            preferred_element_type=F32,
        )
        mixed = product if mixed is None else mixed + product
    mixed = mixed.reshape(2, length, width)
    own = lax.dynamic_index_in_dim(mixed, core, 0, keepdims=False)
    mixed = own + swap(lax.dynamic_index_in_dim(mixed, 1 - core, 0, keepdims=False))
    return (hyena_out, mixed)


def solution(mesh):
    return jax.shard_map(
        shards,
        mesh=mesh,
        in_specs=(
            P("seq", "chan"),
            P("seq", "chan"),
            P("seq", "chan"),
            P(None, "chan"),
            P("seq", "chan"),
            P("seq", "chan"),
            P("chan", "seq"),
            P("seq", "chan"),
            P("seq", "chan"),
            P("chan"),
            P("seq", "chan"),
        ),
        out_specs=(P("seq", "chan"), P("seq", "chan")),
        check_vma=False,
    )
```

time: 917 us -> 710 us (0.77)
  matrix products: 435 us -> 28.9 us
  Pallas kernels: 0 us -> 127 us
  waiting for transfers between devices: 288 us -> 408 us
  other arithmetic: 65.8 us -> 18.8 us
  starting transfers between devices: 56.9 us -> 89.4 us
  local copies, waits for them, and re-layouts: 51 us -> 22.6 us
    dot_general x21 -> x2, matrix products: 404 us -> 28.9 us  [shards(): lax.dot_general(spread, weight[:, n * part:(n + 1) * part, :], (((0, 2),...]
    ppermute x7 -> x12, waiting for transfers between devices: 0.02 us -> 174 us  [the longest x7 162 us: shift(): return lax.ppermute(x, 'seq', pairs)]
    pallas_call x0 -> x6, Pallas kernels: none -> 127 us  [the longest x2 48.9 us: attend_stage(): pl.pallas_call(attend_kernel, grid_spec=pltpu.PrefetchScalarGridSpec(num_...]
    all_gather x2 -> x3, waiting for transfers between devices: 217 us -> 129 us  [the longest x2 129 us: shards(): spread = lax.all_gather(attended, 'chan', axis=0)]
    reduce_sum x3 -> x0, other arithmetic: 38.8 us -> none  [absorb_block(): running_sum = running_sum * shrink + jnp.sum(weight, axis=2)]
    all_to_all x3, waiting for transfers between devices: 70.3 us -> 104 us  [the longest x1 41.4 us: shards(): lax.all_to_all(long_in, 'seq', split_axis=0, concat_axis=0, tiled=True)]
    conv_general_dilated x1 -> x0, matrix products: 31.4 us -> none  [short_convolve(): lax.conv_general_dilated(extended[None], kernel, (1,), 'VALID', dimension...]
    all_to_all x3, starting transfers between devices: 14.3 us -> 33.9 us  [the longest x1 23.9 us: shards(): lax.all_to_all(long_in, 'seq', split_axis=0, concat_axis=0, tiled=True)]
  transfers between devices with their start and end apart: 12 -> 18, of which waited for: 3 -> 15; matrix products, arithmetic and copies ran while one was open for 55% -> 6% of each run, Pallas kernels for 0% -> 18%
where the time goes in v1:
time: 710 us; the launch traced here: 709 us
  waiting for transfers between devices  408 us (57%)
  Pallas kernels  127 us (18%)
  starting transfers between devices  89.4 us (13%)
  matrix products  28.9 us (4%)
  local copies, waits for them, and re-layouts  22.6 us (3%)
  other arithmetic  18.8 us (3%)
  between operations  14 us (2%)
    ppermute x7, waiting for transfers between devices, shift(): return lax.ppermute(x, 'seq', pairs)  162 us
    all_gather x2, waiting for transfers between devices, shards(): spread = lax.all_gather(attended, 'chan', axis=0)  129 us
    ppermute x7, starting transfers between devices, shift(): return lax.ppermute(x, 'seq', pairs)  54.5 us
    pallas_call x2, Pallas kernels, attend_stage(): pl.pallas_call(attend_kernel, grid_spec=pltpu.PrefetchScalarGridSpec(num_...  48.9 us
    all_to_all x1, waiting for transfers between devices, shards(): lax.all_to_all(long_in, 'seq', split_axis=0, concat_axis=0, tiled=True)  41.4 us
    all_to_all x1, waiting for transfers between devices, shards(): filt = lax.all_to_all(filt, 'seq', split_axis=0, concat_axis=0, tiled=True)  39 us
    pallas_call x1, Pallas kernels, signal_stage(): pl.pallas_call(signal_kernel, in_specs=[vmem_spec()] * 8 + [smem_spec()]...  35.9 us
    dot_general x2, matrix products, shards(): lax.dot_general(spread, weight[:, n * part:(n + 1) * part, :], (((0, 2),...  28.9 us
  transfers between devices with their start and end apart: 18, of which 15 were waited for; matrix products, arithmetic and copies ran while one was open for 6% of the time, Pallas kernels for 18%

profile of v1, /device:TPU:0, one launch (start us, length us, event | category | flops | bytes accessed | tf_op | source)
XLA Modules:
  0.0 708.8 jit_solution(16362564579065471084)
XLA Ops:
  7.2 0.7 all-gather.9.cloned.1.call-update
  7.9 5.2 all-to-all-start.1
  13.1 1.3 slice_multiply_fusion
  14.4 2.4 collective-permute-start
  16.8 1.5 collective-permute-done.halo
  18.3 0.8 copy-done.16
  19.1 15.3 %short_stage.1 = (f32[768,1024]{1,0:T(8,128)}, f32[8,768,128]{2,1,0:T(8,128)}) custom-call(bf16[256,256]{1,0:T(8,128)(2,1)} %constant.78.clone.f_hi, bf16[256,256]{1,0:T(8,128)(2,1)} %constant.79.clone.f_lo, bf16[128,256]{1,0:T(8,128)(2,1)} %constant.80.clone.g_hi, bf16[128,256]{1,0:T(8,128)(2,1)} %constant.81.clone.g_lo, f32[128,1024]{1,0:T(8,128)} %copy-done.16, ...), custom_call_target="tpu_custom_call" | custom-call | tf_op jit(solution)/shard_map/short_stage/pallas_call | solution.py:91
  34.4 39.0 %all-to-all-done.1.filt = f32[8,128,768]{2,1,0:T(8,128)S(1)} async-done(((f32[8,128,768]{2,1,0:T(8,128)}), f32[8,128,768]{2,1,0:T(8,128)S(1)}, u32[]{:S(2)}, u32[]{:S(2)}) %all-to-all-start.1) | async-done | bytes 3145760 | tf_op jit(solution)/shard_map/all_to_all | solution.py:470
  73.4 1.7 copy-done.2
  75.1 23.9 %all-to-all-start = ((f32[8,768,128]{2,1,0:T(8,128)}), f32[8,768,128]{2,1,0:T(8,128)}, u32[]{:S(2)}, u32[]{:S(2)}) async-start(f32[8,768,128]{2,1,0:T(8,128)} %get-tuple-element.5), calls=%async_computation | async-start | bytes 6291456 | tf_op jit(solution)/shard_map/all_to_all | solution.py:477
  99.0 19.6 %filter_stage.1.spec = f32[48,256,128]{2,1,0:T(8,128)} custom-call(bf16[768,384]{1,0:T(8,128)(2,1)} %constant.82.clone.w_hi, bf16[768,384]{1,0:T(8,128)(2,1)} %constant.83.clone.w_lo, bf16[256,256]{1,0:T(8,128)(2,1)} %constant.84.clone.b_hi, bf16[256,256]{1,0:T(8,128)(2,1)} %constant.85.clone.b_lo, f32[16,48]{1,0:T(8,128)} %constant.86.clone.t_re, ...), custom_call_target="tpu_custom_call" | custom-call | tf_op jit(solution)/shard_map/filter_stage/pallas_call | solution.py:243
  118.6 41.4 %all-to-all-done = f32[8,768,128]{2,1,0:T(8,128)} async-done(((f32[8,768,128]{2,1,0:T(8,128)}), f32[8,768,128]{2,1,0:T(8,128)}, u32[]{:S(2)}, u32[]{:S(2)}) %all-to-all-start) | async-done | bytes 3145760 | tf_op jit(solution)/shard_map/all_to_all | solution.py:477
  160.0 35.9 %signal_stage.1 = f32[48,128,128]{2,1,0:T(8,128)} custom-call(bf16[768,384]{1,0:T(8,128)(2,1)} %constant.82.clone.w_hi, bf16[768,384]{1,0:T(8,128)(2,1)} %constant.83.clone.w_lo, bf16[384,768]{1,0:T(8,128)(2,1)} %constant.88.clone.v_hi, bf16[384,768]{1,0:T(8,128)(2,1)} %constant.89.clone.v_lo, bf16[256,256]{1,0:T(8,128)(2,1)} %constant.84.clone.b_hi, ...), custom_call_target="tpu_custom_call" | custom-call | tf_op jit(solution)/shard_map/signal_stage/pallas_call | solution.py:260
  195.9 4.7 all-to-all-start.2
  200.7 1.3 constant_dynamic-slice_fusion
  202.0 0.3 collective-permute-start.2
  202.3 3.3 collective-permute-done.2
  205.6 1.8 dynamic-slice_select_fusion
  207.4 2.2 pad_maximum_fusion.1
  209.6 5.3 collective-permute-start.4
  214.9 23.5 %all-to-all-done.2.conv = f32[8,768,128]{2,1,0:T(8,128)} async-done(((f32[8,768,128]{2,1,0:T(8,128)}), f32[8,768,128]{2,1,0:T(8,128)}, u32[]{:S(2)}, u32[]{:S(2)}) %all-to-all-start.2) | async-done | bytes 3145760 | tf_op jit(solution)/shard_map/all_to_all | solution.py:488
  238.5 7.5 %hyena_stage.1 = f32[768,1024]{1,0:T(8,128)} custom-call(f32[768,1024]{1,0:T(8,128)} %get-tuple-element.4.short_out, f32[768,1024]{1,0:T(8,128)} %post.3, f32[8,768,128]{2,1,0:T(8,128)} %all-to-all-done.2.conv), custom_call_target="tpu_custom_call" | custom-call | tf_op jit(solution)/shard_map/hyena_stage/pallas_call | solution.py:318
  246.0 3.5 fusion.7
  249.4 0.9 copy-done.9
  250.3 0.2 fusion.6
  250.5 0.1 copy-done.10
  250.6 1.3 constant_dynamic-slice_fusion.1
  251.9 0.5 collective-permute-start.1
  252.4 0.6 collective-permute-done.5
  253.0 1.9 broadcast_select_fusion.2
  254.9 1.4 pad_maximum_fusion.2
  256.3 3.6 collective-permute-start.7
  259.9 3.1 collective-permute-start.3
  263.1 0.6 fusion.8
  263.7 2.2 select_bitcast_fusion.1
  266.0 1.5 collective-permute-start.6
  267.5 2.0 pad_maximum_fusion.refs_0_
  269.5 33.6 %collective-permute-done.4 = f32[2,768,512]{2,1,0:T(8,128)} collective-permute-done((f32[2,768,512]{2,1,0:T(8,128)}, f32[2,768,512]{2,1,0:T(8,128)}, u32[]{:S(2)}, u32[]{:S(2)}) %collective-permute-start.4) | collective-permute-done | bytes 3145760 | tf_op jit(solution)/shard_map/ppermute | solution.py:451
  303.1 3.8 slice_bitcast_fusion
  307.0 29.6 %collective-permute-done.7 = f32[2,768,256]{2,1,0:T(8,128)} collective-permute-done((f32[2,768,256]{2,1,0:T(8,128)}, f32[2,768,256]{2,1,0:T(8,128)}, u32[]{:S(2)}, u32[]{:S(2)}) %collective-permute-start.7) | collective-permute-done | bytes 1572896 | tf_op jit(solution)/shard_map/ppermute | solution.py:451
  336.6 2.7 slice_bitcast_fusion.4
  339.3 32.0 %collective-permute-done.3.refs_1_ = f32[768,512]{1,0:T(8,128)} collective-permute-done((f32[768,512]{1,0:T(8,128)S(1)}, f32[768,512]{1,0:T(8,128)}, u32[]{:S(2)}, u32[]{:S(2)}) %collective-permute-start.3) | collective-permute-done | bytes 1572896 | tf_op jit(solution)/shard_map/ppermute | solution.py:451
  371.3 16.8 %collective-permute-done.6.refs_6_ = f32[768,256]{1,0:T(8,128)S(1)} collective-permute-done((f32[768,256]{1,0:T(8,128)S(1)}, f32[768,256]{1,0:T(8,128)S(1)}, u32[]{:S(2)}, u32[]{:S(2)}) %collective-permute-start.6) | collective-permute-done | bytes 786464 | tf_op jit(solution)/shard_map/ppermute | solution.py:451
  388.1 0.9 copy-done.14
  389.0 24.4 %attend_stage.2 = f32[2,768,256]{2,1,0:T(8,128)} custom-call(s32[2]{0:T(128)} %get-tuple-element.25.reach_ref, s32[1]{0:T(128)} %bitcast.3.chip_ref, f32[2,768,512]{2,1,0:T(8,128)} %pad_maximum_fusion.refs_0_, f32[768,512]{1,0:T(8,128)} %collective-permute-done.3.refs_1_, f32[768,512]{1,0:T(8,128)} %get-tuple-element.15.refs_2_, ...), custom_call_target="tpu_custom_call" | custom-call | tf_op jit(solution)/shard_map/attend_stage/pallas_call | solution.py:401
  413.5 0.2 fusion.4
  413.6 0.1 collective-permute-start.8
  413.7 2.3 collective-permute-done.8
  416.0 0.2 broadcast_select_fusion
  416.2 0.1 pad_maximum_fusion.3
  416.3 1.4 collective-permute-start.10
  417.7 37.1 %collective-permute-start.9 = (f32[768,256]{1,0:T(8,128)S(1)}, f32[768,256]{1,0:T(8,128)S(1)}, u32[]{:S(2)}, u32[]{:S(2)}) collective-permute-start(f32[768,256]{1,0:T(8,128)S(1)} %get-tuple-element.17.refs_10_), channel_id=1, source_target_pairs={{0,16},{4,20},{8,24},{12,28},{1,17},{5,21},{9,25},{13,29},{2,18},{... | collective-permute-start | bytes 2359304 | tf_op jit(solution)/shard_map/ppermute | solution.py:451
  454.8 1.3 slice_bitcast_fusion.2
  456.1 48.5 %collective-permute-done.9.refs_6_ = f32[768,256]{1,0:T(8,128)S(1)} collective-permute-done((f32[768,256]{1,0:T(8,128)S(1)}, f32[768,256]{1,0:T(8,128)S(1)}, u32[]{:S(2)}, u32[]{:S(2)}) %collective-permute-start.9) | collective-permute-done | bytes 786464 | tf_op jit(solution)/shard_map/ppermute | solution.py:451
  504.6 0.9 copy-done.15
  505.5 24.5 %attend_stage.3 = f32[2,768,256]{2,1,0:T(8,128)} custom-call(s32[2]{0:T(128)} %get-tuple-element.24.reach_ref, s32[1]{0:T(128)} %bitcast.3.chip_ref, f32[2,768,512]{2,1,0:T(8,128)} %pad_maximum_fusion.refs_0_, f32[768,512]{1,0:T(8,128)} %collective-permute-done.3.refs_1_, f32[768,512]{1,0:T(8,128)} %get-tuple-element.15.refs_2_, ...), custom_call_target="tpu_custom_call" | custom-call | tf_op jit(solution)/shard_map/attend_stage/pallas_call | solution.py:401
  530.1 28.9 %all-gather.5.cloned.1.call-done = f32[4,1536,256]{2,1,0:T(8,128)} async-done(((f32[1,1536,256]{2,1,0:T(8,128)}), f32[4,1536,256]{2,1,0:T(8,128)}) %all-gather.5.cloned.1.call-update) | async-done | bytes 6291472 | tf_op jit(solution)/shard_map/all_gather | solution.py:514
  559.1 14.8 %fusion.1 = f32[1536,1024,1]{1,0,2:T(8,128)} fusion(f32[4,1536,256]{2,1,0:T(8,128)} %all-gather.5.cloned.1.call-done, f32[4,512,1024]{2,1,0:T(8,128)} %bitcast.52), kind=kOutput, calls=%fused_computation.2 | convolution fusion | flops 9663676416 | bytes 16777216 | tf_op jit(solution)/shard_map/dot_general | solution.py:515
  573.8 100.4 %all-gather.7.cloned.1.call-done = f32[4,1536,256]{2,1,0:T(8,128)} async-done(((f32[1,1536,256]{2,1,0:T(8,128)}), f32[4,1536,256]{2,1,0:T(8,128)}) %all-gather.7.cloned.1.call-update) | async-done | bytes 6291472 | tf_op jit(solution)/shard_map/all_gather | solution.py:514
  674.2 14.1 %bitcast_add_fusion = f32[1536,1024]{1,0:T(8,128)S(1)} fusion(f32[1536,1024,1]{1,0,2:T(8,128)} %fusion.1, f32[4,1536,256]{2,1,0:T(8,128)} %all-gather.7.cloned.1.call-done, f32[4,512,1024]{2,1,0:T(8,128)} %bitcast.53), kind=kOutput, calls=%fused_computation | convolution fusion | flops 9665249280 | bytes 23068672 | tf_op jit(solution)/shard_map/dot_general | solution.py:515
  688.3 0.4 dynamic-slice_bitcast_fusion
  688.7 2.3 copy-done.11
  691.0 5.8 collective-permute-done.11
  696.8 5.5 bitcast_add_fusion.1
  (40 shorter events, 0.3 us)
Async XLA Ops:
  7.2 522.9 %all-gather.9.cloned.1.call-start = ((), (), s32[]{:S(2)}) async-start(), calls=%async_computation.5 | async-start | bytes 10485760 | tf_op jit(solution)/shard_map/all_gather | solution.py:494
  7.9 65.5 %all-to-all-start.1 = ((f32[8,128,768]{2,1,0:T(8,128)}), f32[8,128,768]{2,1,0:T(8,128)S(1)}, u32[]{:S(2)}, u32[]{:S(2)}) async-start(f32[8,128,768]{2,1,0:T(8,128)} %bitcast.51), calls=%async_computation.1 | async-start | bytes 6291456 | tf_op jit(solution)/shard_map/all_to_all | solution.py:470
  14.4 3.9 collective-permute-start
  18.3 0.8 copy-start.16
  73.4 1.7 copy-start.2
  75.1 84.9 %all-to-all-start = ((f32[8,768,128]{2,1,0:T(8,128)}), f32[8,768,128]{2,1,0:T(8,128)}, u32[]{:S(2)}, u32[]{:S(2)}) async-start(f32[8,768,128]{2,1,0:T(8,128)} %get-tuple-element.5), calls=%async_computation | async-start | bytes 6291456 | tf_op jit(solution)/shard_map/all_to_all | solution.py:477
  195.9 4.8 copy-start.12
  195.9 42.6 %all-to-all-start.2 = ((f32[8,768,128]{2,1,0:T(8,128)}), f32[8,768,128]{2,1,0:T(8,128)}, u32[]{:S(2)}, u32[]{:S(2)}) async-start(f32[8,768,128]{2,1,0:T(8,128)} %bitcast.42), calls=%async_computation.2 | async-start | bytes 6291456 | tf_op jit(solution)/shard_map/all_to_all | solution.py:488
  200.6 358.5 %all-gather.5.cloned.1.call-start = ((), (), s32[]{:S(2)}) async-start(), calls=%async_computation.3 | async-start | bytes 7864320 | tf_op jit(solution)/shard_map/all_gather | solution.py:514
  202.0 3.6 collective-permute-start.2
  207.4 2.2 copy-start
  207.4 52.5 %copy-start.1 = (f32[768,512]{1,0:T(8,128)}, f32[768,512]{1,0:T(8,128)S(1)}, u32[]{:S(2)}) copy-start(f32[768,512]{1,0:T(8,128)S(1)} %get-tuple-element.7.refs_5_) | copy-start | bytes 4718596
  209.6 93.5 %collective-permute-start.4 = (f32[2,768,512]{2,1,0:T(8,128)}, f32[2,768,512]{2,1,0:T(8,128)}, u32[]{:S(2)}, u32[]{:S(2)}) collective-permute-start(f32[2,768,512]{2,1,0:T(8,128)} %pad_maximum_fusion.1), channel_id=1, source_target_pairs={{0,8},{4,12},{8,16},{12,20},{16,24},{20,28},{1,9},{5,13},{9,17},{1... | collective-permute-start | bytes 9437192 | tf_op jit(solution)/shard_map/ppermute | solution.py:451
  246.0 4.6 copy-start.13
  249.4 0.9 copy-start.9
  249.4 1.2 copy-start.10
  250.6 2.4 collective-permute-start.5
  251.9 11.8 %collective-permute-start.1 = (f32[768,512]{1,0:T(8,128)}, f32[768,512]{1,0:T(8,128)}, u32[]{:S(2)}, u32[]{:S(2)}) collective-permute-start(f32[768,512]{1,0:T(8,128)} %constant_dynamic-slice_fusion.1), channel_id=1, source_target_pairs={{0,4},{4,0},{8,12},{12,8},{16,20},{20,16},{24,28},{28,24},{1,5},{5... | collective-permute-start | bytes 4718600 | tf_op jit(solution)/shard_map/ppermute | solution.py:454
  252.4 10.7 %copy-start.17 = (s32[8]{0:T(128)S(1)}, s32[8]{0:T(128)}, u32[]{:S(2)}) copy-start(s32[8]{0:T(128)} %param.34) | copy-start | bytes 100
  254.9 11.1 %copy-start.3 = (f32[768,256]{1,0:T(8,128)}, f32[768,256]{1,0:T(8,128)S(1)}, u32[]{:S(2)}) copy-start(f32[768,256]{1,0:T(8,128)S(1)} %get-tuple-element.18.refs_9_) | copy-start | bytes 2359300
  254.9 11.1 %copy-start.4 = (f32[768,256]{1,0:T(8,128)}, f32[768,256]{1,0:T(8,128)S(1)}, u32[]{:S(2)}) copy-start(f32[768,256]{1,0:T(8,128)S(1)} %get-tuple-element.19.refs_10_) | copy-start | bytes 2359300
  256.3 80.3 %collective-permute-start.7 = (f32[2,768,256]{2,1,0:T(8,128)}, f32[2,768,256]{2,1,0:T(8,128)}, u32[]{:S(2)}, u32[]{:S(2)}) collective-permute-start(f32[2,768,256]{2,1,0:T(8,128)} %pad_maximum_fusion.2), channel_id=1, source_target_pairs={{0,8},{4,12},{8,16},{12,20},{16,24},{20,28},{1,9},{5,13},{9,17},{1... | collective-permute-start | bytes 4718600 | tf_op jit(solution)/shard_map/ppermute | solution.py:451
  259.9 111.4 %collective-permute-start.3 = (f32[768,512]{1,0:T(8,128)S(1)}, f32[768,512]{1,0:T(8,128)}, u32[]{:S(2)}, u32[]{:S(2)}) collective-permute-start(f32[768,512]{1,0:T(8,128)S(1)} %get-tuple-element.7.refs_5_), channel_id=1, source_target_pairs={{0,16},{4,20},{8,24},{12,28},{1,17},{5,21},{9,25},{13,29},{2,18},{... | collective-permute-start | bytes 4718600 | tf_op jit(solution)/shard_map/ppermute | solution.py:451
  266.0 122.1 %collective-permute-start.6 = (f32[768,256]{1,0:T(8,128)S(1)}, f32[768,256]{1,0:T(8,128)S(1)}, u32[]{:S(2)}, u32[]{:S(2)}) collective-permute-start(f32[768,256]{1,0:T(8,128)S(1)} %get-tuple-element.19.refs_10_), channel_id=1, source_target_pairs={{0,16},{4,20},{8,24},{12,28},{1,17},{5,21},{9,25},{13,29},{2,18},{... | collective-permute-start | bytes 2359304 | tf_op jit(solution)/shard_map/ppermute | solution.py:451
  388.1 0.9 copy-start.14
  389.0 24.5 %copy-start.7 = (f32[768,256]{1,0:T(8,128)S(1)}, f32[768,256]{1,0:T(8,128)}, u32[]{:S(2)}) copy-start(f32[768,256]{1,0:T(8,128)} %get-tuple-element.10) | copy-start | bytes 2359300
  389.0 24.5 %copy-start.8 = (f32[768,256]{1,0:T(8,128)S(1)}, f32[768,256]{1,0:T(8,128)}, u32[]{:S(2)}) copy-start(f32[768,256]{1,0:T(8,128)} %get-tuple-element.11) | copy-start | bytes 2359300
  413.4 260.8 %all-gather.7.cloned.1.call-start = ((), (), s32[]{:S(2)}) async-start(), calls=%async_computation.4 | async-start | bytes 7864320 | tf_op jit(solution)/shard_map/all_gather | solution.py:514
  413.6 2.4 collective-permute-start.8
  416.2 39.9 %copy-start.5 = (f32[768,256]{1,0:T(8,128)}, f32[768,256]{1,0:T(8,128)S(1)}, u32[]{:S(2)}) copy-start(f32[768,256]{1,0:T(8,128)S(1)} %get-tuple-element.16.refs_9_) | copy-start | bytes 2359300
  416.2 39.9 %copy-start.6 = (f32[768,256]{1,0:T(8,128)}, f32[768,256]{1,0:T(8,128)S(1)}, u32[]{:S(2)}) copy-start(f32[768,256]{1,0:T(8,128)S(1)} %get-tuple-element.17.refs_10_) | copy-start | bytes 2359300
  416.3 38.5 %collective-permute-start.10 = (f32[2,768,256]{2,1,0:T(8,128)S(1)}, f32[2,768,256]{2,1,0:T(8,128)S(1)}, u32[]{:S(2)}, u32[]{:S(2)}) collective-permute-start(f32[2,768,256]{2,1,0:T(8,128)S(1)} %pad_maximum_fusion.3), channel_id=1, source_target_pairs={{0,8},{4,12},{8,16},{12,20},{16,24},{20,28},{1,9},{5,13},{9,17},{1... | collective-permute-start | bytes 4718600 | tf_op jit(solution)/shard_map/ppermute | solution.py:451
  417.7 86.9 %collective-permute-start.9 = (f32[768,256]{1,0:T(8,128)S(1)}, f32[768,256]{1,0:T(8,128)S(1)}, u32[]{:S(2)}, u32[]{:S(2)}) collective-permute-start(f32[768,256]{1,0:T(8,128)S(1)} %get-tuple-element.17.refs_10_), channel_id=1, source_target_pairs={{0,16},{4,20},{8,24},{12,28},{1,17},{5,21},{9,25},{13,29},{2,18},{... | collective-permute-start | bytes 2359304 | tf_op jit(solution)/shard_map/ppermute | solution.py:451
  504.6 1.0 copy-start.15
  688.3 2.7 copy-start.11
  691.0 5.8 collective-permute-start.11
Sparse Core Ops, SparseCore 0:
  9.8 140.9 all-gather.8
  413.5 145.4 all-gather.4
  560.6 113.5 all-gather.6

commit v2 on v1

--- a/solution.py
+++ b/solution.py
@@ -13,7 +13,7 @@
 REACH = 3
 INNER = 128
 SUB = 8
-CHUNKS = 2
+
 
 F32 = jnp.float32
 BF16 = jnp.bfloat16
@@ -40,7 +40,8 @@
 
 def mm3(a_hi, a_lo, b):
     b_hi, b_lo = halves(b)
-    return mm(a_hi, b_hi) + (mm(a_lo, b_hi) + mm(a_hi, b_lo))
+    left = jnp.concatenate([a_hi, a_lo, a_hi], axis=1)
+    return mm(left, jnp.concatenate([b_hi, b_hi, b_lo], axis=0))
 
 
 @functools.lru_cache(None)
@@ -304,121 +305,223 @@
     return result.reshape(channels, length) / (2.0 * length)
 
 
-def hyena_kernel(short_out, post, conv, out_ref):
+def hyena_kernel(place_ref, short_out, post, conv, out_ref, other_ref, mine_ref):
     parts = [conv[g] for g in range(conv.shape[0])]
     here = parts[0] if len(parts) == 1 else jnp.concatenate(parts, axis=1)
-    out_ref[...] = short_out[...] + post[...] * here
-
-
-def hyena_stage(short_out, post, conv):
+    result = short_out[...] + post[...] * here
+    out_ref[...] = result
+    step, half = pl.program_id(0), pl.num_programs(0) // 2
+
+    @pl.when(step < half)
+    def _():
+        other_ref[...] = result
+
+    @pl.when(step >= half)
+    def _():
+        mine_ref[...] = result
+
+
+def hyena_stage(place, short_out, post, conv):
     length, width = short_out.shape
-    parts, _, group = conv.shape
+    _, _, group = conv.shape
     tile = max(group, 128)
-    wide = pl.BlockSpec((length, tile), lambda i: (0, i))
+    steps = width // tile
+    half = steps // 2
+
+    def col(i, place):
+        return lax.rem((1 - place[1]) * half + i, steps)
+
+    wide = pl.BlockSpec((length, tile), lambda i, place: (0, col(i, place)))
     return pl.pallas_call(
         hyena_kernel,
-        grid=(width // tile,),
-        in_specs=[
-            wide,
-            wide,
-            pl.BlockSpec((tile // group, length, group), lambda i: (i, 0, 0)),
+        grid_spec=pltpu.PrefetchScalarGridSpec(
+            num_scalar_prefetch=1,
+            grid=(steps,),
+            in_specs=[
+                wide,
+                wide,
+                pl.BlockSpec(
+                    (tile // group, length, group), lambda i, place: (col(i, place), 0, 0)
+                ),
+            ],
+            out_specs=[
+                wide,
+                pl.BlockSpec((length, tile), lambda i, place: (0, jnp.minimum(i, half - 1))),
+                pl.BlockSpec((length, tile), lambda i, place: (0, jnp.maximum(i - half, 0))),
+            ],
+        ),
+        out_shape=[
+            jax.ShapeDtypeStruct((length, width), F32),
+            jax.ShapeDtypeStruct((length, width // 2), F32),
+            jax.ShapeDtypeStruct((length, width // 2), F32),
         ],
-        out_specs=wide,
-        out_shape=jax.ShapeDtypeStruct((length, width), F32),
         name="hyena_stage",
-    )(short_out, post, conv)
-
-
-def attend_kernel(reach_ref, chip_ref, *refs):
-    steps = REACH + 2
-    q_ref = refs[0]
-    k_refs = refs[1 : 1 + steps]
-    v_refs = refs[1 + steps : 1 + 2 * steps]
-    out_ref, k_cat, v_cat, top, total, acc = refs[1 + 2 * steps :]
-    head, odd, tile = pl.program_id(0), pl.program_id(1), pl.program_id(2)
-    dim = q_ref.shape[2]
-    rows = q_ref.shape[1]
-    length = k_refs[0].shape[0]
-
-    @pl.when((odd == 0) & (tile == 0))
+    )(place, short_out, post, conv)
+
+
+def attend_kernel(reach_ref, place_ref, *refs, head, names):
+    count = len(names)
+    q_refs = refs[:2]
+    k_refs = dict(zip(names, refs[2 : 2 + count]))
+    v_refs = dict(zip(names, refs[2 + count : 2 + 2 * count]))
+    other_ref, mine_ref, k_cat, v_cat, top, total, acc = refs[2 + 2 * count :]
+    turn = pl.program_id(0)
+    core = place_ref[1]
+    odd = jnp.where(turn == 0, 1 - core, core)
+    length, dim = mine_ref.shape
+
+    def load(ref):
+        return ref[0] if len(ref.shape) == 3 else ref[...]
+
+    def ordered(refs):
+        first = core == 0
+        x = {name: load(ref) for name, ref in refs.items()}
+        yield x["far"]
+        yield jnp.where(first, x["near_mine"], x["near_other"])
+        yield jnp.where(first, x["near_other"], x["near_mine"])
+        yield jnp.where(first, x["mine"], x["other"])
+        yield jnp.where(first, x["other"], x["mine"])
+
+    @pl.when(turn == 0)
     def _():
-        for n in range(steps):
-            hi, lo = halves(k_refs[n][...])
-            k_cat[n] = jnp.concatenate([hi, hi, lo], axis=1)
-            hi, lo = halves(v_refs[n][...])
+        for n, k in enumerate(ordered(k_refs)):
+            hi, lo = halves(k.T)
+            k_cat[n] = jnp.concatenate([hi, hi, lo], axis=0)
+        for n, v in enumerate(ordered(v_refs)):
+            hi, lo = halves(v)
             v_cat[n] = jnp.concatenate([hi, lo], axis=1)
 
     scale = math.log2(math.e) / math.sqrt(dim)
-    q_hi, q_lo = halves(q_ref[0] * scale)
+    queries = jnp.where(turn == 0, q_refs[1][...], q_refs[0][...])
+    q_hi, q_lo = halves(queries * scale)
     q_cat = jnp.concatenate([q_hi, q_lo, q_hi], axis=1)
     reach = reach_ref[head]
-    block = 2 * chip_ref[0] + odd
-
-    def scores_of(slot):
-        return lax.dot_general(
-            q_cat, k_cat[slot], (((1,), (1,)), ((), ())), preferred_element_type=F32
-        )
-
-    def weigh(slot, weight):
+    block = 2 * place_ref[0] + odd
+    own = odd + REACH
+
+    def weigh(weight, values):
         w_hi, w_lo = halves(weight)
-        both = mm(w_hi, v_cat[slot])
-        return both[:, :dim] + both[:, dim:] + mm(w_lo, v_cat[slot][:, :dim])
-
-    own = odd + REACH
-    scores = scores_of(own)
-    row = tile * rows + lax.broadcasted_iota(jnp.int32, (rows, length), 0)
-    col = lax.broadcasted_iota(jnp.int32, (rows, length), 1)
-    scores = jnp.where(row >= col, scores, masked_low)
-    best = jnp.max(scores, axis=1, keepdims=True)
-    weight = jnp.exp2(scores - best)
-    top[...] = best
-    total[...] = jnp.sum(weight, axis=1, keepdims=True)
-    acc[...] = weigh(own, weight)
+        both = mm(w_hi, values)
+        return both[:, :dim] + both[:, dim:] + mm(w_lo, values[:, :dim])
+
+    tile = min(length, 256)
+    for start in range(0, length, tile):
+        rows, stop = pl.ds(start, tile), start + tile
+        scores = mm(q_cat[start:stop], k_cat[own, :, :stop])
+        row = start + lax.broadcasted_iota(jnp.int32, (tile, stop), 0)
+        col = lax.broadcasted_iota(jnp.int32, (tile, stop), 1)
+        scores = jnp.where(row >= col, scores, masked_low)
+        best = jnp.max(scores, axis=1, keepdims=True)
+        weight = jnp.exp2(scores - best)
+        top[rows, :] = best
+        total[rows, :] = jnp.sum(weight, axis=1, keepdims=True)
+        acc[rows, :] = weigh(weight, v_cat[own, :stop, :])
 
     for distance in range(1, REACH + 1):
 
         @pl.when((distance <= reach) & (block >= distance))
         def _():
             slot = own - distance
-            scores = scores_of(slot)
+            scores = mm(q_cat, k_cat[slot])
             old = top[...]
             best = jnp.maximum(old, jnp.max(scores, axis=1, keepdims=True))
             shrink = jnp.exp2(old - best)
             weight = jnp.exp2(scores - best)
             top[...] = best
             total[...] = total[...] * shrink + jnp.sum(weight, axis=1, keepdims=True)
-            acc[...] = acc[...] * shrink + weigh(slot, weight)
-
-    out_ref[0] = acc[...] / total[...]
-
-
-def attend_stage(reach, chip, queries, keys, values, first_head, heads):
-    blocks, length, _ = queries.shape
-    rows = min(length, 256)
+            acc[...] = acc[...] * shrink + weigh(weight, v_cat[slot])
+
+    result = acc[...] / total[...]
+
+    @pl.when(turn == 0)
+    def _():
+        other_ref[...] = result
+
+    @pl.when(turn == 1)
+    def _():
+        mine_ref[...] = result
+
+
+def attend_stage(reach, place, queries, keys, values, head):
+    length = queries[0].shape[0]
     steps = REACH + 2
-    key_spec = pl.BlockSpec((length, HEAD_DIM), lambda h, b, t, *_: (0, first_head + h))
-    value_spec = pl.BlockSpec((length, HEAD_DIM), lambda h, b, t, *_: (0, h))
+
+    def spec_of(x, lead):
+        if lead is not None:
+            return pl.BlockSpec((1, length, HEAD_DIM), lambda i, *_: (lead, 0, 0))
+        at = head if x.shape[1] > HEAD_DIM else 0
+        return pl.BlockSpec((length, HEAD_DIM), lambda i, *_: (0, at))
+
+    operands = [(q, None) for q in queries] + list(keys.values()) + list(values.values())
     return pl.pallas_call(
-        attend_kernel,
+        functools.partial(attend_kernel, head=head, names=tuple(keys)),
         grid_spec=pltpu.PrefetchScalarGridSpec(
             num_scalar_prefetch=2,
-            grid=(heads, blocks, length // rows),
-            in_specs=[pl.BlockSpec((1, rows, HEAD_DIM), lambda h, b, t, *_: (b, t, first_head + h))]
-            + [key_spec] * steps
-            + [value_spec] * steps,
-            out_specs=pl.BlockSpec((1, rows, HEAD_DIM), lambda h, b, t, *_: (b, t, h)),
+            grid=(2,),
+            in_specs=[spec_of(*x) for x in operands],
+            out_specs=[pl.BlockSpec((length, HEAD_DIM), lambda i, *_: (0, 0))] * 2,
             scratch_shapes=[
-                pltpu.VMEM((steps, length, 3 * HEAD_DIM), BF16),
+                pltpu.VMEM((steps, 3 * HEAD_DIM, length), BF16),
                 pltpu.VMEM((steps, length, 2 * HEAD_DIM), BF16),
-                pltpu.VMEM((rows, 1), F32),
-                pltpu.VMEM((rows, 1), F32),
-                pltpu.VMEM((rows, HEAD_DIM), F32),
+                pltpu.VMEM((length, 1), F32),
+                pltpu.VMEM((length, 1), F32),
+                pltpu.VMEM((length, HEAD_DIM), F32),
             ],
         ),
-        out_shape=jax.ShapeDtypeStruct((blocks, length, heads * HEAD_DIM), F32),
+        out_shape=[jax.ShapeDtypeStruct((length, HEAD_DIM), F32)] * 2,
         compiler_params=pltpu.CompilerParams(vmem_limit_bytes=VMEM_CAP),
         name="attend_stage",
-    )(reach, chip, queries, *keys, *values)
+    )(reach, place, *[x for x, _ in operands])
+
+
+def product_kernel(place_ref, *refs, count, added):
+    a_refs, w_refs = refs[:count], refs[count : 3 * count]
+    rest = refs[3 * count :]
+    out_ref, left = rest[-2:]
+
+    @pl.when(pl.program_id(0) == 0)
+    def _():
+        apart = place_ref[0] ^ place_ref[2]
+        for h in range(2):
+            pieces = [r[h] for r in a_refs]
+            bit = 1
+            while bit < count:
+                flip = (apart & bit) != 0
+                pieces = [jnp.where(flip, pieces[m ^ bit], pieces[m]) for m in range(count)]
+                bit *= 2
+            hi, lo = halves(jnp.concatenate(pieces, axis=1))
+            left[h] = jnp.concatenate([hi, lo, hi], axis=1)
+
+    out = None
+    for h in range(2):
+        hi, lo = halves(jnp.concatenate([r[...] for r in w_refs[h * count : (h + 1) * count]], axis=0))
+        here = mm(left[h], jnp.concatenate([hi, hi, lo], axis=0))
+        out = here if out is None else out + here
+    out_ref[...] = rest[0][...] + out if added else out
+
+
+def product_stage(place, pieces, weights, head, total):
+    count = len(pieces)
+    _, length, part = pieces[0].shape
+    width = weights[0].shape[1]
+    tile = min(width, 256)
+    a_spec = pl.BlockSpec((2, length, part), lambda i, place: (0, 0, 0))
+    w_spec = pl.BlockSpec((part, tile), lambda i, place: (head, i))
+    out_spec = pl.BlockSpec((length, tile), lambda i, place: (0, i))
+    extra = [] if total is None else [total]
+    return pl.pallas_call(
+        functools.partial(product_kernel, count=count, added=total is not None),
+        grid_spec=pltpu.PrefetchScalarGridSpec(
+            num_scalar_prefetch=1,
+            grid=(width // tile,),
+            in_specs=[a_spec] * count + [w_spec] * (2 * count) + [out_spec] * len(extra),
+            out_specs=out_spec,
+            scratch_shapes=[pltpu.VMEM((2, length, 3 * count * part), BF16)],
+        ),
+        out_shape=jax.ShapeDtypeStruct((length, width), F32),
+        compiler_params=pltpu.CompilerParams(vmem_limit_bytes=VMEM_CAP),
+        name="product_stage",
+    )(place, *pieces, *weights, *extra)
 
 
 def shards(
@@ -442,43 +545,65 @@
     chip, core = here // 2, here % 2
     half = width // 2
     heads_half = half // HEAD_DIM
-    chunks = math.gcd(CHUNKS, heads_half)
-    heads_chunk = heads_half // chunks
-    part = heads_chunk * HEAD_DIM
+    chips = parts // 2
+    planes = lax.axis_size("chan")
+    plane = lax.axis_index("chan")
+    place = jnp.stack([chip, core, plane]).astype(jnp.int32)
+
+    def send(x, pairs):
+        return lax.ppermute(x, "seq", pairs)
 
     def shift(x, by):
-        pairs = [(i, i + by) for i in range(parts) if i + by < parts]
-        return lax.ppermute(x, "seq", pairs)
+        return send(x, [(i, i + by) for i in range(parts) if i + by < parts])
 
     def swap(x):
-        return lax.ppermute(x, "seq", [(i, i ^ 1) for i in range(parts)])
-
-    def both_blocks(x):
+        return send(x, [(i, i ^ 1) for i in range(parts)])
+
+    def both(x):
         cols = x.shape[1] // 2
-        mine = lax.dynamic_slice_in_dim(x, core * cols, cols, 1)
-        other = swap(lax.dynamic_slice_in_dim(x, (1 - core) * cols, cols, 1))
-        even = jnp.where(core == 0, mine, other)
-        odd = jnp.where(core == 0, other, mine)
-        return jnp.stack([even, odd])
-
-    def window(pair):
-        behind = shift(pair, 2)
-        far = shift(pair[1], 4)
-        return [far, behind[0], behind[1], pair[0], pair[1]]
-
+        other = lax.dynamic_slice_in_dim(x, (1 - core) * cols, cols, 1)
+        other = swap(other)
+        return lax.dynamic_slice_in_dim(x, core * cols, cols, 1), other
+
+    def cut(x, head):
+        return x[:, head * HEAD_DIM : (head + 1) * HEAD_DIM]
+
+    def own_of(mine, other):
+        return {"mine": (mine, None), "other": (other, None)}
+
+    def first_window(mine, other):
+        near_mine = shift(cut(mine, 0), 2)
+        near_other = shift(cut(other, 0), 2)
+        far = shift(jnp.where(core == 0, cut(other, 0), cut(mine, 0)), 4)
+        near = {"far": (far, None), "near_mine": (near_mine, None), "near_other": (near_other, None)}
+        return near | own_of(mine, other)
+
+    def later_windows(mine, other, heads):
+        near = jnp.stack([cut(x, head) for head in heads for x in (mine, other)])
+        far = jnp.stack([jnp.where(core == 0, cut(other, h), cut(mine, h)) for h in heads])
+        near = shift(near, 2)
+        far = shift(far, 4)
+        return [
+            {"far": (far, at), "near_mine": (near, 2 * at), "near_other": (near, 2 * at + 1)}
+            | own_of(mine, other)
+            for at in range(len(heads))
+        ]
+
+    tail = short_gate_pre[length - taps :] * stream[length - taps :]
+    halo = shift(tail, 1)
     filt = long_filter.reshape(parts, group, length)
     filt = lax.all_to_all(filt, "seq", split_axis=0, concat_axis=0, tiled=True)
-
-    tail = short_gate_pre[length - taps :] * stream[length - taps :]
-    halo = shift(tail, 1)
     short_out, long_in = short_stage(
         halo, stream, short_gate_pre, short_gate_post, short_filter, long_gate_pre, parts
     )
     signal = lax.all_to_all(long_in, "seq", split_axis=0, concat_axis=0, tiled=True)
 
+    queries = both(queries)
+    key_mine, key_other = both(key_vectors)
     whole = parts * length
     if group == 128 and whole <= 6144:
         spec = filter_stage(filt, whole)
+        key_mine, key_other, spec = lax.optimization_barrier((key_mine, key_other, spec))
         conv = signal_stage(signal.reshape(whole // INNER, INNER, group), spec)
         conv = conv.reshape(parts, length, group)
     else:
@@ -486,43 +611,34 @@
             signal.reshape(whole, group).T, filt.transpose(1, 0, 2).reshape(group, whole)
         ).T.reshape(parts, length, group)
     back = lax.all_to_all(conv, "seq", split_axis=0, concat_axis=0, tiled=True)
-    hyena_out = hyena_stage(short_out, long_gate_post, back)
-
-    query_pair = both_blocks(queries)
-    keys = window(both_blocks(key_vectors))
-    groups = [list(range(c, parts, 2)) for c in range(2)]
-    weight = lax.all_gather(out_weight, "seq", axis=0, axis_index_groups=groups)
+    hyena_out, value_other, value_mine = hyena_stage(place, short_out, long_gate_post, back)
+    value_other = swap(value_other)
 
     reach = lax.dynamic_slice_in_dim(head_reach, core * heads_half, heads_half)
-    chip_at = chip[None].astype(jnp.int32)
+    weights = None
     mixed = None
-    for n in range(chunks):
-        cols = jnp.concatenate(
-            [hyena_out[:, n * part : (n + 1) * part], hyena_out[:, half + n * part : half + (n + 1) * part]],
-            axis=1,
-        )
-        values = window(both_blocks(cols))
-        attended = attend_stage(
-            lax.dynamic_slice_in_dim(reach, n * heads_chunk, heads_chunk),
-            chip_at,
-            query_pair,
-            keys,
-            values,
-            n * heads_chunk,
-            heads_chunk,
-        ).reshape(2 * length, part)
-        spread = lax.all_gather(attended, "chan", axis=0)
-        product = lax.dot_general(
-            spread,
-            weight[:, n * part : (n + 1) * part, :],
-            (((0, 2), (0, 1)), ((), ())),
-            precision=lax.Precision.HIGH,
-            preferred_element_type=F32,
-        )
-        mixed = product if mixed is None else mixed + product
-    mixed = mixed.reshape(2, length, width)
-    own = lax.dynamic_index_in_dim(mixed, core, 0, keepdims=False)
-    mixed = own + swap(lax.dynamic_index_in_dim(mixed, 1 - core, 0, keepdims=False))
+    key_windows = [first_window(key_mine, key_other)]
+    for n in range(1, heads_half):
+        key_windows += later_windows(key_mine, key_other, [n])
+    for n in range(heads_half):
+        keys = key_windows[n]
+        if n == 0:
+            values = first_window(value_mine, value_other)
+        else:
+            values = later_windows(value_mine, value_other, [n])[0]
+        other, mine = attend_stage(reach, place, queries, keys, values, n)
+        if n == 0:
+            out_weight, mine = lax.optimization_barrier((out_weight, mine))
+            weights = [out_weight]
+            for m in range(1, chips):
+                weights.append(send(out_weight, [(i, i ^ (2 * m)) for i in range(parts)]))
+            for m in range(chips):
+                weights.append(swap(weights[m]))
+        piece = jnp.stack([mine, swap(other)])
+        pieces = [piece]
+        for m in range(1, planes):
+            pieces.append(lax.ppermute(piece, "chan", [(i, i ^ m) for i in range(planes)]))
+        mixed = product_stage(place, pieces, weights, n, mixed)
     return (hyena_out, mixed)
 
 

time: 710 us -> 789 us (1.11)
  the two profiles are of different devices: /device:TPU:0 before, /device:TPU:4 now
where the time goes in v2:
time: 789 us; the launch traced here: 781 us
  waiting for transfers between devices  422 us (53%)
  Pallas kernels  195 us (25%)
  starting transfers between devices  137 us (17%)
  local copies, waits for them, and re-layouts  13.3 us (2%)
  other arithmetic  12.3 us (2%)
    ppermute x33, waiting for transfers between devices, send(): return lax.ppermute(x, 'seq', pairs)  194 us
    ppermute x12, waiting for transfers between devices, shards(): lax.ppermute(piece, 'chan', [(i, i ^ m) for i in range(planes)])  182 us
    ppermute x12, starting transfers between devices, shards(): lax.ppermute(piece, 'chan', [(i, i ^ m) for i in range(planes)])  79.3 us
    pallas_call x4, Pallas kernels, attend_stage(): pl.pallas_call(functools.partial(attend_kernel, head=head, names=tuple(ke...  74.6 us
    pallas_call x4, Pallas kernels, product_stage(): pl.pallas_call(functools.partial(product_kernel, count=count, added=total...  43.5 us
    ppermute x33, starting transfers between devices, send(): return lax.ppermute(x, 'seq', pairs)  42.8 us
    pallas_call x1, Pallas kernels, signal_stage(): pl.pallas_call(signal_kernel, in_specs=[vmem_spec()] * 8 + [smem_spec()]...  34.8 us
    all_to_all x1, waiting for transfers between devices, shards(): back = lax.all_to_all(conv, 'seq', split_axis=0, concat_axis=0, tiled=True)  31.8 us
  transfers between devices with their start and end apart: 48, of which 19 were waited for; matrix products, arithmetic and copies ran while one was open for 2% of the time, Pallas kernels for 19%

profile of v2, /device:TPU:4, one launch (start us, length us, event | category | flops | bytes accessed | tf_op | source)
XLA Modules:
  0.0 781.0 jit_solution(696368409826275602)
XLA Ops:
  0.6 4.2 all-to-all-start.1
  6.1 2.0 collective-permute-start
  8.2 38.7 %collective-permute-done.halo = f32[128,1024]{1,0:T(8,128)S(1)} collective-permute-done((f32[128,1024]{1,0:T(8,128)S(1)}, f32[128,1024]{1,0:T(8,128)S(1)}, u32[]{:S(2)}, u32[]{:S(2)}) %collective-permute-start) | collective-permute-done | bytes 524320 | tf_op jit(solution)/shard_map/ppermute | solution.py:554
  47.7 14.2 %short_stage.1 = (f32[768,1024]{1,0:T(8,128)}, f32[8,768,128]{2,1,0:T(8,128)}) custom-call(bf16[256,256]{1,0:T(8,128)(2,1)} %constant.71.clone.f_hi, bf16[256,256]{1,0:T(8,128)(2,1)} %constant.72.clone.f_lo, bf16[128,256]{1,0:T(8,128)(2,1)} %constant.73.clone.g_hi, bf16[128,256]{1,0:T(8,128)(2,1)} %constant.74.clone.g_lo, f32[128,1024]{1,0:T(8,128)} %copy-done.25, ...), custom_call_target="tpu_custom_call" | custom-call | tf_op jit(solution)/shard_map/short_stage/pallas_call | solution.py:92
  61.9 1.8 copy-done.8
  63.6 4.4 all-to-all-start
  68.1 2.2 constant_dynamic-slice_fusion.2
  70.3 19.0 %filter_stage.1.spec = f32[48,256,128]{2,1,0:T(8,128)} custom-call(bf16[768,384]{1,0:T(8,128)(2,1)} %constant.75.clone.w_hi, bf16[768,384]{1,0:T(8,128)(2,1)} %constant.76.clone.w_lo, bf16[256,256]{1,0:T(8,128)(2,1)} %constant.77.clone.b_hi, bf16[256,256]{1,0:T(8,128)(2,1)} %constant.78.clone.b_lo, f32[16,48]{1,0:T(8,128)} %constant.79.clone.t_re, ...), custom_call_target="tpu_custom_call" | custom-call | tf_op jit(solution)/shard_map/filter_stage/pallas_call | solution.py:244
  89.3 14.1 %all-to-all-done = f32[8,768,128]{2,1,0:T(8,128)} async-done(((f32[8,768,128]{2,1,0:T(8,128)}), f32[8,768,128]{2,1,0:T(8,128)}, u32[]{:S(2)}, u32[]{:S(2)}) %all-to-all-start) | async-done | bytes 3145760 | tf_op jit(solution)/shard_map/all_to_all | solution.py:599
  103.4 34.8 %signal_stage.1 = f32[48,128,128]{2,1,0:T(8,128)} custom-call(bf16[768,384]{1,0:T(8,128)(2,1)} %constant.75.clone.w_hi, bf16[768,384]{1,0:T(8,128)(2,1)} %constant.76.clone.w_lo, bf16[384,768]{1,0:T(8,128)(2,1)} %constant.81.clone.v_hi, bf16[384,768]{1,0:T(8,128)(2,1)} %constant.82.clone.v_lo, bf16[256,256]{1,0:T(8,128)(2,1)} %constant.77.clone.b_hi, ...), custom_call_target="tpu_custom_call" | custom-call | tf_op jit(solution)/shard_map/signal_stage/pallas_call | solution.py:261
  138.2 5.8 all-to-all-start.2
  144.0 3.9 constant_dynamic-slice_fusion
  148.7 31.8 %all-to-all-done.2.conv = f32[8,768,128]{2,1,0:T(8,128)} async-done(((f32[8,768,128]{2,1,0:T(8,128)}), f32[8,768,128]{2,1,0:T(8,128)}, u32[]{:S(2)}, u32[]{:S(2)}) %all-to-all-start.2) | async-done | bytes 3145760 | tf_op jit(solution)/shard_map/all_to_all | solution.py:613
  180.5 9.2 %hyena_stage.1 = (f32[768,1024]{1,0:T(8,128)}, f32[768,512]{1,0:T(8,128)}, f32[768,512]{1,0:T(8,128)}) custom-call(s32[3]{0:T(128)} %pad_add_fusion.place_ref, f32[768,1024]{1,0:T(8,128)} %get-tuple-element.20.short_out, f32[768,1024]{1,0:T(8,128)} %post.3, f32[8,768,128]{2,1,0:T(8,128)} %all-to-all-done.2.conv), custom_call_target="tpu_custom_call" | custom-call | tf_op jit(solution)/shard_map/hyena_stage/pallas_call | solution.py:335
  190.2 1.4 collective-permute-start.3
  194.3 2.5 collective-permute-start.26
  196.9 24.2 %collective-permute-done.3.refs_2_ = f32[1,768,128]{2,1,0:T(8,128)S(1)} collective-permute-done((f32[1,768,128]{2,1,0:T(8,128)S(1)}, f32[1,768,128]{2,1,0:T(8,128)S(1)}, u32[]{:S(2)}, u32[]{:S(2)}) %collective-permute-start.3) | collective-permute-done | bytes 393248 | tf_op jit(solution)/shard_map/ppermute | solution.py:554
  221.1 1.9 collective-permute-start.4
  223.0 23.4 %collective-permute-done.25.refs_2_ = f32[1,768,128]{2,1,0:T(8,128)S(1)} collective-permute-done((f32[1,768,128]{2,1,0:T(8,128)S(1)}, f32[1,768,128]{2,1,0:T(8,128)S(1)}, u32[]{:S(2)}, u32[]{:S(2)}) %collective-permute-start.25) | collective-permute-done | bytes 393248 | tf_op jit(solution)/shard_map/ppermute | solution.py:554
  247.6 7.1 collective-permute-done.12.refs_2_
  254.8 1.9 collective-permute-start.14
  256.7 1.9 collective-permute-start.13
  258.7 2.7 slice_bitcast_fusion.3
  261.3 18.2 %collective-permute-done.33.refs_2_ = f32[1,768,128]{2,1,0:T(8,128)S(1)} collective-permute-done((f32[1,768,128]{2,1,0:T(8,128)S(1)}, f32[1,768,128]{2,1,0:T(8,128)S(1)}, u32[]{:S(2)}, u32[]{:S(2)}) %collective-permute-start.33) | collective-permute-done | bytes 393248 | tf_op jit(solution)/shard_map/ppermute | solution.py:554
  282.2 1.9 collective-permute-start.17
  285.1 1.9 collective-permute-start.16
  287.0 1.9 collective-permute-start.28
  289.9 37.2 %collective-permute-done.6.refs_7_ = f32[1,768,128]{2,1,0:T(8,128)S(1)} collective-permute-done((f32[1,768,128]{2,1,0:T(8,128)S(1)}, f32[1,768,128]{2,1,0:T(8,128)S(1)}, u32[]{:S(2)}, u32[]{:S(2)}) %collective-permute-start.6) | collective-permute-done | bytes 393248 | tf_op jit(solution)/shard_map/ppermute | solution.py:554
  327.2 1.9 collective-permute-start.7
  330.0 21.1 %collective-permute-done.15.refs_7_ = f32[768,128]{1,0:T(8,128)S(1)} collective-permute-done((f32[768,128]{1,0:T(8,128)S(1)}, f32[768,128]{1,0:T(8,128)S(1)}, u32[]{:S(2)}, u32[]{:S(2)}) %collective-permute-start.15) | collective-permute-done | bytes 393248 | tf_op jit(solution)/shard_map/ppermute | solution.py:554
  351.1 1.9 collective-permute-start.34
  356.1 2.1 collective-permute-start.36
  358.9 14.5 %attend_stage.5 = (f32[768,128]{1,0:T(8,128)}, f32[768,128]{1,0:T(8,128)}) custom-call(s32[4]{0:T(128)} %dynamic_slice.17.reach_ref, s32[3]{0:T(128)} %pad_add_fusion.place_ref, f32[768,512]{1,0:T(8,128)} %get-tuple-element.47.refs_0_, f32[768,512]{1,0:T(8,128)} %collective-permute-done.2.refs_1_, f32[768,128]{1,0:T(8,128)} %copy-done.26, ...), custom_call_target="tpu_custom_call" | custom-call | tf_op jit(solution)/shard_map/attend_stage/pallas_call | solution.py:456
  373.4 24.3 %collective-permute-done.27.refs_7_ = f32[1,768,128]{2,1,0:T(8,128)} collective-permute-done((f32[1,768,128]{2,1,0:T(8,128)}, f32[1,768,128]{2,1,0:T(8,128)}, u32[]{:S(2)}, u32[]{:S(2)}) %collective-permute-start.27) | collective-permute-done | bytes 393248 | tf_op jit(solution)/shard_map/ppermute | solution.py:554
  397.7 1.7 collective-permute-start.35
  399.5 19.8 %attend_stage.6 = (f32[768,128]{1,0:T(8,128)}, f32[768,128]{1,0:T(8,128)}) custom-call(s32[4]{0:T(128)} %dynamic_slice.17.reach_ref, s32[3]{0:T(128)} %pad_add_fusion.place_ref, f32[768,512]{1,0:T(8,128)} %get-tuple-element.47.refs_0_, f32[768,512]{1,0:T(8,128)} %collective-permute-done.2.refs_1_, f32[1,768,128]{2,1,0:T(8,128)} %copy-done.37, ...), custom_call_target="tpu_custom_call" | custom-call | tf_op jit(solution)/shard_map/attend_stage/pallas_call | solution.py:456
  419.4 25.6 %attend_stage.4 = (f32[768,128]{1,0:T(8,128)}, f32[768,128]{1,0:T(8,128)}) custom-call(s32[4]{0:T(128)} %dynamic_slice.17.reach_ref, s32[3]{0:T(128)} %pad_add_fusion.place_ref, f32[768,512]{1,0:T(8,128)} %get-tuple-element.47.refs_0_, f32[768,512]{1,0:T(8,128)} %collective-permute-done.2.refs_1_, f32[1,768,128]{2,1,0:T(8,128)} %copy-done.36, ...), custom_call_target="tpu_custom_call" | custom-call | tf_op jit(solution)/shard_map/attend_stage/pallas_call | solution.py:456
  445.5 3.4 collective-permute-start.18
  448.9 14.6 %attend_stage.7 = (f32[768,128]{1,0:T(8,128)}, f32[768,128]{1,0:T(8,128)}) custom-call(s32[4]{0:T(128)} %dynamic_slice.17.reach_ref, s32[3]{0:T(128)} %pad_add_fusion.place_ref, f32[768,512]{1,0:T(8,128)} %get-tuple-element.47.refs_0_, f32[768,512]{1,0:T(8,128)} %collective-permute-done.2.refs_1_, f32[1,768,128]{2,1,0:T(8,128)} %copy-done.35, ...), custom_call_target="tpu_custom_call" | custom-call | tf_op jit(solution)/shard_map/attend_stage/pallas_call | solution.py:456
  463.6 4.8 collective-permute-start.37
  469.6 4.5 collective-permute-start.44
  474.1 9.3 %collective-permute-start.43 = (f32[2,768,128]{2,1,0:T(8,128)S(1)}, f32[2,768,128]{2,1,0:T(8,128)S(1)}, u32[]{:S(2)}, u32[]{:S(2)}) collective-permute-start(f32[2,768,128]{2,1,0:T(8,128)S(1)} %pad_maximum_fusion.9.refs_0_), channel_id=1, source_target_pairs={{0,2},{1,3},{2,0},{3,1},{4,6},{5,7},{6,4},{7,5},{8,10},{9,11},{10,... | collective-permute-start | bytes 2359304 | tf_op jit(solution)/shard_map/ppermute | solution.py:640
  483.4 9.2 %collective-permute-done.44.refs_3_ = f32[2,768,128]{2,1,0:T(8,128)S(1)} collective-permute-done((f32[2,768,128]{2,1,0:T(8,128)S(1)}, f32[2,768,128]{2,1,0:T(8,128)S(1)}, u32[]{:S(2)}, u32[]{:S(2)}) %collective-permute-start.44) | collective-permute-done | bytes 786464 | tf_op jit(solution)/shard_map/ppermute | solution.py:640
  492.6 34.2 %collective-permute-start.42 = (f32[2,768,128]{2,1,0:T(8,128)S(1)}, f32[2,768,128]{2,1,0:T(8,128)S(1)}, u32[]{:S(2)}, u32[]{:S(2)}) collective-permute-start(f32[2,768,128]{2,1,0:T(8,128)S(1)} %pad_maximum_fusion.9.refs_0_), channel_id=1, source_target_pairs={{0,1},{1,0},{2,3},{3,2},{4,5},{5,4},{6,7},{7,6},{8,9},{9,8},{10,11... | collective-permute-start | bytes 2359304 | tf_op jit(solution)/shard_map/ppermute | solution.py:640
  528.0 15.0 %collective-permute-done.43.refs_2_ = f32[2,768,128]{2,1,0:T(8,128)S(1)} collective-permute-done((f32[2,768,128]{2,1,0:T(8,128)S(1)}, f32[2,768,128]{2,1,0:T(8,128)S(1)}, u32[]{:S(2)}, u32[]{:S(2)}) %collective-permute-start.43) | collective-permute-done | bytes 786464 | tf_op jit(solution)/shard_map/ppermute | solution.py:640
  543.0 3.5 collective-permute-start.32
  546.6 30.0 %collective-permute-done.42.refs_1_ = f32[2,768,128]{2,1,0:T(8,128)S(1)} collective-permute-done((f32[2,768,128]{2,1,0:T(8,128)S(1)}, f32[2,768,128]{2,1,0:T(8,128)S(1)}, u32[]{:S(2)}, u32[]{:S(2)}) %collective-permute-start.42) | collective-permute-done | bytes 786464 | tf_op jit(solution)/shard_map/ppermute | solution.py:640
  576.6 3.5 collective-permute-start.40
  581.1 16.8 %collective-permute-done.40.refs_3_ = f32[2,768,128]{2,1,0:T(8,128)S(1)} collective-permute-done((f32[2,768,128]{2,1,0:T(8,128)S(1)}, f32[2,768,128]{2,1,0:T(8,128)S(1)}, u32[]{:S(2)}, u32[]{:S(2)}) %collective-permute-start.40) | collective-permute-done | bytes 786464 | tf_op jit(solution)/shard_map/ppermute | solution.py:640
  598.0 16.6 %collective-permute-start.39 = (f32[2,768,128]{2,1,0:T(8,128)S(1)}, f32[2,768,128]{2,1,0:T(8,128)S(1)}, u32[]{:S(2)}, u32[]{:S(2)}) collective-permute-start(f32[2,768,128]{2,1,0:T(8,128)S(1)} %pad_maximum_fusion.8.refs_0_), channel_id=1, source_target_pairs={{0,2},{1,3},{2,0},{3,1},{4,6},{5,7},{6,4},{7,5},{8,10},{9,11},{10,... | collective-permute-start | bytes 2359304 | tf_op jit(solution)/shard_map/ppermute | solution.py:640
  614.5 33.7 %collective-permute-done.39.refs_2_ = f32[2,768,128]{2,1,0:T(8,128)S(1)} collective-permute-done((f32[2,768,128]{2,1,0:T(8,128)S(1)}, f32[2,768,128]{2,1,0:T(8,128)S(1)}, u32[]{:S(2)}, u32[]{:S(2)}) %collective-permute-start.39) | collective-permute-done | bytes 786464 | tf_op jit(solution)/shard_map/ppermute | solution.py:640
  650.1 16.2 %collective-permute-done.38.refs_1_ = f32[2,768,128]{2,1,0:T(8,128)S(1)} collective-permute-done((f32[2,768,128]{2,1,0:T(8,128)S(1)}, f32[2,768,128]{2,1,0:T(8,128)S(1)}, u32[]{:S(2)}, u32[]{:S(2)}) %collective-permute-start.38) | collective-permute-done | bytes 786464 | tf_op jit(solution)/shard_map/ppermute | solution.py:640
  666.3 1.4 collective-permute-start.31
  667.8 1.7 collective-permute-start.30
  670.9 1.3 copy-done.7
  672.2 1.4 collective-permute-start.10
  673.6 1.7 collective-permute-start.9
  675.4 10.6 %product_stage.4.refs_12_ = f32[768,1024]{1,0:T(8,128)} custom-call(s32[3]{0:T(128)} %pad_add_fusion.place_ref, f32[2,768,128]{2,1,0:T(8,128)} %copy-done.9, f32[2,768,128]{2,1,0:T(8,128)} %copy-done.18, f32[2,768,128]{2,1,0:T(8,128)} %copy-done.17, f32[2,768,128]{2,1,0:T(8,128)} %copy-done.16, f32[512,1024]{1,0:T(8,128)} %refs_4_.3, ...), custom_call_target="tpu_custom_call" | custom-call | tf_op jit(solution)/shard_map/product_stage/pallas_call | solution.py:512
  686.0 11.0 %product_stage.5.refs_12_ = f32[768,1024]{1,0:T(8,128)} custom-call(s32[3]{0:T(128)} %pad_add_fusion.place_ref, f32[2,768,128]{2,1,0:T(8,128)} %copy-done.11, f32[2,768,128]{2,1,0:T(8,128)} %copy-done.23, f32[2,768,128]{2,1,0:T(8,128)} %copy-done.21, f32[2,768,128]{2,1,0:T(8,128)} %copy-done.19, f32[512,1024]{1,0:T(8,128)} %refs_4_.3, ...), custom_call_target="tpu_custom_call" | custom-call | tf_op jit(solution)/shard_map/product_stage/pallas_call | solution.py:512
  697.0 7.3 collective-permute-done.31.refs_2_
  704.3 17.0 %collective-permute-done.30.refs_1_ = f32[2,768,128]{2,1,0:T(8,128)} collective-permute-done((f32[2,768,128]{2,1,0:T(8,128)S(1)}, f32[2,768,128]{2,1,0:T(8,128)}, u32[]{:S(2)}, u32[]{:S(2)}) %collective-permute-start.30) | collective-permute-done | bytes 786464 | tf_op jit(solution)/shard_map/ppermute | solution.py:640
  721.4 11.0 %product_stage.6.refs_12_ = f32[768,1024]{1,0:T(8,128)} custom-call(s32[3]{0:T(128)} %pad_add_fusion.place_ref, f32[2,768,128]{2,1,0:T(8,128)} %copy-done.10, f32[2,768,128]{2,1,0:T(8,128)} %collective-permute-done.30.refs_1_, f32[2,768,128]{2,1,0:T(8,128)} %copy-done.24, f32[2,768,128]{2,1,0:T(8,128)} %collective-permute-done.32.refs_3_, ...), custom_call_target="tpu_custom_call" | custom-call | tf_op jit(solution)/shard_map/product_stage/pallas_call | solution.py:512
  732.4 36.4 %collective-permute-done.10.refs_2_ = f32[2,768,128]{2,1,0:T(8,128)S(1)} collective-permute-done((f32[2,768,128]{2,1,0:T(8,128)}, f32[2,768,128]{2,1,0:T(8,128)S(1)}, u32[]{:S(2)}, u32[]{:S(2)}) %collective-permute-start.10) | collective-permute-done | bytes 786464 | tf_op jit(solution)/shard_map/ppermute | solution.py:640
  769.6 10.9 %product_stage.7 = f32[768,1024]{1,0:T(8,128)} custom-call(s32[3]{0:T(128)} %pad_add_fusion.place_ref, f32[2,768,128]{2,1,0:T(8,128)} %pad_maximum_fusion.2.refs_0_, f32[2,768,128]{2,1,0:T(8,128)} %collective-permute-done.9.refs_1_, f32[2,768,128]{2,1,0:T(8,128)} %copy-done.22, f32[2,768,128]{2,1,0:T(8,128)} %copy-done.20, f32[512,1024]{1,0:T(8,128)} %refs_4_.3, ...), custom_call_target="tpu_custom_call" | custom-call | tf_op jit(solution)/shard_map/product_stage/pallas_call | solution.py:512
  (141 shorter events, 24.6 us)
Async XLA Ops:
  0.6 61.2 %all-to-all-start.1 = ((f32[8,128,768]{2,1,0:T(8,128)}), f32[8,128,768]{2,1,0:T(8,128)S(1)}, u32[]{:S(2)}, u32[]{:S(2)}) async-start(f32[8,128,768]{2,1,0:T(8,128)} %bitcast.51), calls=%async_computation.1 | async-start | bytes 6291456 | tf_op jit(solution)/shard_map/all_to_all | solution.py:595
  6.1 40.7 %collective-permute-start = (f32[128,1024]{1,0:T(8,128)S(1)}, f32[128,1024]{1,0:T(8,128)S(1)}, u32[]{:S(2)}, u32[]{:S(2)}) collective-permute-start(f32[128,1024]{1,0:T(8,128)S(1)} %slice_multiply_fusion), channel_id=1, source_target_pairs={{0,4},{4,8},{8,12},{12,16},{16,20},{20,24},{24,28},{1,5},{5,9},{9,... | collective-permute-start | bytes 1572872 | tf_op jit(solution)/shard_map/ppermute | solution.py:554
  63.6 39.8 %all-to-all-start = ((f32[8,768,128]{2,1,0:T(8,128)}), f32[8,768,128]{2,1,0:T(8,128)}, u32[]{:S(2)}, u32[]{:S(2)}) async-start(f32[8,768,128]{2,1,0:T(8,128)} %get-tuple-element.21), calls=%async_computation | async-start | bytes 6291456 | tf_op jit(solution)/shard_map/all_to_all | solution.py:599
  70.2 119.5 %copy-start = (f32[768,512]{1,0:T(8,128)}, f32[768,512]{1,0:T(8,128)S(1)}, u32[]{:S(2)}) copy-start(f32[768,512]{1,0:T(8,128)S(1)} %get-tuple-element.25.refs_5_) | copy-start | bytes 4718596
  70.3 19.1 %collective-permute-start.1 = (f32[768,512]{1,0:T(8,128)S(1)}, f32[768,512]{1,0:T(8,128)S(1)}, u32[]{:S(2)}, u32[]{:S(2)}) collective-permute-start(f32[768,512]{1,0:T(8,128)S(1)} %get-tuple-element.48), channel_id=1, source_target_pairs={{0,4},{4,0},{8,12},{12,8},{16,20},{20,16},{24,28},{28,24},{1,5},{5... | collective-permute-start | bytes 4718600 | tf_op jit(solution)/shard_map/ppermute | solution.py:554
  89.3 100.4 %copy-start.1 = (f32[768,512]{1,0:T(8,128)}, f32[768,512]{1,0:T(8,128)S(1)}, u32[]{:S(2)}) copy-start(f32[768,512]{1,0:T(8,128)S(1)} %collective-permute-done.1.refs_6_) | copy-start | bytes 4718596
  138.2 42.3 %all-to-all-start.2 = ((f32[8,768,128]{2,1,0:T(8,128)}), f32[8,768,128]{2,1,0:T(8,128)}, u32[]{:S(2)}, u32[]{:S(2)}) async-start(f32[8,768,128]{2,1,0:T(8,128)} %bitcast.50), calls=%async_computation.2 | async-start | bytes 6291456 | tf_op jit(solution)/shard_map/all_to_all | solution.py:613
  147.9 46.3 %collective-permute-start.2 = (f32[768,512]{1,0:T(8,128)}, f32[768,512]{1,0:T(8,128)}, u32[]{:S(2)}, u32[]{:S(2)}) collective-permute-start(f32[768,512]{1,0:T(8,128)} %get-tuple-element.46), channel_id=1, source_target_pairs={{0,4},{4,0},{8,12},{12,8},{16,20},{20,16},{24,28},{28,24},{1,5},{5... | collective-permute-start | bytes 4718600 | tf_op jit(solution)/shard_map/ppermute | solution.py:554
  189.7 67.0 %collective-permute-start.5 = (f32[768,512]{1,0:T(8,128)}, f32[768,512]{1,0:T(8,128)}, u32[]{:S(2)}, u32[]{:S(2)}) collective-permute-start(f32[768,512]{1,0:T(8,128)} %get-tuple-element.26), channel_id=1, source_target_pairs={{0,4},{4,0},{8,12},{12,8},{16,20},{20,16},{24,28},{28,24},{1,5},{5... | collective-permute-start | bytes 4718600 | tf_op jit(solution)/shard_map/ppermute | solution.py:554
  190.2 68.5 %copy-start.2 = (f32[768,512]{1,0:T(8,128)S(1)}, f32[768,512]{1,0:T(8,128)}, u32[]{:S(2)}) copy-start(f32[768,512]{1,0:T(8,128)} %get-tuple-element.27.refs_10_) | copy-start | bytes 4718596
  190.2 30.9 %collective-permute-start.3 = (f32[1,768,128]{2,1,0:T(8,128)S(1)}, f32[1,768,128]{2,1,0:T(8,128)S(1)}, u32[]{:S(2)}, u32[]{:S(2)}) collective-permute-start(f32[1,768,128]{2,1,0:T(8,128)S(1)} %get-tuple-element.65), channel_id=1, source_target_pairs={{0,16},{4,20},{8,24},{12,28},{1,17},{5,21},{9,25},{13,29},{2,18},{... | collective-permute-start | bytes 1179656 | tf_op jit(solution)/shard_map/ppermute | solution.py:554
  191.6 54.7 %collective-permute-start.25 = (f32[1,768,128]{2,1,0:T(8,128)S(1)}, f32[1,768,128]{2,1,0:T(8,128)S(1)}, u32[]{:S(2)}, u32[]{:S(2)}) collective-permute-start(f32[1,768,128]{2,1,0:T(8,128)S(1)} %get-tuple-element.66), channel_id=1, source_target_pairs={{0,16},{4,20},{8,24},{12,28},{1,17},{5,21},{9,25},{13,29},{2,18},{... | collective-permute-start | bytes 1179656 | tf_op jit(solution)/shard_map/ppermute | solution.py:554
  192.9 61.8 %collective-permute-start.12 = (f32[768,128]{1,0:T(8,128)S(1)}, f32[768,128]{1,0:T(8,128)S(1)}, u32[]{:S(2)}, u32[]{:S(2)}) collective-permute-start(f32[768,128]{1,0:T(8,128)S(1)} %get-tuple-element.67), channel_id=1, source_target_pairs={{0,16},{4,20},{8,24},{12,28},{1,17},{5,21},{9,25},{13,29},{2,18},{... | collective-permute-start | bytes 1179656 | tf_op jit(solution)/shard_map/ppermute | solution.py:554
  194.3 90.8 %collective-permute-start.26 = (f32[2,768,128]{2,1,0:T(8,128)S(1)}, f32[2,768,128]{2,1,0:T(8,128)S(1)}, u32[]{:S(2)}, u32[]{:S(2)}) collective-permute-start(f32[2,768,128]{2,1,0:T(8,128)S(1)} %pad_maximum_fusion.3), channel_id=1, source_target_pairs={{0,8},{4,12},{8,16},{12,20},{16,24},{20,28},{1,9},{5,13},{9,17},{1... | collective-permute-start | bytes 2359304 | tf_op jit(solution)/shard_map/ppermute | solution.py:554
  221.1 65.9 %collective-permute-start.4 = (f32[2,768,128]{2,1,0:T(8,128)S(1)}, f32[2,768,128]{2,1,0:T(8,128)S(1)}, u32[]{:S(2)}, u32[]{:S(2)}) collective-permute-start(f32[2,768,128]{2,1,0:T(8,128)S(1)} %pad_maximum_fusion), channel_id=1, source_target_pairs={{0,8},{4,12},{8,16},{12,20},{16,24},{20,28},{1,9},{5,13},{9,17},{1... | collective-permute-start | bytes 2359304 | tf_op jit(solution)/shard_map/ppermute | solution.py:554
  246.3 33.2 %collective-permute-start.33 = (f32[1,768,128]{2,1,0:T(8,128)S(1)}, f32[1,768,128]{2,1,0:T(8,128)S(1)}, u32[]{:S(2)}, u32[]{:S(2)}) collective-permute-start(f32[1,768,128]{2,1,0:T(8,128)S(1)} %get-tuple-element.68), channel_id=1, source_target_pairs={{0,16},{4,20},{8,24},{12,28},{1,17},{5,21},{9,25},{13,29},{2,18},{... | collective-permute-start | bytes 1179656 | tf_op jit(solution)/shard_map/ppermute | solution.py:554
  254.8 26.1 %collective-permute-start.14 = (f32[768,128]{1,0:T(8,128)S(1)}, f32[768,128]{1,0:T(8,128)S(1)}, u32[]{:S(2)}, u32[]{:S(2)}) collective-permute-start(f32[768,128]{1,0:T(8,128)S(1)} %get-tuple-element.72), channel_id=1, source_target_pairs={{0,8},{4,12},{8,16},{12,20},{16,24},{20,28},{1,9},{5,13},{9,17},{1... | collective-permute-start | bytes 1179656 | tf_op jit(solution)/shard_map/ppermute | solution.py:554
  256.7 25.5 %collective-permute-start.13 = (f32[768,128]{1,0:T(8,128)S(1)}, f32[768,128]{1,0:T(8,128)S(1)}, u32[]{:S(2)}, u32[]{:S(2)}) collective-permute-start(f32[768,128]{1,0:T(8,128)S(1)} %get-tuple-element.73), channel_id=1, source_target_pairs={{0,8},{4,12},{8,16},{12,20},{16,24},{20,28},{1,9},{5,13},{9,17},{1... | collective-permute-start | bytes 1179656 | tf_op jit(solution)/shard_map/ppermute | solution.py:554
  279.6 50.4 %copy-start.35 = (f32[1,768,128]{2,1,0:T(8,128)}, f32[1,768,128]{2,1,0:T(8,128)S(1)}, u32[]{:S(2)}) copy-start(f32[1,768,128]{2,1,0:T(8,128)S(1)} %collective-permute-done.33.refs_2_) | copy-start | bytes 1179652
  279.6 47.6 %collective-permute-start.6 = (f32[1,768,128]{2,1,0:T(8,128)S(1)}, f32[1,768,128]{2,1,0:T(8,128)S(1)}, u32[]{:S(2)}, u32[]{:S(2)}) collective-permute-start(f32[1,768,128]{2,1,0:T(8,128)S(1)} %get-tuple-element.53), channel_id=1, source_target_pairs={{0,16},{4,20},{8,24},{12,28},{1,17},{5,21},{9,25},{13,29},{2,18},{... | collective-permute-start | bytes 1179656 | tf_op jit(solution)/shard_map/ppermute | solution.py:554
  280.9 49.1 %copy-start.28 = (f32[768,128]{1,0:T(8,128)}, f32[768,128]{1,0:T(8,128)S(1)}, u32[]{:S(2)}) copy-start(f32[768,128]{1,0:T(8,128)S(1)} %collective-permute-done.14.refs_4_) | copy-start | bytes 1179652
  280.9 70.2 %collective-permute-start.15 = (f32[768,128]{1,0:T(8,128)S(1)}, f32[768,128]{1,0:T(8,128)S(1)}, u32[]{:S(2)}, u32[]{:S(2)}) collective-permute-start(f32[768,128]{1,0:T(8,128)S(1)} %get-tuple-element.55), channel_id=1, source_target_pairs={{0,16},{4,20},{8,24},{12,28},{1,17},{5,21},{9,25},{13,29},{2,18},{... | collective-permute-start | bytes 1179656 | tf_op jit(solution)/shard_map/ppermute | solution.py:554
  282.2 70.8 %collective-permute-start.17 = (f32[768,128]{1,0:T(8,128)S(1)}, f32[768,128]{1,0:T(8,128)S(1)}, u32[]{:S(2)}, u32[]{:S(2)}) collective-permute-start(f32[768,128]{1,0:T(8,128)S(1)} %get-tuple-element.60), channel_id=1, source_target_pairs={{0,8},{4,12},{8,16},{12,20},{16,24},{20,28},{1,9},{5,13},{9,17},{1... | collective-permute-start | bytes 1179656 | tf_op jit(solution)/shard_map/ppermute | solution.py:554
  285.1 70.3 %copy-start.13 = (f32[2,768,128]{2,1,0:T(8,128)}, f32[2,768,128]{2,1,0:T(8,128)S(1)}, u32[]{:S(2)}) copy-start(f32[2,768,128]{2,1,0:T(8,128)S(1)} %collective-permute-done.26.refs_3_.refs_4_) | copy-start | bytes 2359300
  285.1 70.3 %collective-permute-start.16 = (f32[768,128]{1,0:T(8,128)S(1)}, f32[768,128]{1,0:T(8,128)S(1)}, u32[]{:S(2)}, u32[]{:S(2)}) collective-permute-start(f32[768,128]{1,0:T(8,128)S(1)} %get-tuple-element.61), channel_id=1, source_target_pairs={{0,8},{4,12},{8,16},{12,20},{16,24},{20,28},{1,9},{5,13},{9,17},{1... | collective-permute-start | bytes 1179656 | tf_op jit(solution)/shard_map/ppermute | solution.py:554
  287.0 68.3 %copy-start.12 = (f32[2,768,128]{2,1,0:T(8,128)}, f32[2,768,128]{2,1,0:T(8,128)S(1)}, u32[]{:S(2)}) copy-start(f32[2,768,128]{2,1,0:T(8,128)S(1)} %collective-permute-done.4.refs_3_.refs_4_) | copy-start | bytes 2359300
  287.0 112.4 %collective-permute-start.28 = (f32[2,768,128]{2,1,0:T(8,128)}, f32[2,768,128]{2,1,0:T(8,128)}, u32[]{:S(2)}, u32[]{:S(2)}) collective-permute-start(f32[2,768,128]{2,1,0:T(8,128)} %pad_maximum_fusion.4), channel_id=1, source_target_pairs={{0,8},{4,12},{8,16},{12,20},{16,24},{20,28},{1,9},{5,13},{9,17},{1... | collective-permute-start | bytes 2359304 | tf_op jit(solution)/shard_map/ppermute | solution.py:554
  289.0 69.3 %copy-start.39 = (s32[8]{0:T(128)S(1)}, s32[8]{0:T(128)}, u32[]{:S(2)}) copy-start(s32[8]{0:T(128)} %param.34) | copy-start | bytes 100
  327.2 92.2 %collective-permute-start.7 = (f32[2,768,128]{2,1,0:T(8,128)}, f32[2,768,128]{2,1,0:T(8,128)}, u32[]{:S(2)}, u32[]{:S(2)}) collective-permute-start(f32[2,768,128]{2,1,0:T(8,128)} %pad_maximum_fusion.1), channel_id=1, source_target_pairs={{0,8},{4,12},{8,16},{12,20},{16,24},{20,28},{1,9},{5,13},{9,17},{1... | collective-permute-start | bytes 2359304 | tf_op jit(solution)/shard_map/ppermute | solution.py:554
  351.1 93.9 %collective-permute-start.34 = (f32[2,768,128]{2,1,0:T(8,128)}, f32[2,768,128]{2,1,0:T(8,128)S(1)}, u32[]{:S(2)}, u32[]{:S(2)}) collective-permute-start(f32[2,768,128]{2,1,0:T(8,128)} %pad_maximum_fusion.6), channel_id=1, source_target_pairs={{0,8},{4,12},{8,16},{12,20},{16,24},{20,28},{1,9},{5,13},{9,17},{1... | collective-permute-start | bytes 2359304 | tf_op jit(solution)/shard_map/ppermute | solution.py:554
  353.0 44.7 %collective-permute-start.27 = (f32[1,768,128]{2,1,0:T(8,128)}, f32[1,768,128]{2,1,0:T(8,128)}, u32[]{:S(2)}, u32[]{:S(2)}) collective-permute-start(f32[1,768,128]{2,1,0:T(8,128)} %get-tuple-element.54), channel_id=1, source_target_pairs={{0,16},{4,20},{8,24},{12,28},{1,17},{5,21},{9,25},{13,29},{2,18},{... | collective-permute-start | bytes 1179656 | tf_op jit(solution)/shard_map/ppermute | solution.py:554
  356.1 89.4 %collective-permute-start.36 = (f32[2,768,128]{2,1,0:T(8,128)}, f32[2,768,128]{2,1,0:T(8,128)S(1)}, u32[]{:S(2)}, u32[]{:S(2)}) collective-permute-start(f32[2,768,128]{2,1,0:T(8,128)} %pad_maximum_fusion.7), channel_id=1, source_target_pairs={{0,8},{4,12},{8,16},{12,20},{16,24},{20,28},{1,9},{5,13},{9,17},{1... | collective-permute-start | bytes 2359304 | tf_op jit(solution)/shard_map/ppermute | solution.py:554
  397.7 47.7 %collective-permute-start.35 = (f32[1,768,128]{2,1,0:T(8,128)S(1)}, f32[1,768,128]{2,1,0:T(8,128)}, u32[]{:S(2)}, u32[]{:S(2)}) collective-permute-start(f32[1,768,128]{2,1,0:T(8,128)S(1)} %copy-done.27), channel_id=1, source_target_pairs={{0,16},{4,20},{8,24},{12,28},{1,17},{5,21},{9,25},{13,29},{2,18},{... | collective-permute-start | bytes 1179656 | tf_op jit(solution)/shard_map/ppermute | solution.py:554
  399.4 46.0 %collective-permute-start.41 = (f32[768,128]{1,0:T(8,128)}, f32[768,128]{1,0:T(8,128)}, u32[]{:S(2)}, u32[]{:S(2)}) collective-permute-start(f32[768,128]{1,0:T(8,128)} %get-tuple-element.37), channel_id=1, source_target_pairs={{0,4},{4,0},{8,12},{12,8},{16,20},{20,16},{24,28},{28,24},{1,5},{5... | collective-permute-start | bytes 1179656 | tf_op jit(solution)/shard_map/ppermute | solution.py:554
  419.3 44.2 %collective-permute-start.29 = (f32[768,128]{1,0:T(8,128)}, f32[768,128]{1,0:T(8,128)}, u32[]{:S(2)}, u32[]{:S(2)}) collective-permute-start(f32[768,128]{1,0:T(8,128)} %get-tuple-element.33), channel_id=1, source_target_pairs={{0,4},{4,0},{8,12},{12,8},{16,20},{20,16},{24,28},{28,24},{1,5},{5... | collective-permute-start | bytes 1179656 | tf_op jit(solution)/shard_map/ppermute | solution.py:554
  445.0 24.6 %collective-permute-start.8 = (f32[768,128]{1,0:T(8,128)}, f32[768,128]{1,0:T(8,128)S(1)}, u32[]{:S(2)}, u32[]{:S(2)}) collective-permute-start(f32[768,128]{1,0:T(8,128)} %get-tuple-element.29), channel_id=1, source_target_pairs={{0,4},{4,0},{8,12},{12,8},{16,20},{20,16},{24,28},{28,24},{1,5},{5... | collective-permute-start | bytes 1179656 | tf_op jit(solution)/shard_map/ppermute | solution.py:554
  445.4 134.7 %collective-permute-start.20 = (f32[512,1024]{1,0:T(8,128)S(1)}, f32[512,1024]{1,0:T(8,128)S(1)}, u32[]{:S(2)}, u32[]{:S(2)}) collective-permute-start(f32[512,1024]{1,0:T(8,128)S(1)} %copy-done.3), channel_id=1, source_target_pairs={{0,24},{4,28},{8,16},{12,20},{16,8},{20,12},{24,0},{28,4},{1,25},{... | collective-permute-start | bytes 6291464 | tf_op jit(solution)/shard_map/ppermute | solution.py:554
  445.4 135.2 %collective-permute-start.19 = (f32[512,1024]{1,0:T(8,128)S(1)}, f32[512,1024]{1,0:T(8,128)}, u32[]{:S(2)}, u32[]{:S(2)}) collective-permute-start(f32[512,1024]{1,0:T(8,128)S(1)} %copy-done.3), channel_id=1, source_target_pairs={{0,16},{4,20},{8,24},{12,28},{16,0},{20,4},{24,8},{28,12},{1,17},{... | collective-permute-start | bytes 6291464 | tf_op jit(solution)/shard_map/ppermute | solution.py:554
  445.5 135.2 %collective-permute-start.18 = (f32[512,1024]{1,0:T(8,128)S(1)}, f32[512,1024]{1,0:T(8,128)}, u32[]{:S(2)}, u32[]{:S(2)}) collective-permute-start(f32[512,1024]{1,0:T(8,128)S(1)} %copy-done.3), channel_id=1, source_target_pairs={{0,8},{4,12},{8,0},{12,4},{16,24},{20,28},{24,16},{28,20},{1,9},{5... | collective-permute-start | bytes 6291464 | tf_op jit(solution)/shard_map/ppermute | solution.py:554
  463.6 82.9 %copy-start.34 = (f32[768,128]{1,0:T(8,128)S(1)}, f32[768,128]{1,0:T(8,128)}, u32[]{:S(2)}) copy-start(f32[768,128]{1,0:T(8,128)} %get-tuple-element.34) | copy-start | bytes 1179652
  463.6 10.5 %collective-permute-start.37 = (f32[768,128]{1,0:T(8,128)}, f32[768,128]{1,0:T(8,128)S(1)}, u32[]{:S(2)}, u32[]{:S(2)}) collective-permute-start(f32[768,128]{1,0:T(8,128)} %get-tuple-element.35), channel_id=1, source_target_pairs={{0,4},{4,0},{8,12},{12,8},{16,20},{20,16},{24,28},{28,24},{1,5},{5... | collective-permute-start | bytes 1179656 | tf_op jit(solution)/shard_map/ppermute | solution.py:554
  468.4 180.8 %copy-start.33 = (f32[768,128]{1,0:T(8,128)S(1)}, f32[768,128]{1,0:T(8,128)}, u32[]{:S(2)}) copy-start(f32[768,128]{1,0:T(8,128)} %get-tuple-element.28) | copy-start | bytes 1179652
  469.6 180.5 %copy-start.9 = (f32[2,768,128]{2,1,0:T(8,128)}, f32[2,768,128]{2,1,0:T(8,128)S(1)}, u32[]{:S(2)}) copy-start(f32[2,768,128]{2,1,0:T(8,128)S(1)} %pad_maximum_fusion.9.refs_0_) | copy-start | bytes 2359300
  469.6 23.0 %collective-permute-start.44 = (f32[2,768,128]{2,1,0:T(8,128)S(1)}, f32[2,768,128]{2,1,0:T(8,128)S(1)}, u32[]{:S(2)}, u32[]{:S(2)}) collective-permute-start(f32[2,768,128]{2,1,0:T(8,128)S(1)} %pad_maximum_fusion.9.refs_0_), channel_id=1, source_target_pairs={{0,3},{1,2},{2,1},{3,0},{4,7},{5,6},{6,5},{7,4},{8,11},{9,10},{10,... | collective-permute-start | bytes 2359304 | tf_op jit(solution)/shard_map/ppermute | solution.py:640
  474.1 68.8 %collective-permute-start.43 = (f32[2,768,128]{2,1,0:T(8,128)S(1)}, f32[2,768,128]{2,1,0:T(8,128)S(1)}, u32[]{:S(2)}, u32[]{:S(2)}) collective-permute-start(f32[2,768,128]{2,1,0:T(8,128)S(1)} %pad_maximum_fusion.9.refs_0_), channel_id=1, source_target_pairs={{0,2},{1,3},{2,0},{3,1},{4,6},{5,7},{6,4},{7,5},{8,10},{9,11},{10,... | collective-permute-start | bytes 2359304 | tf_op jit(solution)/shard_map/ppermute | solution.py:640
  492.6 157.5 %copy-start.16 = (f32[2,768,128]{2,1,0:T(8,128)}, f32[2,768,128]{2,1,0:T(8,128)S(1)}, u32[]{:S(2)}) copy-start(f32[2,768,128]{2,1,0:T(8,128)S(1)} %collective-permute-done.44.refs_3_) | copy-start | bytes 2359300
  492.6 84.0 %collective-permute-start.42 = (f32[2,768,128]{2,1,0:T(8,128)S(1)}, f32[2,768,128]{2,1,0:T(8,128)S(1)}, u32[]{:S(2)}, u32[]{:S(2)}) collective-permute-start(f32[2,768,128]{2,1,0:T(8,128)S(1)} %pad_maximum_fusion.9.refs_0_), channel_id=1, source_target_pairs={{0,1},{1,0},{2,3},{3,2},{4,5},{5,4},{6,7},{7,6},{8,9},{9,8},{10,11... | collective-permute-start | bytes 2359304 | tf_op jit(solution)/shard_map/ppermute | solution.py:640
  528.0 158.0 %copy-start.10 = (f32[2,768,128]{2,1,0:T(8,128)}, f32[2,768,128]{2,1,0:T(8,128)S(1)}, u32[]{:S(2)}) copy-start(f32[2,768,128]{2,1,0:T(8,128)S(1)} %pad_maximum_fusion.5.refs_0_) | copy-start | bytes 2359300
  543.0 37.2 %collective-permute-start.32 = (f32[2,768,128]{2,1,0:T(8,128)S(1)}, f32[2,768,128]{2,1,0:T(8,128)}, u32[]{:S(2)}, u32[]{:S(2)}) collective-permute-start(f32[2,768,128]{2,1,0:T(8,128)S(1)} %pad_maximum_fusion.5.refs_0_), channel_id=1, source_target_pairs={{0,3},{1,2},{2,1},{3,0},{4,7},{5,6},{6,5},{7,4},{8,11},{9,10},{10,... | collective-permute-start | bytes 2359304 | tf_op jit(solution)/shard_map/ppermute | solution.py:640
  546.6 127.1 %copy-start.11 = (f32[2,768,128]{2,1,0:T(8,128)}, f32[2,768,128]{2,1,0:T(8,128)S(1)}, u32[]{:S(2)}) copy-start(f32[2,768,128]{2,1,0:T(8,128)S(1)} %pad_maximum_fusion.8.refs_0_) | copy-start | bytes 2359300
  576.6 21.4 %collective-permute-start.40 = (f32[2,768,128]{2,1,0:T(8,128)S(1)}, f32[2,768,128]{2,1,0:T(8,128)S(1)}, u32[]{:S(2)}, u32[]{:S(2)}) collective-permute-start(f32[2,768,128]{2,1,0:T(8,128)S(1)} %pad_maximum_fusion.8.refs_0_), channel_id=1, source_target_pairs={{0,3},{1,2},{2,1},{3,0},{4,7},{5,6},{6,5},{7,4},{8,11},{9,10},{10,... | collective-permute-start | bytes 2359304 | tf_op jit(solution)/shard_map/ppermute | solution.py:640
  580.1 87.7 %collective-permute-start.21 = (f32[512,1024]{1,0:T(8,128)S(1)}, f32[512,1024]{1,0:T(8,128)S(1)}, u32[]{:S(2)}, u32[]{:S(2)}) collective-permute-start(f32[512,1024]{1,0:T(8,128)S(1)} %copy-done.3), channel_id=1, source_target_pairs={{0,4},{4,0},{8,12},{12,8},{16,20},{20,16},{24,28},{28,24},{1,5},{5... | collective-permute-start | bytes 6291464 | tf_op jit(solution)/shard_map/ppermute | solution.py:554
  580.1 95.2 %copy-start.4 = (f32[512,1024]{1,0:T(8,128)}, f32[512,1024]{1,0:T(8,128)S(1)}, u32[]{:S(2)}) copy-start(f32[512,1024]{1,0:T(8,128)S(1)} %collective-permute-done.20.refs_7_) | copy-start | bytes 6291460
  580.1 89.4 %collective-permute-start.24 = (f32[512,1024]{1,0:T(8,128)S(1)}, f32[512,1024]{1,0:T(8,128)S(1)}, u32[]{:S(2)}, u32[]{:S(2)}) collective-permute-start(f32[512,1024]{1,0:T(8,128)S(1)} %collective-permute-done.20.refs_7_), channel_id=1, source_target_pairs={{0,4},{4,0},{8,12},{12,8},{16,20},{20,16},{24,28},{28,24},{1,5},{5... | collective-permute-start | bytes 6291464 | tf_op jit(solution)/shard_map/ppermute | solution.py:554
  580.6 90.2 %collective-permute-start.23 = (f32[512,1024]{1,0:T(8,128)}, f32[512,1024]{1,0:T(8,128)S(1)}, u32[]{:S(2)}, u32[]{:S(2)}) collective-permute-start(f32[512,1024]{1,0:T(8,128)} %collective-permute-done.19.refs_6_), channel_id=1, source_target_pairs={{0,4},{4,0},{8,12},{12,8},{16,20},{20,16},{24,28},{28,24},{1,5},{5... | collective-permute-start | bytes 6291464 | tf_op jit(solution)/shard_map/ppermute | solution.py:554
  580.7 92.9 %collective-permute-start.22 = (f32[512,1024]{1,0:T(8,128)}, f32[512,1024]{1,0:T(8,128)}, u32[]{:S(2)}, u32[]{:S(2)}) collective-permute-start(f32[512,1024]{1,0:T(8,128)} %collective-permute-done.18.refs_5_), channel_id=1, source_target_pairs={{0,4},{4,0},{8,12},{12,8},{16,20},{20,16},{24,28},{28,24},{1,5},{5... | collective-permute-start | bytes 6291464 | tf_op jit(solution)/shard_map/ppermute | solution.py:554
  598.0 50.3 %copy-start.19 = (f32[2,768,128]{2,1,0:T(8,128)}, f32[2,768,128]{2,1,0:T(8,128)S(1)}, u32[]{:S(2)}) copy-start(f32[2,768,128]{2,1,0:T(8,128)S(1)} %collective-permute-done.40.refs_3_) | copy-start | bytes 2359300
  598.0 50.3 %collective-permute-start.39 = (f32[2,768,128]{2,1,0:T(8,128)S(1)}, f32[2,768,128]{2,1,0:T(8,128)S(1)}, u32[]{:S(2)}, u32[]{:S(2)}) collective-permute-start(f32[2,768,128]{2,1,0:T(8,128)S(1)} %pad_maximum_fusion.8.refs_0_), channel_id=1, source_target_pairs={{0,2},{1,3},{2,0},{3,1},{4,6},{5,7},{6,4},{7,5},{8,10},{9,11},{10,... | collective-permute-start | bytes 2359304 | tf_op jit(solution)/shard_map/ppermute | solution.py:640
  648.3 18.0 %collective-permute-start.38 = (f32[2,768,128]{2,1,0:T(8,128)S(1)}, f32[2,768,128]{2,1,0:T(8,128)S(1)}, u32[]{:S(2)}, u32[]{:S(2)}) collective-permute-start(f32[2,768,128]{2,1,0:T(8,128)S(1)} %pad_maximum_fusion.8.refs_0_), channel_id=1, source_target_pairs={{0,1},{1,0},{2,3},{3,2},{4,5},{5,4},{6,7},{7,6},{8,9},{9,8},{10,11... | collective-permute-start | bytes 2359304 | tf_op jit(solution)/shard_map/ppermute | solution.py:640
  666.3 38.0 %collective-permute-start.31 = (f32[2,768,128]{2,1,0:T(8,128)S(1)}, f32[2,768,128]{2,1,0:T(8,128)S(1)}, u32[]{:S(2)}, u32[]{:S(2)}) collective-permute-start(f32[2,768,128]{2,1,0:T(8,128)S(1)} %pad_maximum_fusion.5.refs_0_), channel_id=1, source_target_pairs={{0,2},{1,3},{2,0},{3,1},{4,6},{5,7},{6,4},{7,5},{8,10},{9,11},{10,... | collective-permute-start | bytes 2359304 | tf_op jit(solution)/shard_map/ppermute | solution.py:640
  667.8 53.6 %collective-permute-start.30 = (f32[2,768,128]{2,1,0:T(8,128)S(1)}, f32[2,768,128]{2,1,0:T(8,128)}, u32[]{:S(2)}, u32[]{:S(2)}) collective-permute-start(f32[2,768,128]{2,1,0:T(8,128)S(1)} %pad_maximum_fusion.5.refs_0_), channel_id=1, source_target_pairs={{0,1},{1,0},{2,3},{3,2},{4,5},{5,4},{6,7},{7,6},{8,9},{9,8},{10,11... | collective-permute-start | bytes 2359304 | tf_op jit(solution)/shard_map/ppermute | solution.py:640
  669.5 62.8 %collective-permute-start.11 = (f32[2,768,128]{2,1,0:T(8,128)}, f32[2,768,128]{2,1,0:T(8,128)S(1)}, u32[]{:S(2)}, u32[]{:S(2)}) collective-permute-start(f32[2,768,128]{2,1,0:T(8,128)} %pad_maximum_fusion.2.refs_0_), channel_id=1, source_target_pairs={{0,3},{1,2},{2,1},{3,0},{4,7},{5,6},{6,5},{7,4},{8,11},{9,10},{10,... | collective-permute-start | bytes 2359304 | tf_op jit(solution)/shard_map/ppermute | solution.py:640
  672.2 96.5 %collective-permute-start.10 = (f32[2,768,128]{2,1,0:T(8,128)}, f32[2,768,128]{2,1,0:T(8,128)S(1)}, u32[]{:S(2)}, u32[]{:S(2)}) collective-permute-start(f32[2,768,128]{2,1,0:T(8,128)} %pad_maximum_fusion.2.refs_0_), channel_id=1, source_target_pairs={{0,2},{1,3},{2,0},{3,1},{4,6},{5,7},{6,4},{7,5},{8,10},{9,11},{10,... | collective-permute-start | bytes 2359304 | tf_op jit(solution)/shard_map/ppermute | solution.py:640
  673.6 95.1 %collective-permute-start.9 = (f32[2,768,128]{2,1,0:T(8,128)}, f32[2,768,128]{2,1,0:T(8,128)}, u32[]{:S(2)}, u32[]{:S(2)}) collective-permute-start(f32[2,768,128]{2,1,0:T(8,128)} %pad_maximum_fusion.2.refs_0_), channel_id=1, source_target_pairs={{0,1},{1,0},{2,3},{3,2},{4,5},{5,4},{6,7},{7,6},{8,9},{9,8},{10,11... | collective-permute-start | bytes 2359304 | tf_op jit(solution)/shard_map/ppermute | solution.py:640
  (24 other events, 288.3 us)

commit v3 on v2

--- a/solution.py
+++ b/solution.py
@@ -359,6 +359,56 @@
     )(place, short_out, post, conv)
 
 
+def load(ref):
+    return ref[0] if len(ref.shape) == 3 else ref[...]
+
+
+def ordered(refs, core):
+    first = core == 0
+    x = {name: load(ref) for name, ref in refs.items()}
+    yield x["far"] + x["far_more"] if "far_more" in x else x["far"]
+    yield jnp.where(first, x["near_mine"], x["near_other"])
+    yield jnp.where(first, x["near_other"], x["near_mine"])
+    yield jnp.where(first, x["mine"], x["other"])
+    yield jnp.where(first, x["other"], x["mine"])
+
+
+def fill_keys(k_cat, refs, core):
+    for n, k in enumerate(ordered(refs, core)):
+        hi, lo = halves(k.T)
+        k_cat[n] = jnp.concatenate([hi, hi, lo], axis=0)
+
+
+def fill_values(v_cat, refs, core):
+    for n, v in enumerate(ordered(refs, core)):
+        hi, lo = halves(v)
+        v_cat[n] = jnp.concatenate([hi, lo], axis=1)
+
+
+def query_cat(q_refs, turn):
+    scale = math.log2(math.e) / math.sqrt(q_refs[0].shape[1])
+    queries = jnp.where(turn == 0, q_refs[1][...], q_refs[0][...])
+    hi, lo = halves(queries * scale)
+    return jnp.concatenate([hi, lo, hi], axis=1)
+
+
+def weigh(hi, lo, values):
+    dim = values.shape[1] // 2
+    both = mm(hi, values)
+    return both[:, :dim] + both[:, dim:] + mm(lo, values[:, :dim])
+
+
+def own_tiles(q_cat, k_own):
+    length = q_cat.shape[0]
+    tile = min(length, 256)
+    for start in range(0, length, tile):
+        stop = start + tile
+        scores = mm(q_cat[start:stop], k_own[:, :stop])
+        row = start + lax.broadcasted_iota(jnp.int32, (tile, stop), 0)
+        col = lax.broadcasted_iota(jnp.int32, (tile, stop), 1)
+        yield pl.ds(start, tile), stop, jnp.where(row >= col, scores, masked_low)
+
+
 def attend_kernel(reach_ref, place_ref, *refs, head, names):
     count = len(names)
     q_refs = refs[:2]
@@ -368,54 +418,23 @@
     turn = pl.program_id(0)
     core = place_ref[1]
     odd = jnp.where(turn == 0, 1 - core, core)
-    length, dim = mine_ref.shape
-
-    def load(ref):
-        return ref[0] if len(ref.shape) == 3 else ref[...]
-
-    def ordered(refs):
-        first = core == 0
-        x = {name: load(ref) for name, ref in refs.items()}
-        yield x["far"]
-        yield jnp.where(first, x["near_mine"], x["near_other"])
-        yield jnp.where(first, x["near_other"], x["near_mine"])
-        yield jnp.where(first, x["mine"], x["other"])
-        yield jnp.where(first, x["other"], x["mine"])
 
     @pl.when(turn == 0)
     def _():
-        for n, k in enumerate(ordered(k_refs)):
-            hi, lo = halves(k.T)
-            k_cat[n] = jnp.concatenate([hi, hi, lo], axis=0)
-        for n, v in enumerate(ordered(v_refs)):
-            hi, lo = halves(v)
-            v_cat[n] = jnp.concatenate([hi, lo], axis=1)
-
-    scale = math.log2(math.e) / math.sqrt(dim)
-    queries = jnp.where(turn == 0, q_refs[1][...], q_refs[0][...])
-    q_hi, q_lo = halves(queries * scale)
-    q_cat = jnp.concatenate([q_hi, q_lo, q_hi], axis=1)
+        fill_keys(k_cat, k_refs, core)
+        fill_values(v_cat, v_refs, core)
+
+    q_cat = query_cat(q_refs, turn)
     reach = reach_ref[head]
     block = 2 * place_ref[0] + odd
     own = odd + REACH
 
-    def weigh(weight, values):
-        w_hi, w_lo = halves(weight)
-        both = mm(w_hi, values)
-        return both[:, :dim] + both[:, dim:] + mm(w_lo, values[:, :dim])
-
-    tile = min(length, 256)
-    for start in range(0, length, tile):
-        rows, stop = pl.ds(start, tile), start + tile
-        scores = mm(q_cat[start:stop], k_cat[own, :, :stop])
-        row = start + lax.broadcasted_iota(jnp.int32, (tile, stop), 0)
-        col = lax.broadcasted_iota(jnp.int32, (tile, stop), 1)
-        scores = jnp.where(row >= col, scores, masked_low)
+    for rows, stop, scores in own_tiles(q_cat, k_cat[own]):
         best = jnp.max(scores, axis=1, keepdims=True)
         weight = jnp.exp2(scores - best)
         top[rows, :] = best
         total[rows, :] = jnp.sum(weight, axis=1, keepdims=True)
-        acc[rows, :] = weigh(weight, v_cat[own, :stop, :])
+        acc[rows, :] = weigh(*halves(weight), v_cat[own, :stop, :])
 
     for distance in range(1, REACH + 1):
 
@@ -429,7 +448,7 @@
             weight = jnp.exp2(scores - best)
             top[...] = best
             total[...] = total[...] * shrink + jnp.sum(weight, axis=1, keepdims=True)
-            acc[...] = acc[...] * shrink + weigh(weight, v_cat[slot])
+            acc[...] = acc[...] * shrink + weigh(*halves(weight), v_cat[slot])
 
     result = acc[...] / total[...]
 
@@ -440,26 +459,111 @@
     @pl.when(turn == 1)
     def _():
         mine_ref[...] = result
+
+
+def score_kernel(reach_ref, place_ref, *refs, head, names):
+    count = len(names)
+    q_refs = refs[:2]
+    k_refs = dict(zip(names, refs[2 : 2 + count]))
+    hi_ref, lo_ref, total_ref, k_cat, work, top = refs[2 + count :]
+    turn = pl.program_id(0)
+    core = place_ref[1]
+    odd = jnp.where(turn == 0, 1 - core, core)
+
+    @pl.when(turn == 0)
+    def _():
+        fill_keys(k_cat, k_refs, core)
+
+    q_cat = query_cat(q_refs, turn)
+    reach = reach_ref[head]
+    block = 2 * place_ref[0] + odd
+    own = odd + REACH
+    length = work.shape[1]
+
+    for rows, stop, scores in own_tiles(q_cat, k_cat[own]):
+        top[rows, :] = jnp.max(scores, axis=1, keepdims=True)
+        work[0, rows, :stop] = scores
+        if stop < length:
+            work[0, rows, stop:] = jnp.full((scores.shape[0], length - stop), masked_low, F32)
+
+    def used(distance):
+        return (distance <= reach) & (block >= distance)
+
+    for distance in range(1, REACH + 1):
+
+        @pl.when(used(distance))
+        def _():
+            scores = mm(q_cat, k_cat[own - distance])
+            top[...] = jnp.maximum(top[...], jnp.max(scores, axis=1, keepdims=True))
+            work[distance] = scores
+
+    for distance in range(REACH + 1):
+
+        def finish():
+            weight = jnp.exp2(work[distance] - top[...])
+            part = jnp.broadcast_to(jnp.sum(weight, axis=1, keepdims=True), total_ref.shape[1:])
+            total_ref[0] = part if distance == 0 else total_ref[0] + part
+            hi_ref[0, distance], lo_ref[0, distance] = halves(weight)
+
+        if distance:
+            pl.when(used(distance))(finish)
+        else:
+            finish()
+
+
+def value_kernel(reach_ref, place_ref, *refs, head, names):
+    hi_ref, lo_ref, total_ref = refs[:3]
+    v_refs = dict(zip(names, refs[3:-4]))
+    other_ref, mine_ref, v_cat, acc = refs[-4:]
+    turn, distance = pl.program_id(0), pl.program_id(1)
+    core = place_ref[1]
+    odd = jnp.where(turn == 0, 1 - core, core)
+
+    @pl.when((turn == 0) & (distance == 0))
+    def _():
+        fill_values(v_cat, v_refs, core)
+
+    block = 2 * place_ref[0] + odd
+    slot = odd + REACH - distance
+
+    @pl.when(distance == 0)
+    def _():
+        acc[...] = weigh(hi_ref[0, 0], lo_ref[0, 0], v_cat[slot])
+
+    @pl.when((distance > 0) & (distance <= reach_ref[head]) & (block >= distance))
+    def _():
+        acc[...] += weigh(hi_ref[0, 0], lo_ref[0, 0], v_cat[slot])
+
+    @pl.when((distance == REACH) & (turn == 0))
+    def _():
+        other_ref[...] = acc[...] / total_ref[0]
+
+    @pl.when((distance == REACH) & (turn == 1))
+    def _():
+        mine_ref[...] = acc[...] / total_ref[0]
+
+
+def operand_specs(operands, head, length):
+    def spec_of(x, lead):
+        if lead is not None:
+            return pl.BlockSpec((1, length, HEAD_DIM), lambda *_: (lead, 0, 0))
+        at = head if x.shape[1] > HEAD_DIM else 0
+        return pl.BlockSpec((length, HEAD_DIM), lambda *_: (0, at))
+
+    return [spec_of(*x) for x in operands]
 
 
 def attend_stage(reach, place, queries, keys, values, head):
     length = queries[0].shape[0]
     steps = REACH + 2
-
-    def spec_of(x, lead):
-        if lead is not None:
-            return pl.BlockSpec((1, length, HEAD_DIM), lambda i, *_: (lead, 0, 0))
-        at = head if x.shape[1] > HEAD_DIM else 0
-        return pl.BlockSpec((length, HEAD_DIM), lambda i, *_: (0, at))
-
     operands = [(q, None) for q in queries] + list(keys.values()) + list(values.values())
     return pl.pallas_call(
         functools.partial(attend_kernel, head=head, names=tuple(keys)),
         grid_spec=pltpu.PrefetchScalarGridSpec(
             num_scalar_prefetch=2,
             grid=(2,),
-            in_specs=[spec_of(*x) for x in operands],
-            out_specs=[pl.BlockSpec((length, HEAD_DIM), lambda i, *_: (0, 0))] * 2,
+            in_specs=operand_specs(operands, head, length),
+            out_specs=[pl.BlockSpec((length, HEAD_DIM), lambda *_: (0, 0))] * 2,
             scratch_shapes=[
                 pltpu.VMEM((steps, 3 * HEAD_DIM, length), BF16),
                 pltpu.VMEM((steps, length, 2 * HEAD_DIM), BF16),
@@ -474,16 +578,69 @@
     )(reach, place, *[x for x, _ in operands])
 
 
-def product_kernel(place_ref, *refs, count, added):
-    a_refs, w_refs = refs[:count], refs[count : 3 * count]
-    rest = refs[3 * count :]
+def score_stage(reach, place, queries, keys, head):
+    length = queries[0].shape[0]
+    operands = [(q, None) for q in queries] + list(keys.values())
+    big = (1, REACH + 1, length, length)
+    return pl.pallas_call(
+        functools.partial(score_kernel, head=head, names=tuple(keys)),
+        grid_spec=pltpu.PrefetchScalarGridSpec(
+            num_scalar_prefetch=2,
+            grid=(2,),
+            in_specs=operand_specs(operands, head, length),
+            out_specs=[pl.BlockSpec(big, lambda i, *_: (i, 0, 0, 0))] * 2
+            + [pl.BlockSpec((1, length, HEAD_DIM), lambda i, *_: (i, 0, 0))],
+            scratch_shapes=[
+                pltpu.VMEM((REACH + 2, 3 * HEAD_DIM, length), BF16),
+                pltpu.VMEM(big[1:], F32),
+                pltpu.VMEM((length, 1), F32),
+            ],
+        ),
+        out_shape=[jax.ShapeDtypeStruct((2, *big[1:]), BF16)] * 2
+        + [jax.ShapeDtypeStruct((2, length, HEAD_DIM), F32)],
+        compiler_params=pltpu.CompilerParams(vmem_limit_bytes=VMEM_CAP),
+        name="score_stage",
+    )(reach, place, *[x for x, _ in operands])
+
+
+def value_stage(reach, place, scored, values, head):
+    hi, lo, total = scored
+    length = hi.shape[2]
+    operands = list(values.values())
+    part = pl.BlockSpec((1, 1, length, length), lambda i, d, *_: (i, d, 0, 0))
+    return pl.pallas_call(
+        functools.partial(value_kernel, head=head, names=tuple(values)),
+        grid_spec=pltpu.PrefetchScalarGridSpec(
+            num_scalar_prefetch=2,
+            grid=(2, REACH + 1),
+            in_specs=[part, part, pl.BlockSpec((1, length, HEAD_DIM), lambda i, *_: (i, 0, 0))]
+            + operand_specs(operands, head, length),
+            out_specs=[pl.BlockSpec((length, HEAD_DIM), lambda *_: (0, 0))] * 2,
+            scratch_shapes=[
+                pltpu.VMEM((REACH + 2, length, 2 * HEAD_DIM), BF16),
+                pltpu.VMEM((length, HEAD_DIM), F32),
+            ],
+        ),
+        out_shape=[jax.ShapeDtypeStruct((length, HEAD_DIM), F32)] * 2,
+        compiler_params=pltpu.CompilerParams(vmem_limit_bytes=VMEM_CAP),
+        name="value_stage",
+    )(reach, place, hi, lo, total, *[x for x, _ in operands])
+
+
+def product_kernel(place_ref, *refs, sizes, added):
+    count = len(sizes)
+    a_groups, at = [], 0
+    for size in sizes:
+        a_groups.append(refs[at : at + size])
+        at += size
+    w_refs, rest = refs[at : at + 2 * count], refs[at + 2 * count :]
     out_ref, left = rest[-2:]
 
     @pl.when(pl.program_id(0) == 0)
     def _():
         apart = place_ref[0] ^ place_ref[2]
         for h in range(2):
-            pieces = [r[h] for r in a_refs]
+            pieces = [sum((r[h] for r in group[1:]), group[0][h]) for group in a_groups]
             bit = 1
             while bit < count:
                 flip = (apart & bit) != 0
@@ -500,28 +657,34 @@
     out_ref[...] = rest[0][...] + out if added else out
 
 
-def product_stage(place, pieces, weights, head, total):
+def product_stage(place, pieces, weights, total):
     count = len(pieces)
-    _, length, part = pieces[0].shape
-    width = weights[0].shape[1]
+    flat = [x for group in pieces for x in group]
+    _, length, part = flat[0].shape
+    width = weights[0][0].shape[1]
     tile = min(width, 256)
     a_spec = pl.BlockSpec((2, length, part), lambda i, place: (0, 0, 0))
-    w_spec = pl.BlockSpec((part, tile), lambda i, place: (head, i))
+
+    def w_spec(row):
+        return pl.BlockSpec((part, tile), lambda i, place: (row, i))
+
     out_spec = pl.BlockSpec((length, tile), lambda i, place: (0, i))
     extra = [] if total is None else [total]
     return pl.pallas_call(
-        functools.partial(product_kernel, count=count, added=total is not None),
+        functools.partial(
+            product_kernel, sizes=tuple(len(g) for g in pieces), added=total is not None
+        ),
         grid_spec=pltpu.PrefetchScalarGridSpec(
             num_scalar_prefetch=1,
             grid=(width // tile,),
-            in_specs=[a_spec] * count + [w_spec] * (2 * count) + [out_spec] * len(extra),
+            in_specs=[a_spec] * len(flat) + [w_spec(row) for _, row in weights] + [out_spec] * len(extra),
             out_specs=out_spec,
             scratch_shapes=[pltpu.VMEM((2, length, 3 * count * part), BF16)],
         ),
         out_shape=jax.ShapeDtypeStruct((length, width), F32),
         compiler_params=pltpu.CompilerParams(vmem_limit_bytes=VMEM_CAP),
         name="product_stage",
-    )(place, *pieces, *weights, *extra)
+    )(place, *flat, *[w for w, _ in weights], *extra)
 
 
 def shards(
@@ -571,12 +734,15 @@
     def own_of(mine, other):
         return {"mine": (mine, None), "other": (other, None)}
 
-    def first_window(mine, other):
+    def first_window(mine, other_out, other):
+        both = range(0, parts, 2)
         near_mine = shift(cut(mine, 0), 2)
-        near_other = shift(cut(other, 0), 2)
-        far = shift(jnp.where(core == 0, cut(other, 0), cut(mine, 0)), 4)
-        near = {"far": (far, None), "near_mine": (near_mine, None), "near_other": (near_other, None)}
-        return near | own_of(mine, other)
+        crossed = [(c, c + 3) for c in both] + [(c + 1, c + 2) for c in both]
+        near_other = send(cut(other_out, 0), [(i, j) for i, j in crossed if j < parts])
+        far = send(cut(mine, 0), [(c + 1, c + 5) for c in both if c + 5 < parts])
+        more = send(cut(other_out, 0), [(c + 1, c + 4) for c in both if c + 4 < parts])
+        got = {"far": far, "far_more": more, "near_mine": near_mine, "near_other": near_other}
+        return {k: (x, None) for k, x in got.items()} | own_of(mine, other)
 
     def later_windows(mine, other, heads):
         near = jnp.stack([cut(x, head) for head in heads for x in (mine, other)])
@@ -610,35 +776,57 @@
         conv = plain_long_convolve(
             signal.reshape(whole, group).T, filt.transpose(1, 0, 2).reshape(group, whole)
         ).T.reshape(parts, length, group)
+    reach = lax.dynamic_slice_in_dim(head_reach, core * heads_half, heads_half)
+    key_windows = later_windows(key_mine, key_other, range(min(2, heads_half)))
+    for n in range(2, heads_half):
+        key_windows += later_windows(key_mine, key_other, [n])
+    scored = score_stage(reach, place, queries, key_windows[0], 0)
     back = lax.all_to_all(conv, "seq", split_axis=0, concat_axis=0, tiled=True)
-    hyena_out, value_other, value_mine = hyena_stage(place, short_out, long_gate_post, back)
-    value_other = swap(value_other)
-
-    reach = lax.dynamic_slice_in_dim(head_reach, core * heads_half, heads_half)
-    weights = None
+    hyena_out, value_out, value_mine = hyena_stage(place, short_out, long_gate_post, back)
+    value_other = swap(value_out)
+
     mixed = None
-    key_windows = [first_window(key_mine, key_other)]
-    for n in range(1, heads_half):
-        key_windows += later_windows(key_mine, key_other, [n])
     for n in range(heads_half):
-        keys = key_windows[n]
         if n == 0:
-            values = first_window(value_mine, value_other)
+            values = first_window(value_mine, value_out, value_other)
         else:
             values = later_windows(value_mine, value_other, [n])[0]
-        other, mine = attend_stage(reach, place, queries, keys, values, n)
+        if n == 0:
+            other, mine = value_stage(reach, place, scored, values, n)
+        else:
+            other, mine = attend_stage(reach, place, queries, key_windows[n], values, n)
         if n == 0:
             out_weight, mine = lax.optimization_barrier((out_weight, mine))
-            weights = [out_weight]
-            for m in range(1, chips):
-                weights.append(send(out_weight, [(i, i ^ (2 * m)) for i in range(parts)]))
-            for m in range(chips):
-                weights.append(swap(weights[m]))
+            slots = [out_weight]
+            relayed = chips == 4
+            for m in range(1, chips - relayed):
+                slots.append(send(out_weight, [(i, i ^ (2 * m)) for i in range(parts)]))
+            if relayed:
+                cut_at = out_weight.shape[0] // 2
+                for m, piece in ((1, slots[1][:cut_at]), (2, slots[2][cut_at:])):
+                    slots.append(send(piece, [(i, i ^ (6 - 2 * m)) for i in range(parts)]))
+            partner = []
+            for x in slots:
+                partner.append(swap(x))
         piece = jnp.stack([mine, swap(other)])
-        pieces = [piece]
+        pieces = [[piece]]
+        relays = planes == 4 and n < heads_half - 1
         for m in range(1, planes):
-            pieces.append(lax.ppermute(piece, "chan", [(i, i ^ m) for i in range(planes)]))
-        mixed = product_stage(place, pieces, weights, n, mixed)
+            pairs = [(i, i ^ m) for i in range(planes)]
+            if relays and m > 1:
+                pairs = [(0, 2), (3, 1)] if m == 2 else [(1, 2), (2, 1)]
+            pieces.append([lax.ppermute(piece, "chan", pairs)])
+        if relays:
+            passed = {2: pieces[3][0], 3: pieces[2][0]}
+            for m in (2, 3):
+                pieces[m].append(lax.ppermute(passed[m], "chan", [(1, 0), (2, 3)]))
+        if relayed:
+            late = n * 2 // heads_half
+            rows = [(0, n), (1, n), (2, n), (3 + late, n - late * (heads_half // 2))]
+        else:
+            rows = [(m, n) for m in range(chips)]
+        weights = [(side[m], row) for side in (slots, partner) for m, row in rows]
+        mixed = product_stage(place, pieces, weights, mixed)
     return (hyena_out, mixed)
 
 

time: 789 us -> 733 us (0.929)
  the two profiles are of different devices: /device:TPU:4 before, /device:TPU:22 now
where the time goes in v3:
time: 733 us; the launch traced here: 725 us
  waiting for transfers between devices  344 us (47%)
  Pallas kernels  204 us (28%)
  starting transfers between devices  150 us (20%)
  local copies, waits for them, and re-layouts  14.6 us (2%)
  other arithmetic  9.71 us (1%)
    ppermute x33, waiting for transfers between devices, send(): return lax.ppermute(x, 'seq', pairs)  149 us
    ppermute x12, waiting for transfers between devices, shards(): pieces.append([lax.ppermute(piece, 'chan', pairs)])  90.6 us
    ppermute x33, starting transfers between devices, send(): return lax.ppermute(x, 'seq', pairs)  81.7 us
    ppermute x6, waiting for transfers between devices, shards(): pieces[m].append(lax.ppermute(passed[m], 'chan', [(1, 0), (2, 3)]))  59.7 us
    pallas_call x3, Pallas kernels, attend_stage(): pl.pallas_call(functools.partial(attend_kernel, head=head, names=tuple(ke...  49.1 us
    pallas_call x4, Pallas kernels, product_stage(): pl.pallas_call(functools.partial(product_kernel, sizes=tuple((len(g) for...  44.9 us
    pallas_call x1, Pallas kernels, signal_stage(): pl.pallas_call(signal_kernel, in_specs=[vmem_spec()] * 8 + [smem_spec()]...  34.7 us
    all_to_all x1, waiting for transfers between devices, shards(): back = lax.all_to_all(conv, 'seq', split_axis=0, concat_axis=0, tiled=True)  31 us
  transfers between devices with their start and end apart: 54, of which 23 were waited for; matrix products, arithmetic and copies ran while one was open for 2% of the time, Pallas kernels for 22%

profile of v3, /device:TPU:22, one launch (start us, length us, event | category | flops | bytes accessed | tf_op | source)
XLA Modules:
  0.0 724.9 jit_solution(2891622966977646878)
XLA Ops:
  0.6 4.2 all-to-all-start.1
  6.1 2.0 collective-permute-start
  8.1 37.9 %collective-permute-done.halo = f32[128,1024]{1,0:T(8,128)S(1)} collective-permute-done((f32[128,1024]{1,0:T(8,128)S(1)}, f32[128,1024]{1,0:T(8,128)S(1)}, u32[]{:S(2)}, u32[]{:S(2)}) %collective-permute-start) | collective-permute-done | bytes 524320 | tf_op jit(solution)/shard_map/ppermute | solution.py:717
  46.8 14.2 %short_stage.1 = (f32[768,1024]{1,0:T(8,128)}, f32[8,768,128]{2,1,0:T(8,128)}) custom-call(bf16[256,256]{1,0:T(8,128)(2,1)} %constant.71.clone.f_hi, bf16[256,256]{1,0:T(8,128)(2,1)} %constant.72.clone.f_lo, bf16[128,256]{1,0:T(8,128)(2,1)} %constant.73.clone.g_hi, bf16[128,256]{1,0:T(8,128)(2,1)} %constant.74.clone.g_lo, f32[128,1024]{1,0:T(8,128)} %copy-done.33, ...), custom_call_target="tpu_custom_call" | custom-call | tf_op jit(solution)/shard_map/short_stage/pallas_call | solution.py:92
  61.0 1.7 copy-done.10
  62.8 4.4 all-to-all-start
  67.2 2.2 constant_dynamic-slice_fusion.2
  69.5 19.0 %filter_stage.1.spec = f32[48,256,128]{2,1,0:T(8,128)} custom-call(bf16[768,384]{1,0:T(8,128)(2,1)} %constant.75.clone.w_hi, bf16[768,384]{1,0:T(8,128)(2,1)} %constant.76.clone.w_lo, bf16[256,256]{1,0:T(8,128)(2,1)} %constant.77.clone.b_hi, bf16[256,256]{1,0:T(8,128)(2,1)} %constant.78.clone.b_lo, f32[16,48]{1,0:T(8,128)} %constant.79.clone.t_re, ...), custom_call_target="tpu_custom_call" | custom-call | tf_op jit(solution)/shard_map/filter_stage/pallas_call | solution.py:244
  88.5 14.1 %all-to-all-done = f32[8,768,128]{2,1,0:T(8,128)} async-done(((f32[8,768,128]{2,1,0:T(8,128)}), f32[8,768,128]{2,1,0:T(8,128)}, u32[]{:S(2)}, u32[]{:S(2)}) %all-to-all-start) | async-done | bytes 3145760 | tf_op jit(solution)/shard_map/all_to_all | solution.py:765
  102.6 34.7 %signal_stage.1 = f32[48,128,128]{2,1,0:T(8,128)} custom-call(bf16[768,384]{1,0:T(8,128)(2,1)} %constant.75.clone.w_hi, bf16[768,384]{1,0:T(8,128)(2,1)} %constant.76.clone.w_lo, bf16[384,768]{1,0:T(8,128)(2,1)} %constant.81.clone.v_hi, bf16[384,768]{1,0:T(8,128)(2,1)} %constant.82.clone.v_lo, bf16[256,256]{1,0:T(8,128)(2,1)} %constant.77.clone.b_hi, ...), custom_call_target="tpu_custom_call" | custom-call | tf_op jit(solution)/shard_map/signal_stage/pallas_call | solution.py:261
  137.3 6.7 all-to-all-start.2
  144.0 3.9 constant_dynamic-slice_fusion
  148.6 31.0 %all-to-all-done.2.conv = f32[8,768,128]{2,1,0:T(8,128)} async-done(((f32[8,768,128]{2,1,0:T(8,128)}), f32[8,768,128]{2,1,0:T(8,128)}, u32[]{:S(2)}, u32[]{:S(2)}) %all-to-all-start.2) | async-done | bytes 3145760 | tf_op jit(solution)/shard_map/all_to_all | solution.py:784
  179.6 9.2 %hyena_stage.1 = (f32[768,1024]{1,0:T(8,128)}, f32[768,512]{1,0:T(8,128)}, f32[768,512]{1,0:T(8,128)}) custom-call(s32[3]{0:T(128)} %pad_add_fusion.place_ref, f32[768,1024]{1,0:T(8,128)} %get-tuple-element.23.short_out, f32[768,1024]{1,0:T(8,128)} %post.3, f32[8,768,128]{2,1,0:T(8,128)} %all-to-all-done.2.conv), custom_call_target="tpu_custom_call" | custom-call | tf_op jit(solution)/shard_map/hyena_stage/pallas_call | solution.py:335
  190.8 1.4 collective-permute-start.12
  196.8 25.7 %collective-permute-done.3.refs_2_ = f32[1,768,128]{2,1,0:T(8,128)S(1)} collective-permute-done((f32[1,768,128]{2,1,0:T(8,128)S(1)}, f32[1,768,128]{2,1,0:T(8,128)S(1)}, u32[]{:S(2)}, u32[]{:S(2)}) %collective-permute-start.3) | collective-permute-done | bytes 393248 | tf_op jit(solution)/shard_map/ppermute | solution.py:717
  224.7 6.2 collective-permute-done.25.refs_2_
  239.2 69.4 %collective-permute-done.17.refs_6_ = f32[768,128]{1,0:T(8,128)S(1)} collective-permute-done((f32[768,128]{1,0:T(8,128)S(1)}, f32[768,128]{1,0:T(8,128)S(1)}, u32[]{:S(2)}, u32[]{:S(2)}) %collective-permute-start.17) | collective-permute-done | bytes 393248 | tf_op jit(solution)/shard_map/ppermute | solution.py:717
  312.1 6.2 collective-permute-done.16.refs_5_
  319.1 1.5 collective-permute-start.6
  321.3 18.6 %score_stage.1 = (bf16[2,4,768,768]{3,2,1,0:T(8,128)(2,1)}, bf16[2,4,768,768]{3,2,1,0:T(8,128)(2,1)}, f32[2,768,128]{2,1,0:T(8,128)}) custom-call(s32[4]{0:T(128)} %dynamic_slice.17.reach_ref, s32[3]{0:T(128)} %pad_add_fusion.place_ref, f32[768,512]{1,0:T(8,128)} %get-tuple-element.52.refs_0_, f32[768,512]{1,0:T(8,128)} %collective-permute-done.2.refs_1_, ...), custom_call_target="tpu_custom_call" | custom-call | tf_op jit(solution)/shard_map/score_stage/pallas_call | solution.py:585
  340.0 14.4 %value_stage.1 = (f32[768,128]{1,0:T(8,128)}, f32[768,128]{1,0:T(8,128)}) custom-call(s32[4]{0:T(128)} %dynamic_slice.17.reach_ref, s32[3]{0:T(128)} %pad_add_fusion.place_ref, bf16[2,4,768,768]{3,2,1,0:T(8,128)(2,1)} %get-tuple-element.33.refs_0_, bf16[2,4,768,768]{3,2,1,0:T(8,128)(2,1)} %get-tuple-element.34.refs_1_, ...), custom_call_target="tpu_custom_call" | custom-call | tf_op jit(solution)/shard_map/value_stage/pallas_call | solution.py:611
  357.2 1.7 collective-permute-start.35
  358.9 19.8 %attend_stage.3 = (f32[768,128]{1,0:T(8,128)}, f32[768,128]{1,0:T(8,128)}) custom-call(s32[4]{0:T(128)} %dynamic_slice.17.reach_ref, s32[3]{0:T(128)} %pad_add_fusion.place_ref, f32[768,512]{1,0:T(8,128)} %get-tuple-element.52.refs_0_, f32[768,512]{1,0:T(8,128)} %collective-permute-done.2.refs_1_, f32[1,768,128]{2,1,0:T(8,128)} %copy-done.40, ...), custom_call_target="tpu_custom_call" | custom-call | tf_op jit(solution)/shard_map/attend_stage/pallas_call | solution.py:560
  378.7 17.8 %collective-permute-start.8 = (f32[768,128]{1,0:T(8,128)}, f32[768,128]{1,0:T(8,128)S(1)}, u32[]{:S(2)}, u32[]{:S(2)}) collective-permute-start(f32[768,128]{1,0:T(8,128)} %get-tuple-element.32), channel_id=1, source_target_pairs={{0,4},{4,0},{8,12},{12,8},{16,20},{20,16},{24,28},{28,24},{1,5},{5... | collective-permute-start | bytes 1179656 | tf_op jit(solution)/shard_map/ppermute | solution.py:717
  397.4 14.6 %attend_stage.4 = (f32[768,128]{1,0:T(8,128)}, f32[768,128]{1,0:T(8,128)}) custom-call(s32[4]{0:T(128)} %dynamic_slice.17.reach_ref, s32[3]{0:T(128)} %pad_add_fusion.place_ref, f32[768,512]{1,0:T(8,128)} %get-tuple-element.52.refs_0_, f32[768,512]{1,0:T(8,128)} %collective-permute-done.2.refs_1_, f32[1,768,128]{2,1,0:T(8,128)} %copy-done.39, ...), custom_call_target="tpu_custom_call" | custom-call | tf_op jit(solution)/shard_map/attend_stage/pallas_call | solution.py:560
  412.0 11.5 %collective-permute-start.29 = (f32[768,128]{1,0:T(8,128)}, f32[768,128]{1,0:T(8,128)S(1)}, u32[]{:S(2)}, u32[]{:S(2)}) collective-permute-start(f32[768,128]{1,0:T(8,128)} %get-tuple-element.39), channel_id=1, source_target_pairs={{0,4},{4,0},{8,12},{12,8},{16,20},{20,16},{24,28},{28,24},{1,5},{5... | collective-permute-start | bytes 1179656 | tf_op jit(solution)/shard_map/ppermute | solution.py:717
  423.6 1.7 collective-permute-start.46
  426.6 18.3 %collective-permute-start.18 = (f32[512,1024]{1,0:T(8,128)}, f32[512,1024]{1,0:T(8,128)S(1)}, u32[]{:S(2)}, u32[]{:S(2)}) collective-permute-start(f32[512,1024]{1,0:T(8,128)} %refs_4_), channel_id=1, source_target_pairs={{0,8},{4,12},{8,0},{12,4},{16,24},{20,28},{24,16},{28,20},{1,9},{5... | collective-permute-start | bytes 6291464 | tf_op jit(solution)/shard_map/ppermute | solution.py:717
  444.9 4.4 collective-permute-start.48
  449.4 14.7 %attend_stage.5 = (f32[768,128]{1,0:T(8,128)}, f32[768,128]{1,0:T(8,128)}) custom-call(s32[4]{0:T(128)} %dynamic_slice.17.reach_ref, s32[3]{0:T(128)} %pad_add_fusion.place_ref, f32[768,512]{1,0:T(8,128)} %get-tuple-element.52.refs_0_, f32[768,512]{1,0:T(8,128)} %collective-permute-done.2.refs_1_, f32[2,768,128]{2,1,0:T(8,128)} %copy-done.16, ...), custom_call_target="tpu_custom_call" | custom-call | tf_op jit(solution)/shard_map/attend_stage/pallas_call | solution.py:560
  464.1 10.4 %collective-permute-start.37 = (f32[768,128]{1,0:T(8,128)}, f32[768,128]{1,0:T(8,128)S(1)}, u32[]{:S(2)}, u32[]{:S(2)}) collective-permute-start(f32[768,128]{1,0:T(8,128)} %get-tuple-element.41), channel_id=1, source_target_pairs={{0,4},{4,0},{8,12},{12,8},{16,20},{20,16},{24,28},{28,24},{1,5},{5... | collective-permute-start | bytes 1179656 | tf_op jit(solution)/shard_map/ppermute | solution.py:717
  474.5 1.5 collective-permute-done.37
  476.0 3.4 collective-permute-start.30
  480.8 1.9 collective-permute-start.32
  483.9 14.0 %collective-permute-done.30.refs_1_ = f32[2,768,128]{2,1,0:T(8,128)S(1)} collective-permute-done((f32[2,768,128]{2,1,0:T(8,128)S(1)}, f32[2,768,128]{2,1,0:T(8,128)S(1)}, u32[]{:S(2)}, u32[]{:S(2)}) %collective-permute-start.30) | collective-permute-done | bytes 786464 | tf_op jit(solution)/shard_map/ppermute | solution.py:818
  497.9 9.8 %collective-permute-done.31.refs_2_ = f32[2,768,128]{2,1,0:T(8,128)} collective-permute-done((f32[2,768,128]{2,1,0:T(8,128)S(1)}, f32[2,768,128]{2,1,0:T(8,128)}, u32[]{:S(2)}, u32[]{:S(2)}) %collective-permute-start.31) | collective-permute-done | bytes 786464 | tf_op jit(solution)/shard_map/ppermute | solution.py:818
  507.6 6.1 collective-permute-start.38
  513.8 5.1 collective-permute-done.32.refs_4_
  520.1 12.0 %collective-permute-done.38.refs_1_ = f32[2,768,128]{2,1,0:T(8,128)S(1)} collective-permute-done((f32[2,768,128]{2,1,0:T(8,128)S(1)}, f32[2,768,128]{2,1,0:T(8,128)S(1)}, u32[]{:S(2)}, u32[]{:S(2)}) %collective-permute-start.38) | collective-permute-done | bytes 786464 | tf_op jit(solution)/shard_map/ppermute | solution.py:818
  532.1 6.0 collective-permute-start.40
  538.1 13.0 %collective-permute-done.39.refs_2_ = f32[2,768,128]{2,1,0:T(8,128)S(1)} collective-permute-done((f32[2,768,128]{2,1,0:T(8,128)S(1)}, f32[2,768,128]{2,1,0:T(8,128)S(1)}, u32[]{:S(2)}, u32[]{:S(2)}) %collective-permute-start.39) | collective-permute-done | bytes 786464 | tf_op jit(solution)/shard_map/ppermute | solution.py:818
  552.5 2.2 collective-permute-start.50
  554.8 13.1 %collective-permute-done.40.refs_4_ = f32[2,768,128]{2,1,0:T(8,128)S(1)} collective-permute-done((f32[2,768,128]{2,1,0:T(8,128)S(1)}, f32[2,768,128]{2,1,0:T(8,128)S(1)}, u32[]{:S(2)}, u32[]{:S(2)}) %collective-permute-start.40) | collective-permute-done | bytes 786464 | tf_op jit(solution)/shard_map/ppermute | solution.py:818
  567.9 2.8 collective-permute-done.49.refs_3_
  570.7 4.3 collective-permute-start.33
  575.0 12.5 %collective-permute-done.50.refs_5_ = f32[2,768,128]{2,1,0:T(8,128)} collective-permute-done((f32[2,768,128]{2,1,0:T(8,128)}, f32[2,768,128]{2,1,0:T(8,128)}, u32[]{:S(2)}, u32[]{:S(2)}) %collective-permute-start.50) | collective-permute-done | bytes 786464 | tf_op jit(solution)/shard_map/ppermute | solution.py:822
  588.1 4.4 collective-permute-start.41
  592.6 11.7 %collective-permute-done.33.refs_3_ = f32[2,768,128]{2,1,0:T(8,128)S(1)} collective-permute-done((f32[2,768,128]{2,1,0:T(8,128)S(1)}, f32[2,768,128]{2,1,0:T(8,128)S(1)}, u32[]{:S(2)}, u32[]{:S(2)}) %collective-permute-start.33) | collective-permute-done | bytes 786464 | tf_op jit(solution)/shard_map/ppermute | solution.py:822
  604.4 14.7 %collective-permute-done.41.refs_3_ = f32[2,768,128]{2,1,0:T(8,128)S(1)} collective-permute-done((f32[2,768,128]{2,1,0:T(8,128)S(1)}, f32[2,768,128]{2,1,0:T(8,128)S(1)}, u32[]{:S(2)}, u32[]{:S(2)}) %collective-permute-start.41) | collective-permute-done | bytes 786464 | tf_op jit(solution)/shard_map/ppermute | solution.py:822
  619.1 4.4 collective-permute-start.42
  623.5 1.9 collective-permute-done.20.refs_9_.refs_7_
  626.3 12.2 %collective-permute-done.42.refs_5_ = f32[2,768,128]{2,1,0:T(8,128)S(1)} collective-permute-done((f32[2,768,128]{2,1,0:T(8,128)S(1)}, f32[2,768,128]{2,1,0:T(8,128)S(1)}, u32[]{:S(2)}, u32[]{:S(2)}) %collective-permute-start.42) | collective-permute-done | bytes 786464 | tf_op jit(solution)/shard_map/ppermute | solution.py:822
  638.5 5.5 collective-permute-start.34
  644.2 1.7 collective-permute-start.10
  645.9 1.3 copy-done.8
  647.3 1.8 collective-permute-start.11
  649.1 10.9 %product_stage.4.refs_14_ = f32[768,1024]{1,0:T(8,128)} custom-call(s32[3]{0:T(128)} %pad_add_fusion.place_ref, f32[2,768,128]{2,1,0:T(8,128)} %copy-done.13, f32[2,768,128]{2,1,0:T(8,128)} %copy-done.21, f32[2,768,128]{2,1,0:T(8,128)} %collective-permute-done.47.refs_2_, f32[2,768,128]{2,1,0:T(8,128)} %copy-done.28, ...), custom_call_target="tpu_custom_call" | custom-call | tf_op jit(solution)/shard_map/product_stage/pallas_call | solution.py:673
  660.0 11.6 %product_stage.5.refs_14_ = f32[768,1024]{1,0:T(8,128)} custom-call(s32[3]{0:T(128)} %pad_add_fusion.place_ref, f32[2,768,128]{2,1,0:T(8,128)} %copy-done.15, f32[2,768,128]{2,1,0:T(8,128)} %copy-done.24, f32[2,768,128]{2,1,0:T(8,128)} %copy-done.25, f32[2,768,128]{2,1,0:T(8,128)} %copy-done.29, f32[2,768,128]{2,1,0:T(8,128)} %copy-done.26, ...), custom_call_target="tpu_custom_call" | custom-call | tf_op jit(solution)/shard_map/product_stage/pallas_call | solution.py:673
  671.5 5.9 collective-permute-done.34.refs_5_
  677.5 11.5 %product_stage.6.refs_12_ = f32[768,1024]{1,0:T(8,128)} custom-call(s32[3]{0:T(128)} %pad_add_fusion.place_ref, f32[2,768,128]{2,1,0:T(8,128)} %copy-done.14, f32[2,768,128]{2,1,0:T(8,128)} %copy-done.22, f32[2,768,128]{2,1,0:T(8,128)} %collective-permute-done.31.refs_2_, f32[2,768,128]{2,1,0:T(8,128)} %copy-done.27, f32[2,768,128]{2,1,0:T(8,128)} %copy-done.23, ...), custom_call_target="tpu_custom_call" | custom-call | tf_op jit(solution)/shard_map/product_stage/pallas_call | solution.py:673
  688.9 19.0 %collective-permute-done.9.refs_1_ = f32[2,768,128]{2,1,0:T(8,128)} collective-permute-done((f32[2,768,128]{2,1,0:T(8,128)}, f32[2,768,128]{2,1,0:T(8,128)}, u32[]{:S(2)}, u32[]{:S(2)}) %collective-permute-start.9) | collective-permute-done | bytes 786464 | tf_op jit(solution)/shard_map/ppermute | solution.py:818
  708.0 4.6 collective-permute-done.11.refs_3_
  713.5 10.9 %product_stage.7 = f32[768,1024]{1,0:T(8,128)} custom-call(s32[3]{0:T(128)} %pad_add_fusion.place_ref, f32[2,768,128]{2,1,0:T(8,128)} %pad_maximum_fusion.3.refs_0_, f32[2,768,128]{2,1,0:T(8,128)} %collective-permute-done.9.refs_1_, f32[2,768,128]{2,1,0:T(8,128)} %copy-done.31, f32[2,768,128]{2,1,0:T(8,128)} %copy-done.32, f32[512,1024]{1,0:T(8,128)} %refs_4_, ...), custom_call_target="tpu_custom_call" | custom-call | tf_op jit(solution)/shard_map/product_stage/pallas_call | solution.py:673
  (178 shorter events, 37.6 us)
Async XLA Ops:
  0.6 60.4 %all-to-all-start.1 = ((f32[8,128,768]{2,1,0:T(8,128)}), f32[8,128,768]{2,1,0:T(8,128)S(1)}, u32[]{:S(2)}, u32[]{:S(2)}) async-start(f32[8,128,768]{2,1,0:T(8,128)} %bitcast.57), calls=%async_computation.1 | async-start | bytes 6291456 | tf_op jit(solution)/shard_map/all_to_all | solution.py:761
  6.1 39.9 %collective-permute-start = (f32[128,1024]{1,0:T(8,128)S(1)}, f32[128,1024]{1,0:T(8,128)S(1)}, u32[]{:S(2)}, u32[]{:S(2)}) collective-permute-start(f32[128,1024]{1,0:T(8,128)S(1)} %slice_multiply_fusion), channel_id=1, source_target_pairs={{0,4},{4,8},{8,12},{12,16},{16,20},{20,24},{24,28},{1,5},{5,9},{9,... | collective-permute-start | bytes 1572872 | tf_op jit(solution)/shard_map/ppermute | solution.py:717
  62.8 39.8 %all-to-all-start = ((f32[8,768,128]{2,1,0:T(8,128)}), f32[8,768,128]{2,1,0:T(8,128)}, u32[]{:S(2)}, u32[]{:S(2)}) async-start(f32[8,768,128]{2,1,0:T(8,128)} %get-tuple-element.24), calls=%async_computation | async-start | bytes 6291456 | tf_op jit(solution)/shard_map/all_to_all | solution.py:765
  69.4 119.4 %copy-start = (f32[768,512]{1,0:T(8,128)}, f32[768,512]{1,0:T(8,128)S(1)}, u32[]{:S(2)}) copy-start(f32[768,512]{1,0:T(8,128)S(1)} %get-tuple-element.28.refs_5_) | copy-start | bytes 4718596
  69.4 19.1 %collective-permute-start.1 = (f32[768,512]{1,0:T(8,128)S(1)}, f32[768,512]{1,0:T(8,128)S(1)}, u32[]{:S(2)}, u32[]{:S(2)}) collective-permute-start(f32[768,512]{1,0:T(8,128)S(1)} %get-tuple-element.53), channel_id=1, source_target_pairs={{0,4},{4,0},{8,12},{12,8},{16,20},{20,16},{24,28},{28,24},{1,5},{5... | collective-permute-start | bytes 4718600 | tf_op jit(solution)/shard_map/ppermute | solution.py:717
  88.5 100.4 %copy-start.4 = (f32[768,512]{1,0:T(8,128)}, f32[768,512]{1,0:T(8,128)S(1)}, u32[]{:S(2)}) copy-start(f32[768,512]{1,0:T(8,128)S(1)} %collective-permute-done.1.refs_6_) | copy-start | bytes 4718596
  137.3 42.3 %all-to-all-start.2 = ((f32[8,768,128]{2,1,0:T(8,128)}), f32[8,768,128]{2,1,0:T(8,128)}, u32[]{:S(2)}, u32[]{:S(2)}) async-start(f32[8,768,128]{2,1,0:T(8,128)} %bitcast.56), calls=%async_computation.2 | async-start | bytes 6291456 | tf_op jit(solution)/shard_map/all_to_all | solution.py:784
  147.9 45.6 %collective-permute-start.2 = (f32[768,512]{1,0:T(8,128)}, f32[768,512]{1,0:T(8,128)}, u32[]{:S(2)}, u32[]{:S(2)}) collective-permute-start(f32[768,512]{1,0:T(8,128)} %get-tuple-element.51), channel_id=1, source_target_pairs={{0,4},{4,0},{8,12},{12,8},{16,20},{20,16},{24,28},{28,24},{1,5},{5... | collective-permute-start | bytes 4718600 | tf_op jit(solution)/shard_map/ppermute | solution.py:717
  188.8 44.7 %collective-permute-start.5 = (f32[768,512]{1,0:T(8,128)}, f32[768,512]{1,0:T(8,128)S(1)}, u32[]{:S(2)}, u32[]{:S(2)}) collective-permute-start(f32[768,512]{1,0:T(8,128)} %get-tuple-element.29), channel_id=1, source_target_pairs={{0,4},{4,0},{8,12},{12,8},{16,20},{20,16},{24,28},{28,24},{1,5},{5... | collective-permute-start | bytes 4718600 | tf_op jit(solution)/shard_map/ppermute | solution.py:717
  189.4 46.8 %collective-permute-start.13 = (f32[4,768,128]{2,1,0:T(8,128)S(1)}, f32[4,768,128]{2,1,0:T(8,128)S(1)}, u32[]{:S(2)}, u32[]{:S(2)}) collective-permute-start(f32[4,768,128]{2,1,0:T(8,128)S(1)} %pad_maximum_fusion), channel_id=1, source_target_pairs={{0,8},{4,12},{8,16},{12,20},{16,24},{20,28},{1,9},{5,13},{9,17},{1... | collective-permute-start | bytes 4718600 | tf_op jit(solution)/shard_map/ppermute | solution.py:717
  190.8 41.4 %collective-permute-start.12 = (f32[2,768,128]{2,1,0:T(8,128)S(1)}, f32[2,768,128]{2,1,0:T(8,128)S(1)}, u32[]{:S(2)}, u32[]{:S(2)}) collective-permute-start(f32[2,768,128]{2,1,0:T(8,128)S(1)} %pad_maximum_fusion.4), channel_id=1, source_target_pairs={{0,16},{4,20},{8,24},{12,28},{1,17},{5,21},{9,25},{13,29},{2,18},{... | collective-permute-start | bytes 2359304 | tf_op jit(solution)/shard_map/ppermute | solution.py:717
  192.2 30.3 %collective-permute-start.3 = (f32[1,768,128]{2,1,0:T(8,128)S(1)}, f32[1,768,128]{2,1,0:T(8,128)S(1)}, u32[]{:S(2)}, u32[]{:S(2)}) collective-permute-start(f32[1,768,128]{2,1,0:T(8,128)S(1)} %get-tuple-element.69), channel_id=1, source_target_pairs={{0,16},{4,20},{8,24},{12,28},{1,17},{5,21},{9,25},{13,29},{2,18},{... | collective-permute-start | bytes 1179656 | tf_op jit(solution)/shard_map/ppermute | solution.py:717
  193.5 37.4 %collective-permute-start.25 = (f32[1,768,128]{2,1,0:T(8,128)S(1)}, f32[1,768,128]{2,1,0:T(8,128)S(1)}, u32[]{:S(2)}, u32[]{:S(2)}) collective-permute-start(f32[1,768,128]{2,1,0:T(8,128)S(1)} %get-tuple-element.72), channel_id=1, source_target_pairs={{0,16},{4,20},{8,24},{12,28},{1,17},{5,21},{9,25},{13,29},{2,18},{... | collective-permute-start | bytes 1179656 | tf_op jit(solution)/shard_map/ppermute | solution.py:717
  222.5 14.4 %collective-permute-start.15 = (f32[768,128]{1,0:T(8,128)S(1)}, f32[768,128]{1,0:T(8,128)S(1)}, u32[]{:S(2)}, u32[]{:S(2)}) collective-permute-start(f32[768,128]{1,0:T(8,128)S(1)} %slice.87), channel_id=1, source_target_pairs={{4,16},{12,24},{5,17},{13,25},{6,18},{14,26},{7,19},{15,27}} | collective-permute-start | bytes 1179656 | tf_op jit(solution)/shard_map/ppermute | solution.py:717
  230.9 123.5 %collective-permute-start.4 = (f32[2,768,128]{2,1,0:T(8,128)}, f32[2,768,128]{2,1,0:T(8,128)}, u32[]{:S(2)}, u32[]{:S(2)}) collective-permute-start(f32[2,768,128]{2,1,0:T(8,128)} %pad_maximum_fusion.1), channel_id=1, source_target_pairs={{0,8},{4,12},{8,16},{12,20},{16,24},{20,28},{1,9},{5,13},{9,17},{1... | collective-permute-start | bytes 2359304 | tf_op jit(solution)/shard_map/ppermute | solution.py:717
  232.2 123.5 %collective-permute-start.26 = (f32[2,768,128]{2,1,0:T(8,128)}, f32[2,768,128]{2,1,0:T(8,128)S(1)}, u32[]{:S(2)}, u32[]{:S(2)}) collective-permute-start(f32[2,768,128]{2,1,0:T(8,128)} %pad_maximum_fusion.5), channel_id=1, source_target_pairs={{0,8},{4,12},{8,16},{12,20},{16,24},{20,28},{1,9},{5,13},{9,17},{1... | collective-permute-start | bytes 2359304 | tf_op jit(solution)/shard_map/ppermute | solution.py:717
  233.6 75.0 %collective-permute-start.17 = (f32[768,128]{1,0:T(8,128)S(1)}, f32[768,128]{1,0:T(8,128)S(1)}, u32[]{:S(2)}, u32[]{:S(2)}) collective-permute-start(f32[768,128]{1,0:T(8,128)S(1)} %slice.87), channel_id=1, source_target_pairs={{0,12},{8,20},{16,28},{4,8},{12,16},{20,24},{1,13},{9,21},{17,29},... | collective-permute-start | bytes 1179656 | tf_op jit(solution)/shard_map/ppermute | solution.py:717
  236.2 84.5 %copy-start.49 = (s32[8]{0:T(128)S(1)}, s32[8]{0:T(128)}, u32[]{:S(2)}) copy-start(s32[8]{0:T(128)} %param.34) | copy-start | bytes 100
  236.2 85.1 %copy-start.9 = (f32[4,768,128]{2,1,0:T(8,128)}, f32[4,768,128]{2,1,0:T(8,128)S(1)}, u32[]{:S(2)}) copy-start(f32[4,768,128]{2,1,0:T(8,128)S(1)} %collective-permute-done.13.refs_3_.refs_4_) | copy-start | bytes 4718596
  236.2 74.6 %collective-permute-start.14 = (f32[768,128]{1,0:T(8,128)S(1)}, f32[768,128]{1,0:T(8,128)S(1)}, u32[]{:S(2)}, u32[]{:S(2)}) collective-permute-start(f32[768,128]{1,0:T(8,128)S(1)} %get-tuple-element.64), channel_id=1, source_target_pairs={{4,20},{12,28},{5,21},{13,29},{6,22},{14,30},{7,23},{15,31}} | collective-permute-start | bytes 1179656 | tf_op jit(solution)/shard_map/ppermute | solution.py:717
  236.9 81.5 %collective-permute-start.16 = (f32[768,128]{1,0:T(8,128)S(1)}, f32[768,128]{1,0:T(8,128)S(1)}, u32[]{:S(2)}, u32[]{:S(2)}) collective-permute-start(f32[768,128]{1,0:T(8,128)S(1)} %get-tuple-element.64), channel_id=1, source_target_pairs={{0,8},{4,12},{8,16},{12,20},{16,24},{20,28},{1,9},{5,13},{9,17},{1... | collective-permute-start | bytes 1179656 | tf_op jit(solution)/shard_map/ppermute | solution.py:717
  308.5 48.7 %collective-permute-start.7 = (f32[2,768,128]{2,1,0:T(8,128)}, f32[2,768,128]{2,1,0:T(8,128)}, u32[]{:S(2)}, u32[]{:S(2)}) collective-permute-start(f32[2,768,128]{2,1,0:T(8,128)} %pad_maximum_fusion.2), channel_id=1, source_target_pairs={{0,8},{4,12},{8,16},{12,20},{16,24},{20,28},{1,9},{5,13},{9,17},{1... | collective-permute-start | bytes 2359304 | tf_op jit(solution)/shard_map/ppermute | solution.py:717
  310.8 85.7 %collective-permute-start.28 = (f32[2,768,128]{2,1,0:T(8,128)}, f32[2,768,128]{2,1,0:T(8,128)S(1)}, u32[]{:S(2)}, u32[]{:S(2)}) collective-permute-start(f32[2,768,128]{2,1,0:T(8,128)} %pad_maximum_fusion.6), channel_id=1, source_target_pairs={{0,8},{4,12},{8,16},{12,20},{16,24},{20,28},{1,9},{5,13},{9,17},{1... | collective-permute-start | bytes 2359304 | tf_op jit(solution)/shard_map/ppermute | solution.py:717
  319.1 36.7 %collective-permute-start.6 = (f32[1,768,128]{2,1,0:T(8,128)}, f32[1,768,128]{2,1,0:T(8,128)}, u32[]{:S(2)}, u32[]{:S(2)}) collective-permute-start(f32[1,768,128]{2,1,0:T(8,128)} %get-tuple-element.58), channel_id=1, source_target_pairs={{0,16},{4,20},{8,24},{12,28},{1,17},{5,21},{9,25},{13,29},{2,18},{... | collective-permute-start | bytes 1179656 | tf_op jit(solution)/shard_map/ppermute | solution.py:717
  354.4 24.3 %collective-permute-start.27 = (f32[1,768,128]{2,1,0:T(8,128)S(1)}, f32[1,768,128]{2,1,0:T(8,128)S(1)}, u32[]{:S(2)}, u32[]{:S(2)}) collective-permute-start(f32[1,768,128]{2,1,0:T(8,128)S(1)} %copy-done.42), channel_id=1, source_target_pairs={{0,16},{4,20},{8,24},{12,28},{1,17},{5,21},{9,25},{13,29},{2,18},{... | collective-permute-start | bytes 1179656 | tf_op jit(solution)/shard_map/ppermute | solution.py:717
  355.7 67.8 %collective-permute-start.45 = (f32[768,128]{1,0:T(8,128)}, f32[768,128]{1,0:T(8,128)S(1)}, u32[]{:S(2)}, u32[]{:S(2)}) collective-permute-start(f32[768,128]{1,0:T(8,128)} %get-tuple-element.43), channel_id=1, source_target_pairs={{0,4},{4,0},{8,12},{12,8},{16,20},{20,16},{24,28},{28,24},{1,5},{5... | collective-permute-start | bytes 1179656 | tf_op jit(solution)/shard_map/ppermute | solution.py:717
  355.9 70.7 %collective-permute-start.36 = (f32[2,768,128]{2,1,0:T(8,128)S(1)}, f32[2,768,128]{2,1,0:T(8,128)S(1)}, u32[]{:S(2)}, u32[]{:S(2)}) collective-permute-start(f32[2,768,128]{2,1,0:T(8,128)S(1)} %pad_maximum_fusion.8), channel_id=1, source_target_pairs={{0,8},{4,12},{8,16},{12,20},{16,24},{20,28},{1,9},{5,13},{9,17},{1... | collective-permute-start | bytes 2359304 | tf_op jit(solution)/shard_map/ppermute | solution.py:717
  357.2 68.1 %collective-permute-start.35 = (f32[1,768,128]{2,1,0:T(8,128)S(1)}, f32[1,768,128]{2,1,0:T(8,128)S(1)}, u32[]{:S(2)}, u32[]{:S(2)}) collective-permute-start(f32[1,768,128]{2,1,0:T(8,128)S(1)} %copy-done.41), channel_id=1, source_target_pairs={{0,16},{4,20},{8,24},{12,28},{1,17},{5,21},{9,25},{13,29},{2,18},{... | collective-permute-start | bytes 1179656 | tf_op jit(solution)/shard_map/ppermute | solution.py:717
  378.7 66.2 %collective-permute-start.8 = (f32[768,128]{1,0:T(8,128)}, f32[768,128]{1,0:T(8,128)S(1)}, u32[]{:S(2)}, u32[]{:S(2)}) collective-permute-start(f32[768,128]{1,0:T(8,128)} %get-tuple-element.32), channel_id=1, source_target_pairs={{0,4},{4,0},{8,12},{12,8},{16,20},{20,16},{24,28},{28,24},{1,5},{5... | collective-permute-start | bytes 1179656 | tf_op jit(solution)/shard_map/ppermute | solution.py:717
  412.0 52.1 %collective-permute-start.29 = (f32[768,128]{1,0:T(8,128)}, f32[768,128]{1,0:T(8,128)S(1)}, u32[]{:S(2)}, u32[]{:S(2)}) collective-permute-start(f32[768,128]{1,0:T(8,128)} %get-tuple-element.39), channel_id=1, source_target_pairs={{0,4},{4,0},{8,12},{12,8},{16,20},{20,16},{24,28},{28,24},{1,5},{5... | collective-permute-start | bytes 1179656 | tf_op jit(solution)/shard_map/ppermute | solution.py:717
  423.6 55.9 %collective-permute-start.46 = (f32[2,768,128]{2,1,0:T(8,128)S(1)}, f32[2,768,128]{2,1,0:T(8,128)S(1)}, u32[]{:S(2)}, u32[]{:S(2)}) collective-permute-start(f32[2,768,128]{2,1,0:T(8,128)S(1)} %pad_maximum_fusion.10.refs_0_), channel_id=1, source_target_pairs={{0,1},{1,0},{2,3},{3,2},{4,5},{5,4},{6,7},{7,6},{8,9},{9,8},{10,11... | collective-permute-start | bytes 2359304 | tf_op jit(solution)/shard_map/ppermute | solution.py:818
  425.3 55.4 %collective-permute-start.47 = (f32[2,768,128]{2,1,0:T(8,128)S(1)}, f32[2,768,128]{2,1,0:T(8,128)}, u32[]{:S(2)}, u32[]{:S(2)}) collective-permute-start(f32[2,768,128]{2,1,0:T(8,128)S(1)} %pad_maximum_fusion.10.refs_0_), channel_id=1, source_target_pairs={{0,2},{3,1},{4,6},{7,5},{8,10},{11,9},{12,14},{15,13},{16,18},{19,... | collective-permute-start | bytes 2359304 | tf_op jit(solution)/shard_map/ppermute | solution.py:818
  426.6 125.9 %collective-permute-start.18 = (f32[512,1024]{1,0:T(8,128)}, f32[512,1024]{1,0:T(8,128)S(1)}, u32[]{:S(2)}, u32[]{:S(2)}) collective-permute-start(f32[512,1024]{1,0:T(8,128)} %refs_4_), channel_id=1, source_target_pairs={{0,8},{4,12},{8,0},{12,4},{16,24},{20,28},{24,16},{28,20},{1,9},{5... | collective-permute-start | bytes 6291464 | tf_op jit(solution)/shard_map/ppermute | solution.py:717
  444.9 37.8 %collective-permute-start.48 = (f32[2,768,128]{2,1,0:T(8,128)S(1)}, f32[2,768,128]{2,1,0:T(8,128)}, u32[]{:S(2)}, u32[]{:S(2)}) collective-permute-start(f32[2,768,128]{2,1,0:T(8,128)S(1)} %pad_maximum_fusion.10.refs_0_), channel_id=1, source_target_pairs={{1,2},{2,1},{5,6},{6,5},{9,10},{10,9},{13,14},{14,13},{17,18},{18,... | collective-permute-start | bytes 2359304 | tf_op jit(solution)/shard_map/ppermute | solution.py:818
  464.1 11.9 %collective-permute-start.37 = (f32[768,128]{1,0:T(8,128)}, f32[768,128]{1,0:T(8,128)S(1)}, u32[]{:S(2)}, u32[]{:S(2)}) collective-permute-start(f32[768,128]{1,0:T(8,128)} %get-tuple-element.41), channel_id=1, source_target_pairs={{0,4},{4,0},{8,12},{12,8},{16,20},{20,16},{24,28},{28,24},{1,5},{5... | collective-permute-start | bytes 1179656 | tf_op jit(solution)/shard_map/ppermute | solution.py:717
  474.5 80.3 %copy-start.14 = (f32[2,768,128]{2,1,0:T(8,128)}, f32[2,768,128]{2,1,0:T(8,128)S(1)}, u32[]{:S(2)}) copy-start(f32[2,768,128]{2,1,0:T(8,128)S(1)} %pad_maximum_fusion.7.refs_0_) | copy-start | bytes 2359300
  476.0 21.8 %collective-permute-start.30 = (f32[2,768,128]{2,1,0:T(8,128)S(1)}, f32[2,768,128]{2,1,0:T(8,128)S(1)}, u32[]{:S(2)}, u32[]{:S(2)}) collective-permute-start(f32[2,768,128]{2,1,0:T(8,128)S(1)} %pad_maximum_fusion.7.refs_0_), channel_id=1, source_target_pairs={{0,1},{1,0},{2,3},{3,2},{4,5},{5,4},{6,7},{7,6},{8,9},{9,8},{10,11... | collective-permute-start | bytes 2359304 | tf_op jit(solution)/shard_map/ppermute | solution.py:818
  479.5 28.1 %collective-permute-start.31 = (f32[2,768,128]{2,1,0:T(8,128)S(1)}, f32[2,768,128]{2,1,0:T(8,128)}, u32[]{:S(2)}, u32[]{:S(2)}) collective-permute-start(f32[2,768,128]{2,1,0:T(8,128)S(1)} %pad_maximum_fusion.7.refs_0_), channel_id=1, source_target_pairs={{0,2},{3,1},{4,6},{7,5},{8,10},{11,9},{12,14},{15,13},{16,18},{19,... | collective-permute-start | bytes 2359304 | tf_op jit(solution)/shard_map/ppermute | solution.py:818
  480.8 38.0 %collective-permute-start.32 = (f32[2,768,128]{2,1,0:T(8,128)S(1)}, f32[2,768,128]{2,1,0:T(8,128)S(1)}, u32[]{:S(2)}, u32[]{:S(2)}) collective-permute-start(f32[2,768,128]{2,1,0:T(8,128)S(1)} %pad_maximum_fusion.7.refs_0_), channel_id=1, source_target_pairs={{1,2},{2,1},{5,6},{6,5},{9,10},{10,9},{13,14},{14,13},{17,18},{18,... | collective-permute-start | bytes 2359304 | tf_op jit(solution)/shard_map/ppermute | solution.py:818
  482.7 104.8 %collective-permute-start.19 = (f32[512,1024]{1,0:T(8,128)}, f32[512,1024]{1,0:T(8,128)S(1)}, u32[]{:S(2)}, u32[]{:S(2)}) collective-permute-start(f32[512,1024]{1,0:T(8,128)} %refs_4_), channel_id=1, source_target_pairs={{0,16},{4,20},{8,24},{12,28},{16,0},{20,4},{24,8},{28,12},{1,17},{... | collective-permute-start | bytes 6291464 | tf_op jit(solution)/shard_map/ppermute | solution.py:717
  483.9 176.1 %copy-start.15 = (f32[2,768,128]{2,1,0:T(8,128)}, f32[2,768,128]{2,1,0:T(8,128)S(1)}, u32[]{:S(2)}) copy-start(f32[2,768,128]{2,1,0:T(8,128)S(1)} %pad_maximum_fusion.9.refs_0_) | copy-start | bytes 2359300
  483.9 141.5 %copy-start.34 = (f32[768,128]{1,0:T(8,128)S(1)}, f32[768,128]{1,0:T(8,128)}, u32[]{:S(2)}) copy-start(f32[768,128]{1,0:T(8,128)} %get-tuple-element.31) | copy-start | bytes 1179652
  483.9 141.5 %copy-start.36 = (f32[768,128]{1,0:T(8,128)S(1)}, f32[768,128]{1,0:T(8,128)}, u32[]{:S(2)}) copy-start(f32[768,128]{1,0:T(8,128)} %copy-done.35) | copy-start | bytes 1179652
  497.9 90.2 %collective-permute-start.21 = (f32[512,1024]{1,0:T(8,128)}, f32[512,1024]{1,0:T(8,128)S(1)}, u32[]{:S(2)}, u32[]{:S(2)}) collective-permute-start(f32[512,1024]{1,0:T(8,128)} %refs_4_), channel_id=1, source_target_pairs={{0,4},{4,0},{8,12},{12,8},{16,20},{20,16},{24,28},{28,24},{1,5},{5... | collective-permute-start | bytes 6291464 | tf_op jit(solution)/shard_map/ppermute | solution.py:717
  507.6 24.5 %collective-permute-start.38 = (f32[2,768,128]{2,1,0:T(8,128)S(1)}, f32[2,768,128]{2,1,0:T(8,128)S(1)}, u32[]{:S(2)}, u32[]{:S(2)}) collective-permute-start(f32[2,768,128]{2,1,0:T(8,128)S(1)} %pad_maximum_fusion.9.refs_0_), channel_id=1, source_target_pairs={{0,1},{1,0},{2,3},{3,2},{4,5},{5,4},{6,7},{7,6},{8,9},{9,8},{10,11... | collective-permute-start | bytes 2359304 | tf_op jit(solution)/shard_map/ppermute | solution.py:818
  518.8 127.0 %copy-start.23 = (f32[2,768,128]{2,1,0:T(8,128)}, f32[2,768,128]{2,1,0:T(8,128)S(1)}, u32[]{:S(2)}) copy-start(f32[2,768,128]{2,1,0:T(8,128)S(1)} %collective-permute-done.32.refs_4_) | copy-start | bytes 2359300
  518.8 32.3 %collective-permute-start.39 = (f32[2,768,128]{2,1,0:T(8,128)S(1)}, f32[2,768,128]{2,1,0:T(8,128)S(1)}, u32[]{:S(2)}, u32[]{:S(2)}) collective-permute-start(f32[2,768,128]{2,1,0:T(8,128)S(1)} %pad_maximum_fusion.9.refs_0_), channel_id=1, source_target_pairs={{0,2},{3,1},{4,6},{7,5},{8,10},{11,9},{12,14},{15,13},{16,18},{19,... | collective-permute-start | bytes 2359304 | tf_op jit(solution)/shard_map/ppermute | solution.py:818
  532.1 35.8 %collective-permute-start.40 = (f32[2,768,128]{2,1,0:T(8,128)S(1)}, f32[2,768,128]{2,1,0:T(8,128)S(1)}, u32[]{:S(2)}, u32[]{:S(2)}) collective-permute-start(f32[2,768,128]{2,1,0:T(8,128)S(1)} %pad_maximum_fusion.9.refs_0_), channel_id=1, source_target_pairs={{1,2},{2,1},{5,6},{6,5},{9,10},{10,9},{13,14},{14,13},{17,18},{18,... | collective-permute-start | bytes 2359304 | tf_op jit(solution)/shard_map/ppermute | solution.py:818
  551.2 94.7 %copy-start.25 = (f32[2,768,128]{2,1,0:T(8,128)}, f32[2,768,128]{2,1,0:T(8,128)S(1)}, u32[]{:S(2)}) copy-start(f32[2,768,128]{2,1,0:T(8,128)S(1)} %collective-permute-done.39.refs_2_) | copy-start | bytes 2359300
  551.2 19.5 %collective-permute-start.49 = (f32[2,768,128]{2,1,0:T(8,128)}, f32[2,768,128]{2,1,0:T(8,128)S(1)}, u32[]{:S(2)}, u32[]{:S(2)}) collective-permute-start(f32[2,768,128]{2,1,0:T(8,128)} %collective-permute-done.48.refs_4_), channel_id=1, source_target_pairs={{1,0},{2,3},{5,4},{6,7},{9,8},{10,11},{13,12},{14,15},{17,16},{18,... | collective-permute-start | bytes 2359304 | tf_op jit(solution)/shard_map/ppermute | solution.py:822
  552.5 35.0 %collective-permute-start.50 = (f32[2,768,128]{2,1,0:T(8,128)}, f32[2,768,128]{2,1,0:T(8,128)}, u32[]{:S(2)}, u32[]{:S(2)}) collective-permute-start(f32[2,768,128]{2,1,0:T(8,128)} %collective-permute-done.47.refs_2_), channel_id=1, source_target_pairs={{1,0},{2,3},{5,4},{6,7},{9,8},{10,11},{13,12},{14,15},{17,16},{18,... | collective-permute-start | bytes 2359304 | tf_op jit(solution)/shard_map/ppermute | solution.py:822
  567.9 36.4 %collective-permute-start.43 = (f32[256,1024]{1,0:T(8,128)S(1)}, f32[256,1024]{1,0:T(8,128)S(1)}, u32[]{:S(2)}, u32[]{:S(2)}) collective-permute-start(f32[256,1024]{1,0:T(8,128)S(1)} %slice.100), channel_id=1, source_target_pairs={{0,16},{4,20},{8,24},{12,28},{16,0},{20,4},{24,8},{28,12},{1,17},{... | collective-permute-start | bytes 3145736 | tf_op jit(solution)/shard_map/ppermute | solution.py:717
  570.7 33.6 %collective-permute-start.33 = (f32[2,768,128]{2,1,0:T(8,128)S(1)}, f32[2,768,128]{2,1,0:T(8,128)S(1)}, u32[]{:S(2)}, u32[]{:S(2)}) collective-permute-start(f32[2,768,128]{2,1,0:T(8,128)S(1)} %collective-permute-done.32.refs_4_), channel_id=1, source_target_pairs={{1,0},{2,3},{5,4},{6,7},{9,8},{10,11},{13,12},{14,15},{17,16},{18,... | collective-permute-start | bytes 2359304 | tf_op jit(solution)/shard_map/ppermute | solution.py:822
  587.5 56.6 %collective-permute-start.22 = (f32[512,1024]{1,0:T(8,128)S(1)}, f32[512,1024]{1,0:T(8,128)S(1)}, u32[]{:S(2)}, u32[]{:S(2)}) collective-permute-start(f32[512,1024]{1,0:T(8,128)S(1)} %collective-permute-done.18.refs_7_.refs_5_), channel_id=1, source_target_pairs={{0,4},{4,0},{8,12},{12,8},{16,20},{20,16},{24,28},{28,24},{1,5},{5... | collective-permute-start | bytes 6291464 | tf_op jit(solution)/shard_map/ppermute | solution.py:717
  587.5 58.3 %collective-permute-start.23 = (f32[512,1024]{1,0:T(8,128)S(1)}, f32[512,1024]{1,0:T(8,128)S(1)}, u32[]{:S(2)}, u32[]{:S(2)}) collective-permute-start(f32[512,1024]{1,0:T(8,128)S(1)} %collective-permute-done.19.refs_8_.refs_6_), channel_id=1, source_target_pairs={{0,4},{4,0},{8,12},{12,8},{16,20},{20,16},{24,28},{28,24},{1,5},{5... | collective-permute-start | bytes 6291464 | tf_op jit(solution)/shard_map/ppermute | solution.py:717
  588.1 31.0 %collective-permute-start.41 = (f32[2,768,128]{2,1,0:T(8,128)S(1)}, f32[2,768,128]{2,1,0:T(8,128)S(1)}, u32[]{:S(2)}, u32[]{:S(2)}) collective-permute-start(f32[2,768,128]{2,1,0:T(8,128)S(1)} %collective-permute-done.40.refs_4_), channel_id=1, source_target_pairs={{1,0},{2,3},{5,4},{6,7},{9,8},{10,11},{13,12},{14,15},{17,16},{18,... | collective-permute-start | bytes 2359304 | tf_op jit(solution)/shard_map/ppermute | solution.py:822
  604.3 21.1 %collective-permute-start.20 = (f32[256,1024]{1,0:T(8,128)S(1)}, f32[256,1024]{1,0:T(8,128)}, u32[]{:S(2)}, u32[]{:S(2)}) collective-permute-start(f32[256,1024]{1,0:T(8,128)S(1)} %slice.97), channel_id=1, source_target_pairs={{0,8},{4,12},{8,0},{12,4},{16,24},{20,28},{24,16},{28,20},{1,9},{5... | collective-permute-start | bytes 3145736 | tf_op jit(solution)/shard_map/ppermute | solution.py:717
  604.3 39.7 %collective-permute-start.44 = (f32[256,1024]{1,0:T(8,128)S(1)}, f32[256,1024]{1,0:T(8,128)S(1)}, u32[]{:S(2)}, u32[]{:S(2)}) collective-permute-start(f32[256,1024]{1,0:T(8,128)S(1)} %collective-permute-done.43.refs_9_), channel_id=1, source_target_pairs={{0,4},{4,0},{8,12},{12,8},{16,20},{20,16},{24,28},{28,24},{1,5},{5... | collective-permute-start | bytes 3145736 | tf_op jit(solution)/shard_map/ppermute | solution.py:717
  619.1 19.5 %collective-permute-start.42 = (f32[2,768,128]{2,1,0:T(8,128)S(1)}, f32[2,768,128]{2,1,0:T(8,128)S(1)}, u32[]{:S(2)}, u32[]{:S(2)}) collective-permute-start(f32[2,768,128]{2,1,0:T(8,128)S(1)} %collective-permute-done.39.refs_2_), channel_id=1, source_target_pairs={{1,0},{2,3},{5,4},{6,7},{9,8},{10,11},{13,12},{14,15},{17,16},{18,... | collective-permute-start | bytes 2359304 | tf_op jit(solution)/shard_map/ppermute | solution.py:822
  625.4 52.1 %collective-permute-start.24 = (f32[256,1024]{1,0:T(8,128)}, f32[256,1024]{1,0:T(8,128)}, u32[]{:S(2)}, u32[]{:S(2)}) collective-permute-start(f32[256,1024]{1,0:T(8,128)} %collective-permute-done.20.refs_9_.refs_7_), channel_id=1, source_target_pairs={{0,4},{4,0},{8,12},{12,8},{16,20},{20,16},{24,28},{28,24},{1,5},{5... | collective-permute-start | bytes 3145736 | tf_op jit(solution)/shard_map/ppermute | solution.py:717
  638.5 38.9 %collective-permute-start.34 = (f32[2,768,128]{2,1,0:T(8,128)}, f32[2,768,128]{2,1,0:T(8,128)}, u32[]{:S(2)}, u32[]{:S(2)}) collective-permute-start(f32[2,768,128]{2,1,0:T(8,128)} %collective-permute-done.31.refs_2_), channel_id=1, source_target_pairs={{1,0},{2,3},{5,4},{6,7},{9,8},{10,11},{13,12},{14,15},{17,16},{18,... | collective-permute-start | bytes 2359304 | tf_op jit(solution)/shard_map/ppermute | solution.py:822
  644.1 63.9 %collective-permute-start.9 = (f32[2,768,128]{2,1,0:T(8,128)}, f32[2,768,128]{2,1,0:T(8,128)}, u32[]{:S(2)}, u32[]{:S(2)}) collective-permute-start(f32[2,768,128]{2,1,0:T(8,128)} %pad_maximum_fusion.3.refs_0_), channel_id=1, source_target_pairs={{0,1},{1,0},{2,3},{3,2},{4,5},{5,4},{6,7},{7,6},{8,9},{9,8},{10,11... | collective-permute-start | bytes 2359304 | tf_op jit(solution)/shard_map/ppermute | solution.py:818
  644.2 63.8 %collective-permute-start.10 = (f32[2,768,128]{2,1,0:T(8,128)}, f32[2,768,128]{2,1,0:T(8,128)S(1)}, u32[]{:S(2)}, u32[]{:S(2)}) collective-permute-start(f32[2,768,128]{2,1,0:T(8,128)} %pad_maximum_fusion.3.refs_0_), channel_id=1, source_target_pairs={{0,2},{1,3},{2,0},{3,1},{4,6},{5,7},{6,4},{7,5},{8,10},{9,11},{10,... | collective-permute-start | bytes 2359304 | tf_op jit(solution)/shard_map/ppermute | solution.py:818
  647.3 65.4 %collective-permute-start.11 = (f32[2,768,128]{2,1,0:T(8,128)}, f32[2,768,128]{2,1,0:T(8,128)S(1)}, u32[]{:S(2)}, u32[]{:S(2)}) collective-permute-start(f32[2,768,128]{2,1,0:T(8,128)} %pad_maximum_fusion.3.refs_0_), channel_id=1, source_target_pairs={{0,3},{1,2},{2,1},{3,0},{4,7},{5,6},{6,5},{7,4},{8,11},{9,10},{10,... | collective-permute-start | bytes 2359304 | tf_op jit(solution)/shard_map/ppermute | solution.py:818
  (40 other events, 903.1 us)

commit v4 on v3

--- a/solution.py
+++ b/solution.py
@@ -13,6 +13,11 @@
 REACH = 3
 INNER = 128
 SUB = 8
+UNROLL = 2
+SHORT_TILE = 512
+HYENA_TILE = 256
+PRODUCT_TILE = 256
+ROW_TILE = 384
 
 
 F32 = jnp.float32
@@ -83,7 +88,7 @@
 def short_stage(halo, stream, pre, post, taps, long_pre, parts):
     length, width = stream.shape
     taps_n = taps.shape[0]
-    tile = min(width, 256)
+    tile = min(width, SHORT_TILE)
     group = width // parts
     tables = short_tables(taps_n)
     wide = pl.BlockSpec((length, tile), lambda i: (0, i))
@@ -176,14 +181,18 @@
     forward_outer(x_ref, w_hi, w_lo, t_re, t_im, work)
     lanes = x_ref.shape[2]
 
+    rows = pl.ds(0, 2 * INNER)
+
     def inner(i, carry):
-        both = jnp.concatenate([work[2 * i], work[2 * i + 1]], axis=1)
-        out = mm3(b_hi[...], b_lo[...], both)
-        spec[2 * i] = out[:, :lanes]
-        spec[2 * i + 1] = out[:, lanes:]
+        for k in range(UNROLL):
+            k = 2 * (UNROLL * i + k)
+            both = jnp.concatenate([work[k, rows, :], work[k + 1, rows, :]], axis=1)
+            out = mm3(b_hi[...], b_lo[...], both)
+            spec[k] = out[:, :lanes]
+            spec[k + 1] = out[:, lanes:]
         return carry
 
-    lax.fori_loop(0, work.shape[0] // 2, inner, 0)
+    lax.fori_loop(0, work.shape[0] // 2 // UNROLL, inner, 0)
 
 
 def signal_kernel(
@@ -193,18 +202,28 @@
     lanes = x_ref.shape[2]
     forward_outer(x_ref, w_hi, w_lo, t_re, t_im, work)
 
+    rows = pl.ds(0, 2 * INNER)
+
     def inner(i, carry):
-        both = jnp.concatenate([work[2 * i], work[2 * i + 1]], axis=1)
-        x = mm3(b_hi[...], b_lo[...], both)
-        h = jnp.concatenate([spec[2 * i], spec[2 * i + 1]], axis=1)
-        x_re, x_im, h_re, h_im = x[:INNER], x[INNER:], h[:INNER], h[INNER:]
-        z = jnp.concatenate([x_re * h_re - x_im * h_im, x_re * h_im + x_im * h_re], axis=0)
-        y = mm3(u_hi[...], u_lo[...], z)
-        work[2 * i] = y[:, :lanes]
-        work[2 * i + 1] = y[:, lanes:]
+        ks = [2 * (UNROLL * i + k) for k in range(UNROLL)]
+        xs = [
+            mm3(b_hi[...], b_lo[...], jnp.concatenate([work[k, rows, :], work[k + 1, rows, :]], axis=1))
+            for k in ks
+        ]
+        zs = []
+        for k, x in zip(ks, xs):
+            h = jnp.concatenate([spec[k], spec[k + 1]], axis=1)
+            x_re, x_im, h_re, h_im = x[:INNER], x[INNER:], h[:INNER], h[INNER:]
+            zs.append(
+                jnp.concatenate([x_re * h_re - x_im * h_im, x_re * h_im + x_im * h_re], axis=0)
+            )
+        for k, z in zip(ks, zs):
+            y = mm3(u_hi[...], u_lo[...], z)
+            work[k, rows, :] = y[:, :lanes]
+            work[k + 1, rows, :] = y[:, lanes:]
         return carry
 
-    lax.fori_loop(0, outer // 2, inner, 0)
+    lax.fori_loop(0, outer // 2 // UNROLL, inner, 0)
 
     def back(i, carry):
         tiles = []
@@ -324,7 +343,7 @@
 def hyena_stage(place, short_out, post, conv):
     length, width = short_out.shape
     _, _, group = conv.shape
-    tile = max(group, 128)
+    tile = max(group, HYENA_TILE)
     steps = width // tile
     half = steps // 2
 
@@ -367,8 +386,12 @@
     first = core == 0
     x = {name: load(ref) for name, ref in refs.items()}
     yield x["far"] + x["far_more"] if "far_more" in x else x["far"]
-    yield jnp.where(first, x["near_mine"], x["near_other"])
-    yield jnp.where(first, x["near_other"], x["near_mine"])
+    if "even" in x:
+        yield x["even"]
+        yield x["odd"] + x["relay"] if "relay" in x else x["odd"]
+    else:
+        yield jnp.where(first, x["near_mine"], x["near_other"])
+        yield jnp.where(first, x["near_other"], x["near_mine"])
     yield jnp.where(first, x["mine"], x["other"])
     yield jnp.where(first, x["other"], x["mine"])
 
@@ -441,14 +464,18 @@
         @pl.when((distance <= reach) & (block >= distance))
         def _():
             slot = own - distance
-            scores = mm(q_cat, k_cat[slot])
-            old = top[...]
-            best = jnp.maximum(old, jnp.max(scores, axis=1, keepdims=True))
-            shrink = jnp.exp2(old - best)
-            weight = jnp.exp2(scores - best)
-            top[...] = best
-            total[...] = total[...] * shrink + jnp.sum(weight, axis=1, keepdims=True)
-            acc[...] = acc[...] * shrink + weigh(*halves(weight), v_cat[slot])
+            length = q_cat.shape[0]
+            tile = min(length, ROW_TILE)
+            for start in range(0, length, tile):
+                rows = pl.ds(start, tile)
+                scores = mm(q_cat[start : start + tile], k_cat[slot])
+                old = top[rows, :]
+                best = jnp.maximum(old, jnp.max(scores, axis=1, keepdims=True))
+                shrink = jnp.exp2(old - best)
+                weight = jnp.exp2(scores - best)
+                top[rows, :] = best
+                total[rows, :] = total[rows, :] * shrink + jnp.sum(weight, axis=1, keepdims=True)
+                acc[rows, :] = acc[rows, :] * shrink + weigh(*halves(weight), v_cat[slot])
 
     result = acc[...] / total[...]
 
@@ -662,7 +689,7 @@
     flat = [x for group in pieces for x in group]
     _, length, part = flat[0].shape
     width = weights[0][0].shape[1]
-    tile = min(width, 256)
+    tile = min(width, PRODUCT_TILE)
     a_spec = pl.BlockSpec((2, length, part), lambda i, place: (0, 0, 0))
 
     def w_spec(row):
@@ -755,6 +782,23 @@
             for at in range(len(heads))
         ]
 
+    def joint_windows(key_pair, value_pair, head):
+        first = core == 0
+        pairs = [[cut(x, head) for x in pair] for pair in (key_pair, value_pair)]
+        odd = jnp.stack([jnp.where(first, other, mine) for mine, other in pairs])
+        even = jnp.stack([jnp.where(first, mine, other) for mine, other in pairs])
+        got = {}
+        got["far"] = shift(odd, 4)
+        got["even"] = shift(even, 2)
+        direct = (0, 1, 4, 5) if chips == 4 else range(parts - 2)
+        got["odd"] = send(odd, [(i, i + 2) for i in direct])
+        if chips == 4:
+            got["relay"] = send(got["far"], [(6, 4), (7, 5)])
+        return [
+            {name: (x, at) for name, x in got.items()} | own_of(*pair)
+            for at, pair in enumerate((key_pair, value_pair))
+        ]
+
     tail = short_gate_pre[length - taps :] * stream[length - taps :]
     halo = shift(tail, 1)
     filt = long_filter.reshape(parts, group, length)
@@ -777,10 +821,8 @@
             signal.reshape(whole, group).T, filt.transpose(1, 0, 2).reshape(group, whole)
         ).T.reshape(parts, length, group)
     reach = lax.dynamic_slice_in_dim(head_reach, core * heads_half, heads_half)
-    key_windows = later_windows(key_mine, key_other, range(min(2, heads_half)))
-    for n in range(2, heads_half):
-        key_windows += later_windows(key_mine, key_other, [n])
-    scored = score_stage(reach, place, queries, key_windows[0], 0)
+    keys = later_windows(key_mine, key_other, [0])[0]
+    scored = score_stage(reach, place, queries, keys, 0)
     back = lax.all_to_all(conv, "seq", split_axis=0, concat_axis=0, tiled=True)
     hyena_out, value_out, value_mine = hyena_stage(place, short_out, long_gate_post, back)
     value_other = swap(value_out)
@@ -790,11 +832,11 @@
         if n == 0:
             values = first_window(value_mine, value_out, value_other)
         else:
-            values = later_windows(value_mine, value_other, [n])[0]
+            keys, values = joint_windows((key_mine, key_other), (value_mine, value_other), n)
         if n == 0:
             other, mine = value_stage(reach, place, scored, values, n)
         else:
-            other, mine = attend_stage(reach, place, queries, key_windows[n], values, n)
+            other, mine = attend_stage(reach, place, queries, keys, values, n)
         if n == 0:
             out_weight, mine = lax.optimization_barrier((out_weight, mine))
             slots = [out_weight]
@@ -810,7 +852,7 @@
                 partner.append(swap(x))
         piece = jnp.stack([mine, swap(other)])
         pieces = [[piece]]
-        relays = planes == 4 and n < heads_half - 1
+        relays = planes == 4 and 0 < n < heads_half - 1
         for m in range(1, planes):
             pairs = [(i, i ^ m) for i in range(planes)]
             if relays and m > 1:

time: 733 us -> 712 us (0.971)
  the two profiles are of different devices: /device:TPU:22 before, /device:TPU:12 now
where the time goes in v4:
time: 712 us; the launch traced here: 703 us
  waiting for transfers between devices  367 us (52%)
  Pallas kernels  194 us (27%)
  starting transfers between devices  116 us (16%)
  local copies, waits for them, and re-layouts  14.6 us (2%)
  other arithmetic  9.61 us (1%)
    ppermute x35, waiting for transfers between devices, send(): return lax.ppermute(x, 'seq', pairs)  144 us
    ppermute x12, waiting for transfers between devices, shards(): pieces.append([lax.ppermute(piece, 'chan', pairs)])  122 us
    ppermute x35, starting transfers between devices, send(): return lax.ppermute(x, 'seq', pairs)  71.2 us
    pallas_call x3, Pallas kernels, attend_stage(): pl.pallas_call(functools.partial(attend_kernel, head=head, names=tuple(ke...  56.4 us
    ppermute x4, waiting for transfers between devices, shards(): pieces[m].append(lax.ppermute(passed[m], 'chan', [(1, 0), (2, 3)]))  49.3 us
    pallas_call x4, Pallas kernels, product_stage(): pl.pallas_call(functools.partial(product_kernel, sizes=tuple((len(g) for...  44.6 us
    all_to_all x1, waiting for transfers between devices, shards(): back = lax.all_to_all(conv, 'seq', split_axis=0, concat_axis=0, tiled=True)  35.8 us
    pallas_call x1, Pallas kernels, signal_stage(): pl.pallas_call(signal_kernel, in_specs=[vmem_spec()] * 8 + [smem_spec()]...  27.3 us
  transfers between devices with their start and end apart: 54, of which 24 were waited for; matrix products, arithmetic and copies ran while one was open for 2% of the time, Pallas kernels for 21%

profile of v4, /device:TPU:12, one launch (start us, length us, event | category | flops | bytes accessed | tf_op | source)
XLA Modules:
  0.0 702.6 jit_solution(10257800125440268190)
XLA Ops:
  0.6 4.2 all-to-all-start.1
  6.1 2.0 collective-permute-start
  8.2 38.7 %collective-permute-done.halo = f32[128,1024]{1,0:T(8,128)S(1)} collective-permute-done((f32[128,1024]{1,0:T(8,128)S(1)}, f32[128,1024]{1,0:T(8,128)S(1)}, u32[]{:S(2)}, u32[]{:S(2)}) %collective-permute-start) | collective-permute-done | bytes 524320 | tf_op jit(solution)/shard_map/ppermute | solution.py:744
  47.7 12.4 %short_stage.1 = (f32[768,1024]{1,0:T(8,128)}, f32[8,768,128]{2,1,0:T(8,128)}) custom-call(bf16[256,256]{1,0:T(8,128)(2,1)} %constant.71.clone.f_hi, bf16[256,256]{1,0:T(8,128)(2,1)} %constant.72.clone.f_lo, bf16[128,256]{1,0:T(8,128)(2,1)} %constant.73.clone.g_hi, bf16[128,256]{1,0:T(8,128)(2,1)} %constant.74.clone.g_lo, f32[128,1024]{1,0:T(8,128)} %copy-done.30, ...), custom_call_target="tpu_custom_call" | custom-call | tf_op jit(solution)/shard_map/short_stage/pallas_call | solution.py:97
  60.1 1.7 copy-done.7
  61.8 4.4 all-to-all-start
  66.2 2.2 constant_dynamic-slice_fusion.2
  68.5 17.0 %filter_stage.1.spec = f32[48,256,128]{2,1,0:T(8,128)} custom-call(bf16[768,384]{1,0:T(8,128)(2,1)} %constant.75.clone.w_hi, bf16[768,384]{1,0:T(8,128)(2,1)} %constant.76.clone.w_lo, bf16[256,256]{1,0:T(8,128)(2,1)} %constant.77.clone.b_hi, bf16[256,256]{1,0:T(8,128)(2,1)} %constant.78.clone.b_lo, f32[16,48]{1,0:T(8,128)} %constant.79.clone.t_re, ...), custom_call_target="tpu_custom_call" | custom-call | tf_op jit(solution)/shard_map/filter_stage/pallas_call | solution.py:263
  85.5 16.1 %all-to-all-done = f32[8,768,128]{2,1,0:T(8,128)} async-done(((f32[8,768,128]{2,1,0:T(8,128)}), f32[8,768,128]{2,1,0:T(8,128)}, u32[]{:S(2)}, u32[]{:S(2)}) %all-to-all-start) | async-done | bytes 3145760 | tf_op jit(solution)/shard_map/all_to_all | solution.py:809
  101.6 27.3 %signal_stage.1 = f32[48,128,128]{2,1,0:T(8,128)} custom-call(bf16[768,384]{1,0:T(8,128)(2,1)} %constant.75.clone.w_hi, bf16[768,384]{1,0:T(8,128)(2,1)} %constant.76.clone.w_lo, bf16[384,768]{1,0:T(8,128)(2,1)} %constant.81.clone.v_hi, bf16[384,768]{1,0:T(8,128)(2,1)} %constant.82.clone.v_lo, bf16[256,256]{1,0:T(8,128)(2,1)} %constant.77.clone.b_hi, ...), custom_call_target="tpu_custom_call" | custom-call | tf_op jit(solution)/shard_map/signal_stage/pallas_call | solution.py:280
  128.9 5.8 all-to-all-start.2
  135.4 35.8 %all-to-all-done.2.conv = f32[8,768,128]{2,1,0:T(8,128)} async-done(((f32[8,768,128]{2,1,0:T(8,128)}), f32[8,768,128]{2,1,0:T(8,128)}, u32[]{:S(2)}, u32[]{:S(2)}) %all-to-all-start.2) | async-done | bytes 3145760 | tf_op jit(solution)/shard_map/all_to_all | solution.py:826
  171.2 7.4 %hyena_stage.1 = (f32[768,1024]{1,0:T(8,128)}, f32[768,512]{1,0:T(8,128)}, f32[768,512]{1,0:T(8,128)}) custom-call(s32[3]{0:T(128)} %pad_add_fusion.place_ref, f32[768,1024]{1,0:T(8,128)} %get-tuple-element.23.short_out, f32[768,1024]{1,0:T(8,128)} %post.3, f32[8,768,128]{2,1,0:T(8,128)} %all-to-all-done.2.conv), custom_call_target="tpu_custom_call" | custom-call | tf_op jit(solution)/shard_map/hyena_stage/pallas_call | solution.py:354
  178.6 3.9 constant_dynamic-slice_fusion
  183.4 2.7 collective-permute-start.13
  189.7 1.9 collective-permute-start.17
  191.6 1.5 select_bitcast_fusion
  194.6 28.1 %collective-permute-done.12.refs_2_ = f32[1,768,128]{2,1,0:T(8,128)S(1)} collective-permute-done((f32[1,768,128]{2,1,0:T(8,128)S(1)}, f32[1,768,128]{2,1,0:T(8,128)S(1)}, u32[]{:S(2)}, u32[]{:S(2)}) %collective-permute-start.12) | collective-permute-done | bytes 393248 | tf_op jit(solution)/shard_map/ppermute | solution.py:744
  222.7 1.9 collective-permute-start.5
  225.3 26.7 %collective-permute-done.15.refs_4_ = f32[768,128]{1,0:T(8,128)S(1)} collective-permute-done((f32[768,128]{1,0:T(8,128)S(1)}, f32[768,128]{1,0:T(8,128)S(1)}, u32[]{:S(2)}, u32[]{:S(2)}) %collective-permute-start.15) | collective-permute-done | bytes 393248 | tf_op jit(solution)/shard_map/ppermute | solution.py:744
  252.0 1.9 collective-permute-start.16
  256.8 5.8 collective-permute-done.16.refs_5_
  262.7 2.2 collective-permute-start.27
  264.9 1.9 collective-permute-start.26
  269.3 2.7 collective-permute-start.36
  272.0 26.5 %collective-permute-done.25.refs_2_.refs_8_ = f32[2,768,128]{2,1,0:T(8,128)} collective-permute-done((f32[2,768,128]{2,1,0:T(8,128)S(1)}, f32[2,768,128]{2,1,0:T(8,128)}, u32[]{:S(2)}, u32[]{:S(2)}) %collective-permute-start.25) | collective-permute-done | bytes 786464 | tf_op jit(solution)/shard_map/ppermute | solution.py:744
  298.6 2.2 collective-permute-start.37
  302.9 1.5 collective-permute-start.28
  305.0 15.5 %score_stage.1 = (bf16[2,4,768,768]{3,2,1,0:T(8,128)(2,1)}, bf16[2,4,768,768]{3,2,1,0:T(8,128)(2,1)}, f32[2,768,128]{2,1,0:T(8,128)}) custom-call(s32[4]{0:T(128)} %dynamic_slice.17.reach_ref, s32[3]{0:T(128)} %pad_add_fusion.place_ref, f32[768,512]{1,0:T(8,128)} %get-tuple-element.58.refs_0_, f32[768,512]{1,0:T(8,128)} %collective-permute-done.2.refs_1_, ...), custom_call_target="tpu_custom_call" | custom-call | tf_op jit(solution)/shard_map/score_stage/pallas_call | solution.py:612
  320.6 13.3 %value_stage.1 = (f32[768,128]{1,0:T(8,128)}, f32[768,128]{1,0:T(8,128)}) custom-call(s32[4]{0:T(128)} %dynamic_slice.17.reach_ref, s32[3]{0:T(128)} %pad_add_fusion.place_ref, bf16[2,4,768,768]{3,2,1,0:T(8,128)(2,1)} %get-tuple-element.33.refs_0_, bf16[2,4,768,768]{3,2,1,0:T(8,128)(2,1)} %get-tuple-element.34.refs_1_, ...), custom_call_target="tpu_custom_call" | custom-call | tf_op jit(solution)/shard_map/value_stage/pallas_call | solution.py:638
  333.8 33.6 %collective-permute-start.47 = (f32[768,128]{1,0:T(8,128)}, f32[768,128]{1,0:T(8,128)S(1)}, u32[]{:S(2)}, u32[]{:S(2)}) collective-permute-start(f32[768,128]{1,0:T(8,128)} %get-tuple-element.43), channel_id=1, source_target_pairs={{0,4},{4,0},{8,12},{12,8},{16,20},{20,16},{24,28},{28,24},{1,5},{5... | collective-permute-start | bytes 1179656 | tf_op jit(solution)/shard_map/ppermute | solution.py:744
  367.4 1.5 collective-permute-start.38
  369.0 4.2 collective-permute-start.18
  373.2 1.9 pad_maximum_fusion.10.refs_0_
  375.3 16.1 %collective-permute-done.38.refs_5_.refs_11_ = f32[2,768,128]{2,1,0:T(8,128)S(1)} collective-permute-done((f32[2,768,128]{2,1,0:T(8,128)}, f32[2,768,128]{2,1,0:T(8,128)S(1)}, u32[]{:S(2)}, u32[]{:S(2)}) %collective-permute-start.38) | collective-permute-done | bytes 786464 | tf_op jit(solution)/shard_map/ppermute | solution.py:744
  391.4 2.6 collective-permute-start.49
  394.0 4.9 collective-permute-done.48.refs_1_
  398.9 13.8 %attend_stage.4 = (f32[768,128]{1,0:T(8,128)}, f32[768,128]{1,0:T(8,128)}) custom-call(s32[4]{0:T(128)} %dynamic_slice.17.reach_ref, s32[3]{0:T(128)} %pad_add_fusion.place_ref, f32[768,512]{1,0:T(8,128)} %get-tuple-element.58.refs_0_, f32[768,512]{1,0:T(8,128)} %collective-permute-done.2.refs_1_, f32[2,768,128]{2,1,0:T(8,128)} %collective-permute-done.25.refs_2_.refs_8_, ...), custom_call_target="tpu_custom_call" | custom-call | tf_op jit(solution)/shard_map/attend_stage/pallas_call | solution.py:587
  412.7 31.8 %collective-permute-done.49.refs_2_ = f32[2,768,128]{2,1,0:T(8,128)S(1)} collective-permute-done((f32[2,768,128]{2,1,0:T(8,128)}, f32[2,768,128]{2,1,0:T(8,128)S(1)}, u32[]{:S(2)}, u32[]{:S(2)}) %collective-permute-start.49) | collective-permute-done | bytes 786464 | tf_op jit(solution)/shard_map/ppermute | solution.py:860
  444.5 23.7 %attend_stage.3 = (f32[768,128]{1,0:T(8,128)}, f32[768,128]{1,0:T(8,128)}) custom-call(s32[4]{0:T(128)} %dynamic_slice.17.reach_ref, s32[3]{0:T(128)} %pad_add_fusion.place_ref, f32[768,512]{1,0:T(8,128)} %get-tuple-element.58.refs_0_, f32[768,512]{1,0:T(8,128)} %collective-permute-done.2.refs_1_, f32[2,768,128]{2,1,0:T(8,128)} %copy-done.10, ...), custom_call_target="tpu_custom_call" | custom-call | tf_op jit(solution)/shard_map/attend_stage/pallas_call | solution.py:587
  468.3 18.9 %attend_stage.5 = (f32[768,128]{1,0:T(8,128)}, f32[768,128]{1,0:T(8,128)}) custom-call(s32[4]{0:T(128)} %dynamic_slice.17.reach_ref, s32[3]{0:T(128)} %pad_add_fusion.place_ref, f32[768,512]{1,0:T(8,128)} %get-tuple-element.58.refs_0_, f32[768,512]{1,0:T(8,128)} %collective-permute-done.2.refs_1_, f32[2,768,128]{2,1,0:T(8,128)} %collective-permute-done.35.refs_2_.refs_8_, ...), custom_call_target="tpu_custom_call" | custom-call | tf_op jit(solution)/shard_map/attend_stage/pallas_call | solution.py:587
  487.7 1.4 collective-permute-done.39
  490.5 3.9 collective-permute-start.32
  495.5 1.8 collective-permute-start.40
  498.6 9.5 %collective-permute-done.30.refs_1_ = f32[2,768,128]{2,1,0:T(8,128)S(1)} collective-permute-done((f32[2,768,128]{2,1,0:T(8,128)S(1)}, f32[2,768,128]{2,1,0:T(8,128)S(1)}, u32[]{:S(2)}, u32[]{:S(2)}) %collective-permute-start.30) | collective-permute-done | bytes 786464 | tf_op jit(solution)/shard_map/ppermute | solution.py:860
  509.0 4.0 collective-permute-start.42
  513.2 13.4 %collective-permute-done.31.refs_2_ = f32[2,768,128]{2,1,0:T(8,128)} collective-permute-done((f32[2,768,128]{2,1,0:T(8,128)S(1)}, f32[2,768,128]{2,1,0:T(8,128)}, u32[]{:S(2)}, u32[]{:S(2)}) %collective-permute-start.31) | collective-permute-done | bytes 786464 | tf_op jit(solution)/shard_map/ppermute | solution.py:860
  526.6 3.0 collective-permute-done.32.refs_4_
  529.6 12.3 %collective-permute-done.40.refs_1_ = f32[2,768,128]{2,1,0:T(8,128)} collective-permute-done((f32[2,768,128]{2,1,0:T(8,128)S(1)}, f32[2,768,128]{2,1,0:T(8,128)}, u32[]{:S(2)}, u32[]{:S(2)}) %collective-permute-start.40) | collective-permute-done | bytes 786464 | tf_op jit(solution)/shard_map/ppermute | solution.py:860
  542.0 17.4 %collective-permute-done.41.refs_2_ = f32[2,768,128]{2,1,0:T(8,128)S(1)} collective-permute-done((f32[2,768,128]{2,1,0:T(8,128)S(1)}, f32[2,768,128]{2,1,0:T(8,128)S(1)}, u32[]{:S(2)}, u32[]{:S(2)}) %collective-permute-start.41) | collective-permute-done | bytes 786464 | tf_op jit(solution)/shard_map/ppermute | solution.py:860
  559.4 3.6 collective-permute-done.42.refs_4_
  565.8 16.4 %collective-permute-done.33.refs_3_ = f32[2,768,128]{2,1,0:T(8,128)S(1)} collective-permute-done((f32[2,768,128]{2,1,0:T(8,128)S(1)}, f32[2,768,128]{2,1,0:T(8,128)S(1)}, u32[]{:S(2)}, u32[]{:S(2)}) %collective-permute-start.33) | collective-permute-done | bytes 786464 | tf_op jit(solution)/shard_map/ppermute | solution.py:864
  582.2 4.4 collective-permute-start.44
  586.7 12.4 %collective-permute-done.43.refs_3_ = f32[2,768,128]{2,1,0:T(8,128)S(1)} collective-permute-done((f32[2,768,128]{2,1,0:T(8,128)S(1)}, f32[2,768,128]{2,1,0:T(8,128)S(1)}, u32[]{:S(2)}, u32[]{:S(2)}) %collective-permute-start.43) | collective-permute-done | bytes 786464 | tf_op jit(solution)/shard_map/ppermute | solution.py:864
  600.5 14.6 %collective-permute-done.44.refs_5_ = f32[2,768,128]{2,1,0:T(8,128)S(1)} collective-permute-done((f32[2,768,128]{2,1,0:T(8,128)S(1)}, f32[2,768,128]{2,1,0:T(8,128)S(1)}, u32[]{:S(2)}, u32[]{:S(2)}) %collective-permute-start.44) | collective-permute-done | bytes 786464 | tf_op jit(solution)/shard_map/ppermute | solution.py:864
  615.1 5.3 collective-permute-start.34
  620.4 2.9 collective-permute-start.10
  625.2 10.6 %product_stage.4.refs_14_ = f32[768,1024]{1,0:T(8,128)} custom-call(s32[3]{0:T(128)} %pad_add_fusion.place_ref, f32[2,768,128]{2,1,0:T(8,128)} %pad_maximum_fusion.10.refs_0_, f32[2,768,128]{2,1,0:T(8,128)} %collective-permute-done.48.refs_1_, f32[2,768,128]{2,1,0:T(8,128)} %copy-done.20, f32[2,768,128]{2,1,0:T(8,128)} %collective-permute-done.50.refs_3_, ...), custom_call_target="tpu_custom_call" | custom-call | tf_op jit(solution)/shard_map/product_stage/pallas_call | solution.py:700
  635.8 11.6 %product_stage.5.refs_14_ = f32[768,1024]{1,0:T(8,128)} custom-call(s32[3]{0:T(128)} %pad_add_fusion.place_ref, f32[2,768,128]{2,1,0:T(8,128)} %copy-done.17, f32[2,768,128]{2,1,0:T(8,128)} %collective-permute-done.40.refs_1_, f32[2,768,128]{2,1,0:T(8,128)} %copy-done.23, f32[2,768,128]{2,1,0:T(8,128)} %copy-done.26, f32[2,768,128]{2,1,0:T(8,128)} %copy-done.24, ...), custom_call_target="tpu_custom_call" | custom-call | tf_op jit(solution)/shard_map/product_stage/pallas_call | solution.py:700
  647.4 5.9 collective-permute-done.34.refs_5_
  653.3 11.5 %product_stage.6.refs_12_ = f32[768,1024]{1,0:T(8,128)} custom-call(s32[3]{0:T(128)} %pad_add_fusion.place_ref, f32[2,768,128]{2,1,0:T(8,128)} %copy-done.16, f32[2,768,128]{2,1,0:T(8,128)} %copy-done.21, f32[2,768,128]{2,1,0:T(8,128)} %collective-permute-done.31.refs_2_, f32[2,768,128]{2,1,0:T(8,128)} %copy-done.25, f32[2,768,128]{2,1,0:T(8,128)} %copy-done.22, ...), custom_call_target="tpu_custom_call" | custom-call | tf_op jit(solution)/shard_map/product_stage/pallas_call | solution.py:700
  664.8 21.6 %collective-permute-done.9.refs_1_ = f32[2,768,128]{2,1,0:T(8,128)} collective-permute-done((f32[2,768,128]{2,1,0:T(8,128)S(1)}, f32[2,768,128]{2,1,0:T(8,128)}, u32[]{:S(2)}, u32[]{:S(2)}) %collective-permute-start.9) | collective-permute-done | bytes 786464 | tf_op jit(solution)/shard_map/ppermute | solution.py:860
  686.4 4.2 collective-permute-done.11.refs_3_
  691.5 10.9 %product_stage.7 = f32[768,1024]{1,0:T(8,128)} custom-call(s32[3]{0:T(128)} %pad_add_fusion.place_ref, f32[2,768,128]{2,1,0:T(8,128)} %copy-done.19, f32[2,768,128]{2,1,0:T(8,128)} %collective-permute-done.9.refs_1_, f32[2,768,128]{2,1,0:T(8,128)} %copy-done.28, f32[2,768,128]{2,1,0:T(8,128)} %copy-done.29, f32[512,1024]{1,0:T(8,128)} %refs_4_.1, ...), custom_call_target="tpu_custom_call" | custom-call | tf_op jit(solution)/shard_map/product_stage/pallas_call | solution.py:700
  (158 shorter events, 30.0 us)
Async XLA Ops:
  0.6 59.4 %all-to-all-start.1 = ((f32[8,128,768]{2,1,0:T(8,128)}), f32[8,128,768]{2,1,0:T(8,128)S(1)}, u32[]{:S(2)}, u32[]{:S(2)}) async-start(f32[8,128,768]{2,1,0:T(8,128)} %bitcast.45), calls=%async_computation.1 | async-start | bytes 6291456 | tf_op jit(solution)/shard_map/all_to_all | solution.py:805
  6.1 40.7 %collective-permute-start = (f32[128,1024]{1,0:T(8,128)S(1)}, f32[128,1024]{1,0:T(8,128)S(1)}, u32[]{:S(2)}, u32[]{:S(2)}) collective-permute-start(f32[128,1024]{1,0:T(8,128)S(1)} %slice_multiply_fusion), channel_id=1, source_target_pairs={{0,4},{4,8},{8,12},{12,16},{16,20},{20,24},{24,28},{1,5},{5,9},{9,... | collective-permute-start | bytes 1572872 | tf_op jit(solution)/shard_map/ppermute | solution.py:744
  61.8 39.8 %all-to-all-start = ((f32[8,768,128]{2,1,0:T(8,128)}), f32[8,768,128]{2,1,0:T(8,128)}, u32[]{:S(2)}, u32[]{:S(2)}) async-start(f32[8,768,128]{2,1,0:T(8,128)} %get-tuple-element.24), calls=%async_computation | async-start | bytes 6291456 | tf_op jit(solution)/shard_map/all_to_all | solution.py:809
  68.4 114.6 %copy-start = (f32[768,512]{1,0:T(8,128)}, f32[768,512]{1,0:T(8,128)S(1)}, u32[]{:S(2)}) copy-start(f32[768,512]{1,0:T(8,128)S(1)} %get-tuple-element.28.refs_6_.refs_5_) | copy-start | bytes 4718596
  68.4 17.1 %collective-permute-start.1 = (f32[768,512]{1,0:T(8,128)S(1)}, f32[768,512]{1,0:T(8,128)S(1)}, u32[]{:S(2)}, u32[]{:S(2)}) collective-permute-start(f32[768,512]{1,0:T(8,128)S(1)} %get-tuple-element.59), channel_id=1, source_target_pairs={{0,4},{4,0},{8,12},{12,8},{16,20},{20,16},{24,28},{28,24},{1,5},{5... | collective-permute-start | bytes 4718600 | tf_op jit(solution)/shard_map/ppermute | solution.py:744
  85.5 97.5 %copy-start.3 = (f32[768,512]{1,0:T(8,128)}, f32[768,512]{1,0:T(8,128)S(1)}, u32[]{:S(2)}) copy-start(f32[768,512]{1,0:T(8,128)S(1)} %collective-permute-done.1.refs_7_.refs_6_) | copy-start | bytes 4718596
  128.9 42.3 %all-to-all-start.2 = ((f32[8,768,128]{2,1,0:T(8,128)}), f32[8,768,128]{2,1,0:T(8,128)}, u32[]{:S(2)}, u32[]{:S(2)}) async-start(f32[8,768,128]{2,1,0:T(8,128)} %bitcast.44), calls=%async_computation.2 | async-start | bytes 6291456 | tf_op jit(solution)/shard_map/all_to_all | solution.py:826
  178.6 11.1 %collective-permute-start.3 = (f32[768,512]{1,0:T(8,128)}, f32[768,512]{1,0:T(8,128)}, u32[]{:S(2)}, u32[]{:S(2)}) collective-permute-start(f32[768,512]{1,0:T(8,128)} %get-tuple-element.29), channel_id=1, source_target_pairs={{0,4},{4,0},{8,12},{12,8},{16,20},{20,16},{24,28},{28,24},{1,5},{5... | collective-permute-start | bytes 4718600 | tf_op jit(solution)/shard_map/ppermute | solution.py:744
  182.5 10.7 %collective-permute-start.2 = (f32[768,512]{1,0:T(8,128)}, f32[768,512]{1,0:T(8,128)}, u32[]{:S(2)}, u32[]{:S(2)}) collective-permute-start(f32[768,512]{1,0:T(8,128)} %get-tuple-element.57), channel_id=1, source_target_pairs={{0,4},{4,0},{8,12},{12,8},{16,20},{20,16},{24,28},{28,24},{1,5},{5... | collective-permute-start | bytes 4718600 | tf_op jit(solution)/shard_map/ppermute | solution.py:744
  183.4 41.3 %collective-permute-start.13 = (f32[2,768,128]{2,1,0:T(8,128)S(1)}, f32[2,768,128]{2,1,0:T(8,128)S(1)}, u32[]{:S(2)}, u32[]{:S(2)}) collective-permute-start(f32[2,768,128]{2,1,0:T(8,128)S(1)} %pad_maximum_fusion.3), channel_id=1, source_target_pairs={{0,8},{4,12},{8,16},{12,20},{16,24},{20,28},{1,9},{5,13},{9,17},{1... | collective-permute-start | bytes 2359304 | tf_op jit(solution)/shard_map/ppermute | solution.py:744
  186.0 36.7 %collective-permute-start.12 = (f32[1,768,128]{2,1,0:T(8,128)S(1)}, f32[1,768,128]{2,1,0:T(8,128)S(1)}, u32[]{:S(2)}, u32[]{:S(2)}) collective-permute-start(f32[1,768,128]{2,1,0:T(8,128)S(1)} %get-tuple-element.49), channel_id=1, source_target_pairs={{0,16},{4,20},{8,24},{12,28},{1,17},{5,21},{9,25},{13,29},{2,18},{... | collective-permute-start | bytes 1179656 | tf_op jit(solution)/shard_map/ppermute | solution.py:744
  188.4 63.6 %collective-permute-start.15 = (f32[768,128]{1,0:T(8,128)S(1)}, f32[768,128]{1,0:T(8,128)S(1)}, u32[]{:S(2)}, u32[]{:S(2)}) collective-permute-start(f32[768,128]{1,0:T(8,128)S(1)} %slice.73), channel_id=1, source_target_pairs={{4,16},{12,24},{5,17},{13,25},{6,18},{14,26},{7,19},{15,27}} | collective-permute-start | bytes 1179656 | tf_op jit(solution)/shard_map/ppermute | solution.py:744
  189.7 64.3 %collective-permute-start.17 = (f32[768,128]{1,0:T(8,128)S(1)}, f32[768,128]{1,0:T(8,128)S(1)}, u32[]{:S(2)}, u32[]{:S(2)}) collective-permute-start(f32[768,128]{1,0:T(8,128)S(1)} %slice.73), channel_id=1, source_target_pairs={{0,12},{8,20},{16,28},{4,8},{12,16},{20,24},{1,13},{9,21},{17,29},... | collective-permute-start | bytes 1179656 | tf_op jit(solution)/shard_map/ppermute | solution.py:744
  193.2 71.7 %collective-permute-start.4 = (f32[2,768,128]{2,1,0:T(8,128)S(1)}, f32[2,768,128]{2,1,0:T(8,128)S(1)}, u32[]{:S(2)}, u32[]{:S(2)}) collective-permute-start(f32[2,768,128]{2,1,0:T(8,128)S(1)} %pad_maximum_fusion), channel_id=1, source_target_pairs={{0,16},{4,20},{8,24},{12,28},{1,17},{5,21},{9,25},{13,29},{2,18},{... | collective-permute-start | bytes 2359304 | tf_op jit(solution)/shard_map/ppermute | solution.py:744
  222.7 45.1 %collective-permute-start.5 = (f32[2,768,128]{2,1,0:T(8,128)S(1)}, f32[2,768,128]{2,1,0:T(8,128)S(1)}, u32[]{:S(2)}, u32[]{:S(2)}) collective-permute-start(f32[2,768,128]{2,1,0:T(8,128)S(1)} %pad_maximum_fusion.1), channel_id=1, source_target_pairs={{0,8},{4,12},{8,16},{12,20},{16,24},{20,28},{1,9},{5,13},{9,17},{1... | collective-permute-start | bytes 2359304 | tf_op jit(solution)/shard_map/ppermute | solution.py:744
  224.6 30.8 %collective-permute-start.14 = (f32[768,128]{1,0:T(8,128)S(1)}, f32[768,128]{1,0:T(8,128)S(1)}, u32[]{:S(2)}, u32[]{:S(2)}) collective-permute-start(f32[768,128]{1,0:T(8,128)S(1)} %get-tuple-element.63), channel_id=1, source_target_pairs={{4,20},{12,28},{5,21},{13,29},{6,22},{14,30},{7,23},{15,31}} | collective-permute-start | bytes 1179656 | tf_op jit(solution)/shard_map/ppermute | solution.py:744
  252.0 10.7 %collective-permute-start.16 = (f32[768,128]{1,0:T(8,128)S(1)}, f32[768,128]{1,0:T(8,128)S(1)}, u32[]{:S(2)}, u32[]{:S(2)}) collective-permute-start(f32[768,128]{1,0:T(8,128)S(1)} %get-tuple-element.63), channel_id=1, source_target_pairs={{0,8},{4,12},{8,16},{12,20},{16,24},{20,28},{1,9},{5,13},{9,17},{1... | collective-permute-start | bytes 1179656 | tf_op jit(solution)/shard_map/ppermute | solution.py:744
  253.9 15.3 %collective-permute-start.6 = (f32[2,768,128]{2,1,0:T(8,128)S(1)}, f32[2,768,128]{2,1,0:T(8,128)S(1)}, u32[]{:S(2)}, u32[]{:S(2)}) collective-permute-start(f32[2,768,128]{2,1,0:T(8,128)S(1)} %pad_maximum_fusion), channel_id=1, source_target_pairs={{0,8},{4,12},{16,24},{20,28},{1,9},{5,13},{17,25},{21,29},{2,10},{... | collective-permute-start | bytes 2359304 | tf_op jit(solution)/shard_map/ppermute | solution.py:744
  255.4 43.1 %collective-permute-start.25 = (f32[2,768,128]{2,1,0:T(8,128)S(1)}, f32[2,768,128]{2,1,0:T(8,128)}, u32[]{:S(2)}, u32[]{:S(2)}) collective-permute-start(f32[2,768,128]{2,1,0:T(8,128)S(1)} %pad_maximum_fusion.4), channel_id=1, source_target_pairs={{0,16},{4,20},{8,24},{12,28},{1,17},{5,21},{9,25},{13,29},{2,18},{... | collective-permute-start | bytes 2359304 | tf_op jit(solution)/shard_map/ppermute | solution.py:744
  262.7 40.2 %collective-permute-start.27 = (f32[2,768,128]{2,1,0:T(8,128)S(1)}, f32[2,768,128]{2,1,0:T(8,128)}, u32[]{:S(2)}, u32[]{:S(2)}) collective-permute-start(f32[2,768,128]{2,1,0:T(8,128)S(1)} %pad_maximum_fusion.4), channel_id=1, source_target_pairs={{0,8},{4,12},{16,24},{20,28},{1,9},{5,13},{17,25},{21,29},{2,10},{... | collective-permute-start | bytes 2359304 | tf_op jit(solution)/shard_map/ppermute | solution.py:744
  264.9 35.8 %collective-permute-start.26 = (f32[2,768,128]{2,1,0:T(8,128)S(1)}, f32[2,768,128]{2,1,0:T(8,128)S(1)}, u32[]{:S(2)}, u32[]{:S(2)}) collective-permute-start(f32[2,768,128]{2,1,0:T(8,128)S(1)} %pad_maximum_fusion.5), channel_id=1, source_target_pairs={{0,8},{4,12},{8,16},{12,20},{16,24},{20,28},{1,9},{5,13},{9,17},{1... | collective-permute-start | bytes 2359304 | tf_op jit(solution)/shard_map/ppermute | solution.py:744
  267.8 66.0 %collective-permute-start.35 = (f32[2,768,128]{2,1,0:T(8,128)}, f32[2,768,128]{2,1,0:T(8,128)}, u32[]{:S(2)}, u32[]{:S(2)}) collective-permute-start(f32[2,768,128]{2,1,0:T(8,128)} %pad_maximum_fusion.7), channel_id=1, source_target_pairs={{0,16},{4,20},{8,24},{12,28},{1,17},{5,21},{9,25},{13,29},{2,18},{... | collective-permute-start | bytes 2359304 | tf_op jit(solution)/shard_map/ppermute | solution.py:744
  269.3 98.1 %collective-permute-start.36 = (f32[2,768,128]{2,1,0:T(8,128)S(1)}, f32[2,768,128]{2,1,0:T(8,128)S(1)}, u32[]{:S(2)}, u32[]{:S(2)}) collective-permute-start(f32[2,768,128]{2,1,0:T(8,128)S(1)} %pad_maximum_fusion.8), channel_id=1, source_target_pairs={{0,8},{4,12},{8,16},{12,20},{16,24},{20,28},{1,9},{5,13},{9,17},{1... | collective-permute-start | bytes 2359304 | tf_op jit(solution)/shard_map/ppermute | solution.py:744
  298.6 76.5 %collective-permute-start.37 = (f32[2,768,128]{2,1,0:T(8,128)}, f32[2,768,128]{2,1,0:T(8,128)}, u32[]{:S(2)}, u32[]{:S(2)}) collective-permute-start(f32[2,768,128]{2,1,0:T(8,128)} %pad_maximum_fusion.7), channel_id=1, source_target_pairs={{0,8},{4,12},{16,24},{20,28},{1,9},{5,13},{17,25},{21,29},{2,10},{... | collective-permute-start | bytes 2359304 | tf_op jit(solution)/shard_map/ppermute | solution.py:744
  301.6 73.5 %collective-permute-start.7 = (f32[2,768,128]{2,1,0:T(8,128)S(1)}, f32[2,768,128]{2,1,0:T(8,128)}, u32[]{:S(2)}, u32[]{:S(2)}) collective-permute-start(f32[2,768,128]{2,1,0:T(8,128)S(1)} %collective-permute-done.4.refs_2_.refs_8_), channel_id=1, source_target_pairs={{24,16},{28,20},{25,17},{29,21},{26,18},{30,22},{27,19},{31,23}} | collective-permute-start | bytes 2359304 | tf_op jit(solution)/shard_map/ppermute | solution.py:744
  302.9 72.3 %collective-permute-start.28 = (f32[2,768,128]{2,1,0:T(8,128)}, f32[2,768,128]{2,1,0:T(8,128)}, u32[]{:S(2)}, u32[]{:S(2)}) collective-permute-start(f32[2,768,128]{2,1,0:T(8,128)} %collective-permute-done.25.refs_2_.refs_8_), channel_id=1, source_target_pairs={{24,16},{28,20},{25,17},{29,21},{26,18},{30,22},{27,19},{31,23}} | collective-permute-start | bytes 2359304 | tf_op jit(solution)/shard_map/ppermute | solution.py:744
  333.8 35.1 %collective-permute-start.47 = (f32[768,128]{1,0:T(8,128)}, f32[768,128]{1,0:T(8,128)S(1)}, u32[]{:S(2)}, u32[]{:S(2)}) collective-permute-start(f32[768,128]{1,0:T(8,128)} %get-tuple-element.43), channel_id=1, source_target_pairs={{0,4},{4,0},{8,12},{12,8},{16,20},{20,16},{24,28},{28,24},{1,5},{5... | collective-permute-start | bytes 1179656 | tf_op jit(solution)/shard_map/ppermute | solution.py:744
  367.4 24.0 %collective-permute-start.38 = (f32[2,768,128]{2,1,0:T(8,128)}, f32[2,768,128]{2,1,0:T(8,128)S(1)}, u32[]{:S(2)}, u32[]{:S(2)}) collective-permute-start(f32[2,768,128]{2,1,0:T(8,128)} %collective-permute-done.35.refs_2_.refs_8_), channel_id=1, source_target_pairs={{24,16},{28,20},{25,17},{29,21},{26,18},{30,22},{27,19},{31,23}} | collective-permute-start | bytes 2359304 | tf_op jit(solution)/shard_map/ppermute | solution.py:744
  369.0 121.5 %collective-permute-start.18 = (f32[512,1024]{1,0:T(8,128)}, f32[512,1024]{1,0:T(8,128)S(1)}, u32[]{:S(2)}, u32[]{:S(2)}) collective-permute-start(f32[512,1024]{1,0:T(8,128)} %refs_4_.1), channel_id=1, source_target_pairs={{0,8},{4,12},{8,0},{12,4},{16,24},{20,28},{24,16},{28,20},{1,9},{5... | collective-permute-start | bytes 6291464 | tf_op jit(solution)/shard_map/ppermute | solution.py:744
  375.1 23.8 %collective-permute-start.48 = (f32[2,768,128]{2,1,0:T(8,128)}, f32[2,768,128]{2,1,0:T(8,128)}, u32[]{:S(2)}, u32[]{:S(2)}) collective-permute-start(f32[2,768,128]{2,1,0:T(8,128)} %pad_maximum_fusion.10.refs_0_), channel_id=1, source_target_pairs={{0,1},{1,0},{2,3},{3,2},{4,5},{5,4},{6,7},{7,6},{8,9},{9,8},{10,11... | collective-permute-start | bytes 2359304 | tf_op jit(solution)/shard_map/ppermute | solution.py:860
  375.1 120.4 %collective-permute-start.19 = (f32[512,1024]{1,0:T(8,128)}, f32[512,1024]{1,0:T(8,128)S(1)}, u32[]{:S(2)}, u32[]{:S(2)}) collective-permute-start(f32[512,1024]{1,0:T(8,128)} %refs_4_.1), channel_id=1, source_target_pairs={{0,16},{4,20},{8,24},{12,28},{16,0},{20,4},{24,8},{28,12},{1,17},{... | collective-permute-start | bytes 6291464 | tf_op jit(solution)/shard_map/ppermute | solution.py:744
  375.2 122.1 %collective-permute-start.21 = (f32[512,1024]{1,0:T(8,128)}, f32[512,1024]{1,0:T(8,128)}, u32[]{:S(2)}, u32[]{:S(2)}) collective-permute-start(f32[512,1024]{1,0:T(8,128)} %refs_4_.1), channel_id=1, source_target_pairs={{0,4},{4,0},{8,12},{12,8},{16,20},{20,16},{24,28},{28,24},{1,5},{5... | collective-permute-start | bytes 6291464 | tf_op jit(solution)/shard_map/ppermute | solution.py:744
  391.4 53.1 %collective-permute-start.49 = (f32[2,768,128]{2,1,0:T(8,128)}, f32[2,768,128]{2,1,0:T(8,128)S(1)}, u32[]{:S(2)}, u32[]{:S(2)}) collective-permute-start(f32[2,768,128]{2,1,0:T(8,128)} %pad_maximum_fusion.10.refs_0_), channel_id=1, source_target_pairs={{0,2},{1,3},{2,0},{3,1},{4,6},{5,7},{6,4},{7,5},{8,10},{9,11},{10,... | collective-permute-start | bytes 2359304 | tf_op jit(solution)/shard_map/ppermute | solution.py:860
  398.9 69.3 %collective-permute-start.50 = (f32[2,768,128]{2,1,0:T(8,128)}, f32[2,768,128]{2,1,0:T(8,128)}, u32[]{:S(2)}, u32[]{:S(2)}) collective-permute-start(f32[2,768,128]{2,1,0:T(8,128)} %pad_maximum_fusion.10.refs_0_), channel_id=1, source_target_pairs={{0,3},{1,2},{2,1},{3,0},{4,7},{5,6},{6,5},{7,4},{8,11},{9,10},{10,... | collective-permute-start | bytes 2359304 | tf_op jit(solution)/shard_map/ppermute | solution.py:860
  444.5 42.6 %collective-permute-start.29 = (f32[768,128]{1,0:T(8,128)}, f32[768,128]{1,0:T(8,128)S(1)}, u32[]{:S(2)}, u32[]{:S(2)}) collective-permute-start(f32[768,128]{1,0:T(8,128)} %get-tuple-element.39), channel_id=1, source_target_pairs={{0,4},{4,0},{8,12},{12,8},{16,20},{20,16},{24,28},{28,24},{1,5},{5... | collective-permute-start | bytes 1179656 | tf_op jit(solution)/shard_map/ppermute | solution.py:744
  468.2 19.4 %collective-permute-start.8 = (f32[768,128]{1,0:T(8,128)}, f32[768,128]{1,0:T(8,128)S(1)}, u32[]{:S(2)}, u32[]{:S(2)}) collective-permute-start(f32[768,128]{1,0:T(8,128)} %get-tuple-element.32), channel_id=1, source_target_pairs={{0,4},{4,0},{8,12},{12,8},{16,20},{20,16},{24,28},{28,24},{1,5},{5... | collective-permute-start | bytes 1179656 | tf_op jit(solution)/shard_map/ppermute | solution.py:744
  487.1 2.0 collective-permute-start.39
  487.6 112.8 %copy-start.16 = (f32[2,768,128]{2,1,0:T(8,128)}, f32[2,768,128]{2,1,0:T(8,128)S(1)}, u32[]{:S(2)}) copy-start(f32[2,768,128]{2,1,0:T(8,128)S(1)} %pad_maximum_fusion.6.refs_0_) | copy-start | bytes 2359300
  487.6 111.5 %copy-start.32 = (f32[768,128]{1,0:T(8,128)S(1)}, f32[768,128]{1,0:T(8,128)}, u32[]{:S(2)}) copy-start(f32[768,128]{1,0:T(8,128)} %get-tuple-element.31) | copy-start | bytes 1179652
  487.6 111.5 %copy-start.33 = (f32[768,128]{1,0:T(8,128)}, f32[768,128]{1,0:T(8,128)S(1)}, u32[]{:S(2)}) copy-start(f32[768,128]{1,0:T(8,128)S(1)} %collective-permute-done.8) | copy-start | bytes 1179652
  487.7 20.5 %collective-permute-start.30 = (f32[2,768,128]{2,1,0:T(8,128)S(1)}, f32[2,768,128]{2,1,0:T(8,128)S(1)}, u32[]{:S(2)}, u32[]{:S(2)}) collective-permute-start(f32[2,768,128]{2,1,0:T(8,128)S(1)} %pad_maximum_fusion.6.refs_0_), channel_id=1, source_target_pairs={{0,1},{1,0},{2,3},{3,2},{4,5},{5,4},{6,7},{7,6},{8,9},{9,8},{10,11... | collective-permute-start | bytes 2359304 | tf_op jit(solution)/shard_map/ppermute | solution.py:860
  489.1 37.5 %collective-permute-start.31 = (f32[2,768,128]{2,1,0:T(8,128)S(1)}, f32[2,768,128]{2,1,0:T(8,128)}, u32[]{:S(2)}, u32[]{:S(2)}) collective-permute-start(f32[2,768,128]{2,1,0:T(8,128)S(1)} %pad_maximum_fusion.6.refs_0_), channel_id=1, source_target_pairs={{0,2},{3,1},{4,6},{7,5},{8,10},{11,9},{12,14},{15,13},{16,18},{19,... | collective-permute-start | bytes 2359304 | tf_op jit(solution)/shard_map/ppermute | solution.py:860
  490.4 110.0 %copy-start.1 = (f32[512,1024]{1,0:T(8,128)}, f32[512,1024]{1,0:T(8,128)S(1)}, u32[]{:S(2)}) copy-start(f32[512,1024]{1,0:T(8,128)S(1)} %collective-permute-done.18.refs_5_.refs_7_) | copy-start | bytes 6291460
  490.5 39.2 %collective-permute-start.32 = (f32[2,768,128]{2,1,0:T(8,128)S(1)}, f32[2,768,128]{2,1,0:T(8,128)S(1)}, u32[]{:S(2)}, u32[]{:S(2)}) collective-permute-start(f32[2,768,128]{2,1,0:T(8,128)S(1)} %pad_maximum_fusion.6.refs_0_), channel_id=1, source_target_pairs={{1,2},{2,1},{5,6},{6,5},{9,10},{10,9},{13,14},{14,13},{17,18},{18,... | collective-permute-start | bytes 2359304 | tf_op jit(solution)/shard_map/ppermute | solution.py:860
  495.5 70.3 %copy-start.17 = (f32[2,768,128]{2,1,0:T(8,128)}, f32[2,768,128]{2,1,0:T(8,128)S(1)}, u32[]{:S(2)}) copy-start(f32[2,768,128]{2,1,0:T(8,128)S(1)} %pad_maximum_fusion.9.refs_0_) | copy-start | bytes 2359300
  495.5 129.8 %copy-start.2 = (f32[512,1024]{1,0:T(8,128)}, f32[512,1024]{1,0:T(8,128)S(1)}, u32[]{:S(2)}) copy-start(f32[512,1024]{1,0:T(8,128)S(1)} %collective-permute-done.19.refs_6_.refs_8_) | copy-start | bytes 6291460
  495.5 46.5 %collective-permute-start.40 = (f32[2,768,128]{2,1,0:T(8,128)S(1)}, f32[2,768,128]{2,1,0:T(8,128)}, u32[]{:S(2)}, u32[]{:S(2)}) collective-permute-start(f32[2,768,128]{2,1,0:T(8,128)S(1)} %pad_maximum_fusion.9.refs_0_), channel_id=1, source_target_pairs={{0,1},{1,0},{2,3},{3,2},{4,5},{5,4},{6,7},{7,6},{8,9},{9,8},{10,11... | collective-permute-start | bytes 2359304 | tf_op jit(solution)/shard_map/ppermute | solution.py:860
  497.3 62.1 %collective-permute-start.41 = (f32[2,768,128]{2,1,0:T(8,128)S(1)}, f32[2,768,128]{2,1,0:T(8,128)S(1)}, u32[]{:S(2)}, u32[]{:S(2)}) collective-permute-start(f32[2,768,128]{2,1,0:T(8,128)S(1)} %pad_maximum_fusion.9.refs_0_), channel_id=1, source_target_pairs={{0,2},{3,1},{4,6},{7,5},{8,10},{11,9},{12,14},{15,13},{16,18},{19,... | collective-permute-start | bytes 2359304 | tf_op jit(solution)/shard_map/ppermute | solution.py:860
  509.0 54.0 %collective-permute-start.42 = (f32[2,768,128]{2,1,0:T(8,128)S(1)}, f32[2,768,128]{2,1,0:T(8,128)S(1)}, u32[]{:S(2)}, u32[]{:S(2)}) collective-permute-start(f32[2,768,128]{2,1,0:T(8,128)S(1)} %pad_maximum_fusion.9.refs_0_), channel_id=1, source_target_pairs={{1,2},{2,1},{5,6},{6,5},{9,10},{10,9},{13,14},{14,13},{17,18},{18,... | collective-permute-start | bytes 2359304 | tf_op jit(solution)/shard_map/ppermute | solution.py:860
  526.6 37.7 %collective-permute-start.20 = (f32[256,1024]{1,0:T(8,128)S(1)}, f32[256,1024]{1,0:T(8,128)}, u32[]{:S(2)}, u32[]{:S(2)}) collective-permute-start(f32[256,1024]{1,0:T(8,128)S(1)} %slice.85), channel_id=1, source_target_pairs={{0,8},{4,12},{8,0},{12,4},{16,24},{20,28},{24,16},{28,20},{1,9},{5... | collective-permute-start | bytes 3145736 | tf_op jit(solution)/shard_map/ppermute | solution.py:744
  529.6 93.6 %copy-start.22 = (f32[2,768,128]{2,1,0:T(8,128)}, f32[2,768,128]{2,1,0:T(8,128)S(1)}, u32[]{:S(2)}) copy-start(f32[2,768,128]{2,1,0:T(8,128)S(1)} %collective-permute-done.32.refs_4_) | copy-start | bytes 2359300
  529.6 36.1 %collective-permute-start.45 = (f32[256,1024]{1,0:T(8,128)S(1)}, f32[256,1024]{1,0:T(8,128)S(1)}, u32[]{:S(2)}, u32[]{:S(2)}) collective-permute-start(f32[256,1024]{1,0:T(8,128)S(1)} %slice.88), channel_id=1, source_target_pairs={{0,16},{4,20},{8,24},{12,28},{16,0},{20,4},{24,8},{28,12},{1,17},{... | collective-permute-start | bytes 3145736 | tf_op jit(solution)/shard_map/ppermute | solution.py:744
  542.0 78.4 %collective-permute-start.22 = (f32[512,1024]{1,0:T(8,128)S(1)}, f32[512,1024]{1,0:T(8,128)S(1)}, u32[]{:S(2)}, u32[]{:S(2)}) collective-permute-start(f32[512,1024]{1,0:T(8,128)S(1)} %collective-permute-done.18.refs_5_.refs_7_), channel_id=1, source_target_pairs={{0,4},{4,0},{8,12},{12,8},{16,20},{20,16},{24,28},{28,24},{1,5},{5... | collective-permute-start | bytes 6291464 | tf_op jit(solution)/shard_map/ppermute | solution.py:744
  559.4 63.9 %copy-start.23 = (f32[2,768,128]{2,1,0:T(8,128)}, f32[2,768,128]{2,1,0:T(8,128)S(1)}, u32[]{:S(2)}) copy-start(f32[2,768,128]{2,1,0:T(8,128)S(1)} %collective-permute-done.41.refs_2_) | copy-start | bytes 2359300
  559.4 63.9 %collective-permute-start.23 = (f32[512,1024]{1,0:T(8,128)S(1)}, f32[512,1024]{1,0:T(8,128)S(1)}, u32[]{:S(2)}, u32[]{:S(2)}) collective-permute-start(f32[512,1024]{1,0:T(8,128)S(1)} %collective-permute-done.19.refs_6_.refs_8_), channel_id=1, source_target_pairs={{0,4},{4,0},{8,12},{12,8},{16,20},{20,16},{24,28},{28,24},{1,5},{5... | collective-permute-start | bytes 6291464 | tf_op jit(solution)/shard_map/ppermute | solution.py:744
  563.0 19.2 %collective-permute-start.33 = (f32[2,768,128]{2,1,0:T(8,128)S(1)}, f32[2,768,128]{2,1,0:T(8,128)S(1)}, u32[]{:S(2)}, u32[]{:S(2)}) collective-permute-start(f32[2,768,128]{2,1,0:T(8,128)S(1)} %collective-permute-done.32.refs_4_), channel_id=1, source_target_pairs={{1,0},{2,3},{5,4},{6,7},{9,8},{10,11},{13,12},{14,15},{17,16},{18,... | collective-permute-start | bytes 2359304 | tf_op jit(solution)/shard_map/ppermute | solution.py:864
  564.4 34.7 %collective-permute-start.43 = (f32[2,768,128]{2,1,0:T(8,128)S(1)}, f32[2,768,128]{2,1,0:T(8,128)S(1)}, u32[]{:S(2)}, u32[]{:S(2)}) collective-permute-start(f32[2,768,128]{2,1,0:T(8,128)S(1)} %collective-permute-done.42.refs_4_), channel_id=1, source_target_pairs={{1,0},{2,3},{5,4},{6,7},{9,8},{10,11},{13,12},{14,15},{17,16},{18,... | collective-permute-start | bytes 2359304 | tf_op jit(solution)/shard_map/ppermute | solution.py:864
  565.8 54.6 %collective-permute-start.46 = (f32[256,1024]{1,0:T(8,128)S(1)}, f32[256,1024]{1,0:T(8,128)S(1)}, u32[]{:S(2)}, u32[]{:S(2)}) collective-permute-start(f32[256,1024]{1,0:T(8,128)S(1)} %collective-permute-done.45.refs_7_.refs_9_), channel_id=1, source_target_pairs={{0,4},{4,0},{8,12},{12,8},{16,20},{20,16},{24,28},{28,24},{1,5},{5... | collective-permute-start | bytes 3145736 | tf_op jit(solution)/shard_map/ppermute | solution.py:744
  582.2 32.8 %collective-permute-start.44 = (f32[2,768,128]{2,1,0:T(8,128)S(1)}, f32[2,768,128]{2,1,0:T(8,128)S(1)}, u32[]{:S(2)}, u32[]{:S(2)}) collective-permute-start(f32[2,768,128]{2,1,0:T(8,128)S(1)} %collective-permute-done.41.refs_2_), channel_id=1, source_target_pairs={{1,0},{2,3},{5,4},{6,7},{9,8},{10,11},{13,12},{14,15},{17,16},{18,... | collective-permute-start | bytes 2359304 | tf_op jit(solution)/shard_map/ppermute | solution.py:864
  599.1 54.2 %collective-permute-start.24 = (f32[256,1024]{1,0:T(8,128)}, f32[256,1024]{1,0:T(8,128)}, u32[]{:S(2)}, u32[]{:S(2)}) collective-permute-start(f32[256,1024]{1,0:T(8,128)} %collective-permute-done.20.refs_9_.refs_7_), channel_id=1, source_target_pairs={{0,4},{4,0},{8,12},{12,8},{16,20},{20,16},{24,28},{28,24},{1,5},{5... | collective-permute-start | bytes 3145736 | tf_op jit(solution)/shard_map/ppermute | solution.py:744
  615.1 38.2 %collective-permute-start.34 = (f32[2,768,128]{2,1,0:T(8,128)}, f32[2,768,128]{2,1,0:T(8,128)}, u32[]{:S(2)}, u32[]{:S(2)}) collective-permute-start(f32[2,768,128]{2,1,0:T(8,128)} %collective-permute-done.31.refs_2_), channel_id=1, source_target_pairs={{1,0},{2,3},{5,4},{6,7},{9,8},{10,11},{13,12},{14,15},{17,16},{18,... | collective-permute-start | bytes 2359304 | tf_op jit(solution)/shard_map/ppermute | solution.py:864
  620.3 66.0 %collective-permute-start.9 = (f32[2,768,128]{2,1,0:T(8,128)S(1)}, f32[2,768,128]{2,1,0:T(8,128)}, u32[]{:S(2)}, u32[]{:S(2)}) collective-permute-start(f32[2,768,128]{2,1,0:T(8,128)S(1)} %pad_maximum_fusion.2.refs_0_), channel_id=1, source_target_pairs={{0,1},{1,0},{2,3},{3,2},{4,5},{5,4},{6,7},{7,6},{8,9},{9,8},{10,11... | collective-permute-start | bytes 2359304 | tf_op jit(solution)/shard_map/ppermute | solution.py:860
  620.4 66.0 %collective-permute-start.10 = (f32[2,768,128]{2,1,0:T(8,128)S(1)}, f32[2,768,128]{2,1,0:T(8,128)S(1)}, u32[]{:S(2)}, u32[]{:S(2)}) collective-permute-start(f32[2,768,128]{2,1,0:T(8,128)S(1)} %pad_maximum_fusion.2.refs_0_), channel_id=1, source_target_pairs={{0,2},{1,3},{2,0},{3,1},{4,6},{5,7},{6,4},{7,5},{8,10},{9,11},{10,... | collective-permute-start | bytes 2359304 | tf_op jit(solution)/shard_map/ppermute | solution.py:860
  624.7 65.9 %collective-permute-start.11 = (f32[2,768,128]{2,1,0:T(8,128)S(1)}, f32[2,768,128]{2,1,0:T(8,128)S(1)}, u32[]{:S(2)}, u32[]{:S(2)}) collective-permute-start(f32[2,768,128]{2,1,0:T(8,128)S(1)} %pad_maximum_fusion.2.refs_0_), channel_id=1, source_target_pairs={{0,3},{1,2},{2,1},{3,0},{4,7},{5,6},{6,5},{7,4},{8,11},{9,10},{10,... | collective-permute-start | bytes 2359304 | tf_op jit(solution)/shard_map/ppermute | solution.py:860
  (30 other events, 702.1 us)
